TPU v7x, 32 devices: a whole 2x2x4 slice. The times are simulated.
32 devices in a mesh: mem: 4 (over x, core), lat: 8 (over z, y).
Axes of the slice: x: 2, y: 2, z: 4, core: 2. Of those that a mesh axis runs over, the one named last changes fastest.
Arguments:
- perturbation: bfloat16 [64, 128, 2048], P('mem', 'lat'), may hold values from -6 to 6
- obs_cells: int32 [8, 2048], P('lat'), may hold values from 0 to 32767
- obs_count: int32 [8], P('lat'), may hold values from 682 to 2048, as said below
- innovation: float32 [8, 2048], P('lat'), may hold values from -8 to 8
- obs_scale: float32 [8, 2048], P('lat'), may hold values from 0.3 to 3
Outputs:
- control: float32 [64, 64, 1024], P('mem', 'lat')
- increment: float32 [128, 2048], P('lat', 'mem')
Inputs may be any that keep to these rules, and one draw needn't show every extreme that they name: `obs_count`: at most 2048 live slots in a band, and some band has exactly 2048.
All inputs are finite; a program needn't handle non-finite values.
Results may differ from a plain program's by a relative error of at most 0.00035.
Values sent between devices are 32-bit elements; how exact they have to be, the bound alone decides.
No kernel may reach another device: no remote copies, remote signals or barrier semaphores. Data moves between devices by JAX's collectives and lax.ppermute only.
A program may use at most 64 MiB of HBM per device.

v0:
```python
import jax
import jax.numpy as jnp
from jax import lax
from jax.sharding import PartitionSpec as P

HALO = 8
LSIG = 3
ITERS = 3


def padded_2(block, sides, width):
    for axis, dim in sides:
        count = lax.axis_size(axis)
        forward = [(i, i + 1) for i in range(count - 1)]
        backward = [(target, source) for source, target in forward]
        low = lax.ppermute(
            lax.slice_in_dim(block, block.shape[dim] - width, None, axis=dim), axis, forward
        )
        high = lax.ppermute(lax.slice_in_dim(block, 0, width, axis=dim), axis, backward)
        block = jnp.concatenate([low, block, high], axis=dim)
    return block


def lat_weights():
    offsets = jnp.arange(2 * HALO + 1).astype(jnp.float32) - HALO
    spread = HALO / 2.0
    return 0.5 * jnp.exp(-offsets * offsets / (2.0 * spread * spread))


def lon_weights(coarse_cols):
    columns = jnp.arange(coarse_cols)
    distance = jnp.abs(columns[:, None] - columns[None, :])
    distance = jnp.minimum(distance, coarse_cols - distance).astype(jnp.float32)
    return jnp.exp(-distance * distance / (2.0 * LSIG * LSIG))


def band_matrix(row_count, lat_taps):
    rows = jnp.arange(row_count)[:, None]
    columns = jnp.arange(row_count + 2 * HALO)[None, :]
    offset_grid = columns - rows
    matrix = jnp.zeros((row_count, row_count + 2 * HALO), jnp.float32)
    for offset in range(2 * HALO + 1):
        matrix = matrix + jnp.where(offset_grid == offset, lat_taps[offset], 0.0)
    return matrix


def widen_lon(coarse):
    odd_part = 0.5 * (coarse + jnp.roll(coarse, -1, axis=-1))
    return jnp.stack([coarse, odd_part], axis=-1).reshape(
        coarse.shape[:-1] + (2 * coarse.shape[-1],)
    )


def narrow_lon(fine):
    paired = fine.reshape(fine.shape[:-1] + (fine.shape[-1] // 2, 2))
    odd_part = paired[..., 1]
    return paired[..., 0] + 0.5 * odd_part + 0.5 * jnp.roll(odd_part, 1, axis=-1)


def on_device(perturbation, obs_cells, obs_count, innovation, obs_scale):
    mem_count = lax.axis_size("mem")
    local_members, fine_rows, lon_cells = perturbation.shape
    coarse_rows = fine_rows // 2
    coarse_cols = lon_cells // 2
    member_scale = (local_members * mem_count - 1) ** (-0.5)
    lat_taps = lat_weights()
    banded = band_matrix(coarse_rows, lat_taps)
    circulant = lon_weights(coarse_cols)
    obs_index = obs_cells[0]
    row_index = obs_index // lon_cells
    col_index = obs_index % lon_cells
    active = jnp.arange(obs_index.shape[0]) < obs_count[0]
    is_first = lax.axis_index("mem") == 0
    target = innovation[0]
    saturation = obs_scale[0]

    def smooth(coarse):
        padded = padded_2(coarse, (("lat", 1),), HALO)
        return jnp.einsum(
            "ij,mjk->mik",
            banded,
            padded,
            precision=lax.Precision.HIGHEST,
            preferred_element_type=jnp.float32,
        )

    bend_mask = active & is_first
    increment = jnp.zeros((fine_rows, lon_cells), jnp.float32)
    control = jnp.zeros((local_members, coarse_rows, coarse_cols), jnp.float32)
    observed = jnp.zeros(obs_index.shape, jnp.float32)
    for iteration in range(ITERS):
        misfit = target - observed
        bounded = jnp.tanh(misfit / saturation)
        pull = jnp.where(active, saturation * bounded, 0.0)
        weight = jnp.where(bend_mask, 1.0 - bounded * bounded, 0.0)
        obs_field = (
            jnp.zeros((fine_rows * lon_cells,), jnp.float32)
            .at[obs_index]
            .add(pull)
            .reshape(fine_rows, lon_cells)
        )
        weighted = perturbation.astype(jnp.float32) * obs_field[None] * member_scale
        folded = narrow_lon(weighted.reshape(local_members, coarse_rows, 2, lon_cells).sum(axis=2))
        gradient = control - smooth(
            jnp.dot(
                folded,
                circulant,
                precision=lax.Precision.HIGHEST,
                preferred_element_type=jnp.float32,
            )
        )
        local_norm = jnp.sum(gradient * gradient)
        grad_norm = lax.psum(local_norm, ("mem", "lat"))
        direction = -gradient
        smoothed = smooth(direction)
        along = jnp.dot(
            smoothed, circulant, precision=lax.Precision.HIGHEST, preferred_element_type=jnp.float32
        )
        fine_block = jnp.repeat(widen_lon(along), 2, axis=1)
        partial_image = (
            jnp.sum(perturbation.astype(jnp.float32) * fine_block, axis=0) * member_scale
        )
        hits = lax.psum(partial_image[row_index, col_index], "mem")
        local_bend = jnp.sum(weight * hits * hits)
        bending = lax.psum(local_bend, ("mem", "lat"))
        step_size = grad_norm / (grad_norm + bending + 1e-06)
        control = control + step_size * direction
        increment = increment + step_size * partial_image
        observed = observed + step_size * hits
    increment = lax.psum_scatter(increment, "mem", scatter_dimension=1, tiled=True)
    return (control, increment)


def solution(mesh):
    in_specs = (P("mem", "lat", None), P("lat", None), P("lat"), P("lat", None), P("lat", None))
    out_specs = (P("mem", "lat", None), P("lat", "mem"))
    return jax.shard_map(
        on_device, mesh=mesh, in_specs=in_specs, out_specs=out_specs, check_vma=False
    )
```

profile of v0, /device:TPU:0, one launch (start us, length us, event | category | flops | bytes accessed | tf_op | source)
XLA Modules:
  0.0 612.5 jit_solution(4146181760270412733)
XLA Ops:
  9.4 11.3 %scatter_custom_fusion = f32[32768]{0:T(1024)S(1)} fusion(s32[2048]{0:T(1024)S(1)} %bitcast.168, f32[2048]{0:T(1024)S(1)} %multiply_select_fusion.2, f32[]{:T(128)} %constant.31.clone.1), kind=kCustom, calls=%fused_computation.133 | custom fusion | flops 2048 | bytes 131076 | tf_op jit(solution)/shard_map/scatter-add | solution.py:99
  28.8 4.8 copy.19
  33.6 7.2 %fusion.188 = (f32[16,8,1024,1]{0,1,3,2:T(8,128)}, f32[16,8,1024,1]{0,1,3,2:T(8,128)}) fusion(f32[16,8,1024,2]{0,1,3,2:T(8,128)} %bitcast.146), kind=kLoop, calls=%fused_computation.221 | loop fusion | bytes 2097152 | tf_op jit(solution)/shard_map/slice | solution.py:57
  50.9 4.9 collective-permute-start
  58.1 10.6 %select_add_fusion = f32[8,24]{1,0:T(8,128)S(1)} fusion(f32[]{:T(128)} %bitcast.25, f32[]{:T(128)} %bitcast.24, f32[]{:T(128)} %bitcast.23, f32[]{:T(128)} %bitcast.22, f32[]{:T(128)} %bitcast.21, f32[]{:T(128)} %bitcast.20, f32[]{:T(128)} %bitcast.19, f32[]{:T(128)} %bitcast.18, f32[]{:T(128)} %bitcast.17, f32[]{:T(128)} %bitcast.16, f32[]{:T(128)} %bitcast.15, ...), kind=kLoop, calls=%fused_computation.169 | loop fusion | flops 9792 | bytes 836 | tf_op jit(solution)/shard_map/add | solution.py:43
  68.7 9.5 %collective-permute-done = f32[16,8,1024]{2,1,0:T(8,128)S(1)} collective-permute-done((f32[16,8,1024]{2,1,0:T(8,128)S(1)}, f32[16,8,1024]{2,1,0:T(8,128)S(1)}, u32[]{:S(2)}, u32[]{:S(2)}) %collective-permute-start) | collective-permute-done | bytes 524320 | tf_op jit(solution)/shard_map/ppermute | solution.py:16
  85.6 20.2 %collective-permute-done.2 = f32[16,8,1024]{2,1,0:T(8,128)S(1)} collective-permute-done((f32[16,8,1024]{2,1,0:T(8,128)S(1)}, f32[16,8,1024]{2,1,0:T(8,128)S(1)}, u32[]{:S(2)}, u32[]{:S(2)}) %collective-permute-start.2) | collective-permute-done | bytes 524320 | tf_op jit(solution)/shard_map/ppermute | solution.py:16
  111.1 6.2 %copy.22 = f32[16,8,1024,2]{0,1,3,2:T(8,128)} copy(f32[16,8,1024,2]{2,1,0,3:T(8,128)S(1)} %pad_maximum_fusion) | data formatting | bytes 2097152 | tf_op jit(solution)/shard_map/stack | solution.py:49
  117.3 5.4 copy.23
  130.8 16.6 %gather_fusion = f32[2048]{0:T(1024)S(1)} fusion(f32[16,2048]{1,0:T(8,128)S(1)} %broadcast_multiply_fusion.2, s32[2048]{0:T(1024)S(1)} %bitcast.140), kind=kCustom, calls=%fused_computation | custom fusion | bytes 32768 | tf_op jit(solution)/shard_map/gather | solution.py:123
  147.4 5.8 psum.64
  153.8 45.1 %all-reduce.2 = (f32[]{:T(128)}, f32[]{:T(128)}) all-reduce(f32[]{:T(128)} %get-tuple-element.20, f32[]{:T(128)} %fusion.124), channel_id=1, replica_groups=mesh['mem'=4,'lat'=8] {'mem','lat'}, use_global_device_ids=true, to_apply=%region_3.4 | all-reduce | flops 2 | bytes 16 | tf_op jit(solution)/shard_map/psum | solution.py:113
  200.9 11.3 %scatter_custom_fusion.1 = f32[32768]{0:T(1024)S(1)} fusion(s32[2048]{0:T(1024)S(1)} %bitcast.169, f32[2048]{0:T(1024)S(1)} %multiply_select_fusion.1, f32[]{:T(128)} %constant.31.clone.1), kind=kCustom, calls=%fused_computation.131 | custom fusion | flops 2048 | bytes 131076 | tf_op jit(solution)/shard_map/scatter-add | solution.py:99
  226.4 7.2 %fusion.187 = (f32[16,8,1024,1]{0,1,3,2:T(8,128)}, f32[16,8,1024,1]{0,1,3,2:T(8,128)}) fusion(f32[16,8,1024,2]{0,1,3,2:T(8,128)} %bitcast.147), kind=kLoop, calls=%fused_computation.220 | loop fusion | bytes 2097152 | tf_op jit(solution)/shard_map/slice | solution.py:57
  249.7 19.2 %collective-permute-done.4 = f32[16,8,1024]{2,1,0:T(8,128)S(1)} collective-permute-done((f32[16,8,1024]{2,1,0:T(8,128)S(1)}, f32[16,8,1024]{2,1,0:T(8,128)S(1)}, u32[]{:S(2)}, u32[]{:S(2)}) %collective-permute-start.4) | collective-permute-done | bytes 524320 | tf_op jit(solution)/shard_map/ppermute | solution.py:16
  276.1 18.5 %collective-permute-done.6 = f32[16,8,1024]{2,1,0:T(8,128)S(1)} collective-permute-done((f32[16,8,1024]{2,1,0:T(8,128)S(1)}, f32[16,8,1024]{2,1,0:T(8,128)S(1)}, u32[]{:S(2)}, u32[]{:S(2)}) %collective-permute-start.6) | collective-permute-done | bytes 524320 | tf_op jit(solution)/shard_map/ppermute | solution.py:16
  299.9 6.2 %copy.27 = f32[16,8,1024,2]{0,1,3,2:T(8,128)} copy(f32[16,8,1024,2]{2,1,0,3:T(8,128)S(1)} %pad_maximum_fusion.1) | data formatting | bytes 2097152 | tf_op jit(solution)/shard_map/stack | solution.py:49
  306.1 5.4 copy.28
  319.6 16.6 %gather_fusion.1 = f32[2048]{0:T(1024)S(1)} fusion(f32[16,2048]{1,0:T(8,128)S(1)} %broadcast_multiply_fusion.1, s32[2048]{0:T(1024)S(1)} %bitcast.141), kind=kCustom, calls=%fused_computation.1 | custom fusion | bytes 32768 | tf_op jit(solution)/shard_map/gather | solution.py:123
  336.2 6.1 psum.67
  342.9 46.1 %all-reduce.1 = (f32[]{:T(128)}, f32[]{:T(128)}) all-reduce(f32[]{:T(128)} %get-tuple-element.18, f32[]{:T(128)} %fusion.125), channel_id=1, replica_groups=mesh['mem'=4,'lat'=8] {'mem','lat'}, use_global_device_ids=true, to_apply=%region_11.12 | all-reduce | flops 2 | bytes 16 | tf_op jit(solution)/shard_map/psum | solution.py:113
  391.7 11.4 %scatter_custom_fusion.2 = f32[32768]{0:T(1024)S(1)} fusion(s32[2048]{0:T(1024)} %bitcast.170, f32[2048]{0:T(1024)S(1)} %get-tuple-element.8, f32[]{:T(128)} %constant.31.clone.1), kind=kCustom, calls=%fused_computation.129 | custom fusion | flops 2048 | bytes 131584 | tf_op jit(solution)/shard_map/scatter-add | solution.py:99
  417.3 7.2 %fusion.186 = (f32[16,8,1024,1]{0,1,3,2:T(8,128)}, f32[16,8,1024,1]{0,1,3,2:T(8,128)}) fusion(f32[16,8,1024,2]{0,1,3,2:T(8,128)} %bitcast.148), kind=kLoop, calls=%fused_computation.219 | loop fusion | bytes 2097152 | tf_op jit(solution)/shard_map/slice | solution.py:57
  431.2 5.1 fusion.6
  442.3 19.2 %collective-permute-done.8 = f32[16,8,1024]{2,1,0:T(8,128)S(1)} collective-permute-done((f32[16,8,1024]{2,1,0:T(8,128)S(1)}, f32[16,8,1024]{2,1,0:T(8,128)S(1)}, u32[]{:S(2)}, u32[]{:S(2)}) %collective-permute-start.8) | collective-permute-done | bytes 524320 | tf_op jit(solution)/shard_map/ppermute | solution.py:16
  469.6 18.6 %collective-permute-done.10 = f32[16,8,1024]{2,1,0:T(8,128)S(1)} collective-permute-done((f32[16,8,1024]{2,1,0:T(8,128)S(1)}, f32[16,8,1024]{2,1,0:T(8,128)S(1)}, u32[]{:S(2)}, u32[]{:S(2)}) %collective-permute-start.10) | collective-permute-done | bytes 524320 | tf_op jit(solution)/shard_map/ppermute | solution.py:16
  494.7 6.2 %copy.32 = f32[16,8,1024,2]{0,1,3,2:T(8,128)} copy(f32[16,8,1024,2]{2,1,0,3:T(8,128)S(1)} %pad_maximum_fusion.2) | data formatting | bytes 2097152 | tf_op jit(solution)/shard_map/stack | solution.py:49
  500.9 5.4 copy.33
  514.4 16.6 %gather_fusion.2 = f32[2048]{0:T(1024)S(1)} fusion(f32[16,2048]{1,0:T(8,128)S(1)} %broadcast_multiply_fusion, s32[2048]{0:T(1024)S(1)} %bitcast.142), kind=kCustom, calls=%fused_computation.2 | custom fusion | bytes 32768 | tf_op jit(solution)/shard_map/gather | solution.py:123
  531.0 5.8 psum.70
  537.5 45.1 %all-reduce = (f32[]{:T(128)}, f32[]{:T(128)}) all-reduce(f32[]{:T(128)} %get-tuple-element.17, f32[]{:T(128)} %fusion.126), channel_id=1, replica_groups=mesh['mem'=4,'lat'=8] {'mem','lat'}, use_global_device_ids=true, to_apply=%region_19.20 | all-reduce | flops 2 | bytes 16 | tf_op jit(solution)/shard_map/psum | solution.py:113
  586.2 19.0 %reduce-scatter.2.cloned.1.call-done = f32[16,512]{1,0:T(8,128)} async-done(((f32[16,2048]{1,0:T(8,128)}), f32[16,512]{1,0:T(8,128)}) %reduce-scatter.2.cloned.1.call-update) | async-done | bytes 32784 | tf_op jit(solution)/shard_map/reduce_scatter | solution.py:130
  (111 shorter events, 147.0 us)
Async XLA Ops:
  7.2 598.1 %reduce-scatter.2.cloned.1.call-start = ((), (), s32[]{:S(2)}) async-start(), calls=%async_computation.1 | async-start | bytes 163840 | tf_op jit(solution)/shard_map/reduce_scatter | solution.py:130
  8.7 192.2 %copy-start.10 = (s32[2048,1]{0,1:T(1,128)}, s32[2048,1]{0,1:T(1,128)S(1)}, u32[]{:S(2)}) copy-start(s32[2048,1]{0,1:T(1,128)S(1)} %get-tuple-element.23) | copy-start | bytes 24580
  50.9 27.3 %collective-permute-start = (f32[16,8,1024]{2,1,0:T(8,128)S(1)}, f32[16,8,1024]{2,1,0:T(8,128)S(1)}, u32[]{:S(2)}, u32[]{:S(2)}) collective-permute-start(f32[16,8,1024]{2,1,0:T(8,128)S(1)} %fusion.14), channel_id=1, source_target_pairs={{0,1},{1,2},{2,3},{3,4},{4,5},{5,6},{6,7},{8,9},{9,10},{10,11},{11... | collective-permute-start | bytes 1572872 | tf_op jit(solution)/shard_map/ppermute | solution.py:16
  55.8 22.4 %collective-permute-start.1 = (f32[16,8,1024]{2,1,0:T(8,128)S(1)}, f32[16,8,1024]{2,1,0:T(8,128)S(1)}, u32[]{:S(2)}, u32[]{:S(2)}) collective-permute-start(f32[16,8,1024]{2,1,0:T(8,128)S(1)} %fusion.14), channel_id=1, source_target_pairs={{1,0},{2,1},{3,2},{4,3},{5,4},{6,5},{7,6},{9,8},{10,9},{11,10},{12... | collective-permute-start | bytes 1572872 | tf_op jit(solution)/shard_map/ppermute | solution.py:19
  68.7 225.9 %copy-start.7 = (f32[8,24]{1,0:T(8,128)}, f32[8,24]{1,0:T(8,128)S(1)}, u32[]{:S(2)}) copy-start(f32[8,24]{1,0:T(8,128)S(1)} %select_add_fusion) | copy-start | bytes 2308
  79.9 25.9 %collective-permute-start.2 = (f32[16,8,1024]{2,1,0:T(8,128)S(1)}, f32[16,8,1024]{2,1,0:T(8,128)S(1)}, u32[]{:S(2)}, u32[]{:S(2)}) collective-permute-start(f32[16,8,1024]{2,1,0:T(8,128)S(1)} %get-tuple-element.21), channel_id=1, source_target_pairs={{0,1},{1,2},{2,3},{3,4},{4,5},{5,6},{6,7},{8,9},{9,10},{10,11},{11... | collective-permute-start | bytes 1572872 | tf_op jit(solution)/shard_map/ppermute | solution.py:16
  84.3 21.5 %collective-permute-start.3 = (f32[16,8,1024]{2,1,0:T(8,128)S(1)}, f32[16,8,1024]{2,1,0:T(8,128)S(1)}, u32[]{:S(2)}, u32[]{:S(2)}) collective-permute-start(f32[16,8,1024]{2,1,0:T(8,128)S(1)} %get-tuple-element.21), channel_id=1, source_target_pairs={{1,0},{2,1},{3,2},{4,3},{5,4},{6,5},{7,6},{9,8},{10,9},{11,10},{12... | collective-permute-start | bytes 1572872 | tf_op jit(solution)/shard_map/ppermute | solution.py:19
  122.7 6.2 %copy-start = (bf16[16,16,2048]{2,1,0:T(8,128)(2,1)S(1)}, bf16[16,16,2048]{2,1,0:T(8,128)(2,1)}, u32[]{:S(2)}) copy-start(bf16[16,16,2048]{2,1,0:T(8,128)(2,1)} %param.5) | copy-start | bytes 3145732
  130.7 22.5 %copy-start.2 = (f32[1,2048]{1,0:T(1,128)S(1)}, f32[1,2048]{1,0:T(1,128)}, u32[]{:S(2)}) copy-start(f32[1,2048]{1,0:T(1,128)} %param.9) | copy-start | bytes 24580
  130.8 22.5 %copy-start.3 = (f32[1,2048]{1,0:T(1,128)S(1)}, f32[1,2048]{1,0:T(1,128)}, u32[]{:S(2)}) copy-start(f32[1,2048]{1,0:T(1,128)} %param.8) | copy-start | bytes 24580
  153.2 68.4 %copy-start.5 = (f32[2048]{0:T(1024)}, f32[2048]{0:T(1024)S(1)}, u32[]{:S(2)}) copy-start(f32[2048]{0:T(1024)S(1)} %psum.64) | copy-start | bytes 24580
  243.7 25.1 %collective-permute-start.4 = (f32[16,8,1024]{2,1,0:T(8,128)S(1)}, f32[16,8,1024]{2,1,0:T(8,128)S(1)}, u32[]{:S(2)}, u32[]{:S(2)}) collective-permute-start(f32[16,8,1024]{2,1,0:T(8,128)S(1)} %fusion.10), channel_id=1, source_target_pairs={{0,1},{1,2},{2,3},{3,4},{4,5},{5,6},{6,7},{8,9},{9,10},{10,11},{11... | collective-permute-start | bytes 1572872 | tf_op jit(solution)/shard_map/ppermute | solution.py:16
  248.2 20.6 %collective-permute-start.5 = (f32[16,8,1024]{2,1,0:T(8,128)S(1)}, f32[16,8,1024]{2,1,0:T(8,128)S(1)}, u32[]{:S(2)}, u32[]{:S(2)}) collective-permute-start(f32[16,8,1024]{2,1,0:T(8,128)S(1)} %fusion.10), channel_id=1, source_target_pairs={{1,0},{2,1},{3,2},{4,3},{5,4},{6,5},{7,6},{9,8},{10,9},{11,10},{12... | collective-permute-start | bytes 1572872 | tf_op jit(solution)/shard_map/ppermute | solution.py:19
  270.4 24.2 %collective-permute-start.6 = (f32[16,8,1024]{2,1,0:T(8,128)S(1)}, f32[16,8,1024]{2,1,0:T(8,128)S(1)}, u32[]{:S(2)}, u32[]{:S(2)}) collective-permute-start(f32[16,8,1024]{2,1,0:T(8,128)S(1)} %get-tuple-element.19), channel_id=1, source_target_pairs={{0,1},{1,2},{2,3},{3,4},{4,5},{5,6},{6,7},{8,9},{9,10},{10,11},{11... | collective-permute-start | bytes 1572872 | tf_op jit(solution)/shard_map/ppermute | solution.py:16
  274.8 19.8 %collective-permute-start.7 = (f32[16,8,1024]{2,1,0:T(8,128)S(1)}, f32[16,8,1024]{2,1,0:T(8,128)S(1)}, u32[]{:S(2)}, u32[]{:S(2)}) collective-permute-start(f32[16,8,1024]{2,1,0:T(8,128)S(1)} %get-tuple-element.19), channel_id=1, source_target_pairs={{1,0},{2,1},{3,2},{4,3},{5,4},{6,5},{7,6},{9,8},{10,9},{11,10},{12... | collective-permute-start | bytes 1572872 | tf_op jit(solution)/shard_map/ppermute | solution.py:19
  319.6 22.7 %copy-start.4 = (f32[1,2048]{1,0:T(1,128)S(1)}, f32[1,2048]{1,0:T(1,128)}, u32[]{:S(2)}) copy-start(f32[1,2048]{1,0:T(1,128)} %param.8) | copy-start | bytes 24580
  319.6 22.7 %copy-start.6 = (f32[2048]{0:T(1024)S(1)}, f32[2048]{0:T(1024)}, u32[]{:S(2)}) copy-start(f32[2048]{0:T(1024)} %copy-done.5) | copy-start | bytes 24580
  431.2 30.3 %copy-start.8 = (f32[8,24]{1,0:T(8,128)S(1)}, f32[8,24]{1,0:T(8,128)}, u32[]{:S(2)}) copy-start(f32[8,24]{1,0:T(8,128)} %copy-done.7) | copy-start | bytes 2308
  436.3 25.3 %collective-permute-start.8 = (f32[16,8,1024]{2,1,0:T(8,128)S(1)}, f32[16,8,1024]{2,1,0:T(8,128)S(1)}, u32[]{:S(2)}, u32[]{:S(2)}) collective-permute-start(f32[16,8,1024]{2,1,0:T(8,128)S(1)} %fusion.6), channel_id=1, source_target_pairs={{0,1},{1,2},{2,3},{3,4},{4,5},{5,6},{6,7},{8,9},{9,10},{10,11},{11... | collective-permute-start | bytes 1572872 | tf_op jit(solution)/shard_map/ppermute | solution.py:16
  440.8 20.8 %collective-permute-start.9 = (f32[16,8,1024]{2,1,0:T(8,128)S(1)}, f32[16,8,1024]{2,1,0:T(8,128)S(1)}, u32[]{:S(2)}, u32[]{:S(2)}) collective-permute-start(f32[16,8,1024]{2,1,0:T(8,128)S(1)} %fusion.6), channel_id=1, source_target_pairs={{1,0},{2,1},{3,2},{4,3},{5,4},{6,5},{7,6},{9,8},{10,9},{11,10},{12... | collective-permute-start | bytes 1572872 | tf_op jit(solution)/shard_map/ppermute | solution.py:19
  463.9 24.3 %collective-permute-start.10 = (f32[16,8,1024]{2,1,0:T(8,128)S(1)}, f32[16,8,1024]{2,1,0:T(8,128)S(1)}, u32[]{:S(2)}, u32[]{:S(2)}) collective-permute-start(f32[16,8,1024]{2,1,0:T(8,128)S(1)} %get-tuple-element.16), channel_id=1, source_target_pairs={{0,1},{1,2},{2,3},{3,4},{4,5},{5,6},{6,7},{8,9},{9,10},{10,11},{11... | collective-permute-start | bytes 1572872 | tf_op jit(solution)/shard_map/ppermute | solution.py:16
  468.3 19.9 %collective-permute-start.11 = (f32[16,8,1024]{2,1,0:T(8,128)S(1)}, f32[16,8,1024]{2,1,0:T(8,128)}, u32[]{:S(2)}, u32[]{:S(2)}) collective-permute-start(f32[16,8,1024]{2,1,0:T(8,128)S(1)} %get-tuple-element.16), channel_id=1, source_target_pairs={{1,0},{2,1},{3,2},{4,3},{5,4},{6,5},{7,6},{9,8},{10,9},{11,10},{12... | collective-permute-start | bytes 1572872 | tf_op jit(solution)/shard_map/ppermute | solution.py:19
  514.4 22.5 %copy-start.9 = (f32[2048]{0:T(1024)S(1)}, f32[2048]{0:T(1024)}, u32[]{:S(2)}) copy-start(f32[2048]{0:T(1024)} %get-tuple-element.9) | copy-start | bytes 24580
  514.4 70.9 %copy-start.1 = (f32[16,8,1024]{2,1,0:T(8,128)S(1)}, f32[16,8,1024]{2,1,0:T(8,128)}, u32[]{:S(2)}) copy-start(f32[16,8,1024]{2,1,0:T(8,128)} %get-tuple-element.42) | copy-start | bytes 1572868
Sparse Core Ops, SparseCore 0:
  585.4 19.8 reduce-scatter.1
where the time goes:
time: 622 us; the launch traced here: 613 us
  local copies, waits for them, and re-layouts  169 us (27%)
  blocking collectives  154 us (25%)
  waiting for transfers between devices  124 us (20%)
  other arithmetic  74.9 us (12%)
  starting transfers between devices  35.5 us (6%)
  matrix products  33.7 us (5%)
  between operations  21.7 us (3%)
    psum x3, blocking collectives, on_device(): grad_norm = lax.psum(local_norm, ('mem', 'lat'))  136 us
    ppermute x6, waiting for transfers between devices, padded_2(): lax.ppermute(lax.slice_in_dim(block, block.shape[dim] - width, None, axis...  105 us
    gather x3, local copies, waits for them, and re-layouts, on_device(): hits = lax.psum(partial_image[row_index, col_index], 'mem')  50 us
    scatter-add x3, other arithmetic, on_device(): obs_field = jnp.zeros((fine_rows * lon_cells,), jnp.float32).at[obs_index...  34 us
    ppermute x6, starting transfers between devices, padded_2(): lax.ppermute(lax.slice_in_dim(block, block.shape[dim] - width, None, axis...  27.1 us
    slice x3, local copies, waits for them, and re-layouts, narrow_lon(): paired[..., 0] + 0.5 * odd_part + 0.5 * jnp.roll(odd_part, 1, axis=-1)  21.6 us
    reduce_scatter x1, waiting for transfers between devices, on_device(): lax.psum_scatter(increment, 'mem', scatter_dimension=1, tiled=True)  19 us
    another operation x3, local copies, waits for them, and re-layouts, widen_lon(): jnp.stack([coarse, odd_part], axis=-1)  18.6 us
  transfers between devices with their start and end apart: 13, of which 7 were waited for; matrix products, arithmetic and copies ran while one was open for 2% of the time, Pallas kernels for 0%

commit v1 on v0

v1 whole, which is shorter than its diff:
```python
import functools

import jax
import jax.numpy as jnp
import numpy as np
from jax import lax
from jax.experimental import pallas as pl
from jax.experimental.pallas import tpu as pltpu
from jax.sharding import PartitionSpec as P

HALO = 8
LSIG = 3
ITERS = 3
REACH = 2
NREL = 2 * REACH + 1
BLK = 256
EDGE = 128
META = 8


def lat_tables(bands, coarse_rows):
    rows = bands * coarse_rows
    offset = np.arange(rows)[:, None] - np.arange(rows)[None, :]
    spread = HALO / 2.0
    r1 = np.where(np.abs(offset) <= HALO, 0.5 * np.exp(-offset * offset / (2.0 * spread * spread)), 0.0)
    r2 = r1 @ r1
    out = np.zeros((bands, 2, NREL, coarse_rows, 128), np.float32)
    for b in range(bands):
        for d in range(NREL):
            s = b + d - REACH
            if 0 <= s < bands:
                own = slice(b * coarse_rows, (b + 1) * coarse_rows)
                other = slice(s * coarse_rows, (s + 1) * coarse_rows)
                out[b, 0, d, :, :coarse_rows] = r2[own, other]
                out[b, 1, d, :, :coarse_rows] = r1[own, other]
    return out


def lon_blocks(coarse_cols):
    d = np.arange(coarse_cols)
    d = np.minimum(d, coarse_cols - d).astype(np.float32)
    c1 = np.exp(-d * d / np.float32(2.0 * LSIG * LSIG)).astype(np.float32).astype(np.float64)
    c2 = np.real(np.fft.ifft(np.fft.fft(c1) ** 2))
    away = np.arange(BLK + 2 * EDGE)[:, None] - EDGE - np.arange(BLK)[None, :]
    inside = np.abs(away) <= EDGE
    blocks = []
    for c in (c1, c2):
        t = jnp.asarray(np.where(inside, c[away % coarse_cols], 0.0).astype(np.float32))
        hi = t.astype(jnp.bfloat16)
        lo = (t - hi.astype(jnp.float32)).astype(jnp.bfloat16)
        blocks.append(jnp.stack([hi, lo]))
    return blocks


def split(a):
    hi = a.astype(jnp.bfloat16)
    return hi, (a - hi.astype(jnp.float32)).astype(jnp.bfloat16)


def dot(a, b, dims=((1,), (0,))):
    return lax.dot_general(a, b, (dims, ((), ())), preferred_element_type=jnp.float32)


def full(ref_shape, dim):
    return lax.broadcasted_iota(jnp.int32, ref_shape, dim).astype(jnp.float32)


def pick_kernel(p_ref, meta_ref, out_ref, *, members, fine_rows, chunk):
    lon = p_ref.shape[1]
    slots = meta_ref.shape[1]

    def body(n, _):
        at = pl.ds(pl.multiple_of(n * chunk, chunk), chunk)
        col = 2.0 * meta_ref[0:1, at]
        row = meta_ref[1:2, at]
        one = jnp.where(full((lon, chunk), 0) == col, 1.0, 0.0).astype(jnp.bfloat16)
        got = dot(p_ref[...], one).reshape(members, fine_rows, chunk)
        mask = jnp.where(full((fine_rows, chunk), 0) == row, 1.0, 0.0)
        out_ref[0:members, at] = jnp.sum(got * mask[None], axis=1)
        out_ref[members : members + META, at] = meta_ref[:, at]
        return 0

    lax.fori_loop(0, slots // chunk, body, 0)


def scatter(q_ref, tab, v_of, first, last, lhs_ref, x_ref, members, coarse_rows):
    cols = x_ref.shape[1]
    slots = q_ref.shape[2]
    half = members * coarse_rows
    x_ref[...] = jnp.zeros_like(x_ref)

    def band(d, _):
        at_col = q_ref[d, members : members + 1, :]
        row = jnp.floor(q_ref[d, members + 1 : members + 2, :] * 0.5)
        v = v_of(d)
        weights = jnp.zeros((coarse_rows, slots), jnp.float32)
        for r in range(coarse_rows):
            weights = jnp.where(row == float(r), tab[d, :, r : r + 1], weights)
        weights = weights * v
        for k in range(members):
            hi, lo = split(weights * q_ref[d, k : k + 1, :])
            lhs_ref[k * coarse_rows : (k + 1) * coarse_rows, :] = hi
            lhs_ref[half + k * coarse_rows : half + (k + 1) * coarse_rows, :] = lo

        def block(c, _):
            base = (c * BLK).astype(jnp.float32)
            near = jnp.where(jnp.logical_and(c == 0, at_col > cols - 1.0), at_col - float(cols), at_col)
            hat = jnp.maximum(1.0 - jnp.abs((near - base) - full((BLK, slots), 0)), 0.0)
            got = dot(lhs_ref[...], hat.astype(jnp.bfloat16), ((1,), (1,)))
            at = pl.ds(pl.multiple_of(c * BLK, BLK), BLK)
            x_ref[:, at] = x_ref[:, at] + (got[:half] + got[half:])
            return 0

        return lax.fori_loop(0, cols // BLK, block, 0)

    lax.fori_loop(first, last, band, 0)


def lon_filter(x, t_ref):
    half, cols = x.shape
    ext = jnp.concatenate([x[:, cols - EDGE :], x, x[:, :EDGE]], axis=1)
    hi, lo = split(ext)
    parts = []
    for c in range(cols // BLK):
        at = slice(c * BLK, (c + 1) * BLK + 2 * EDGE)
        parts.append(dot(hi[:, at], t_ref[0]) + dot(lo[:, at], t_ref[0]) + dot(hi[:, at], t_ref[1]))
    return jnp.concatenate(parts, axis=1)


def step_of(hits, v, w):
    gg = jnp.sum(v * hits)
    cc = jnp.sum(w * hits * hits)
    gg = jnp.full((1, 128), gg, jnp.float32)
    cc = jnp.full((1, 128), cc, jnp.float32)
    return gg / (gg + cc + 1e-6)


def iter_kernel(slot_ref, obs_ref, q_ref, tab_ref, t2_ref, *refs, members, coarse_rows, scale2, first):
    if first:
        (part_ref, b_ref, state_ref, lhs_ref, x_ref, bhl_ref) = refs
    else:
        (old_ref, hits_ref, part_ref, b_ref, state_ref, step_ref, lhs_ref, x_ref, bhl_ref) = refs
    slots = q_ref.shape[2]
    cols = x_ref.shape[1]
    half = members * coarse_rows
    target, saturation, live = obs_ref[0], obs_ref[1], obs_ref[2]
    if first:
        observed = jnp.zeros_like(target)
        lam = jnp.zeros_like(target)
    else:
        hits = hits_ref[...]
        step = step_of(hits, old_ref[0], old_ref[1])
        step_ref[...] = step
        observed = old_ref[2] + step[0:1, 0:1] * hits
        lam = old_ref[3] + step[0:1, 0:1] * old_ref[0]
    bounded = jnp.tanh((target - observed) / saturation)
    v = jnp.where(live > 0.5, saturation * bounded, 0.0) - lam
    state_ref[0] = v
    state_ref[1] = jnp.where(live > 0.5, 1.0 - bounded * bounded, 0.0)
    state_ref[2] = observed
    state_ref[3] = lam

    def v_of(d):
        return state_ref[0, pl.ds(slot_ref[d], 1), :]

    scatter(q_ref, tab_ref, v_of, 0, NREL, lhs_ref, x_ref, members, coarse_rows)
    b = lon_filter(x_ref[...], t2_ref)
    b_ref[...] = b
    hi, lo = split(b)
    bhl_ref[:half] = hi
    bhl_ref[half:] = lo
    chunk = 512

    def gather(n, _):
        at = pl.ds(pl.multiple_of(n * chunk, chunk), chunk)
        at_col = q_ref[REACH, members : members + 1, at]
        row = jnp.floor(q_ref[REACH, members + 1 : members + 2, at] * 0.5)
        away = jnp.abs(at_col - full((cols, chunk), 0))
        hat = jnp.maximum(1.0 - jnp.minimum(away, cols - away), 0.0).astype(jnp.bfloat16)
        got = dot(bhl_ref[...], hat)
        mask = jnp.where(full((coarse_rows, chunk), 0) == row, scale2, 0.0)
        total = jnp.zeros((coarse_rows, chunk), jnp.float32)
        for k in range(members):
            r = slice(k * coarse_rows, (k + 1) * coarse_rows)
            r2 = slice(half + k * coarse_rows, half + (k + 1) * coarse_rows)
            total = total + q_ref[REACH, k : k + 1, at] * (got[r] + got[r2])
        part_ref[:, at] = jnp.sum(total * mask, axis=0, keepdims=True)
        return 0

    lax.fori_loop(0, slots // chunk, gather, 0)


def final_kernel(
    slot_ref, state_ref, hits_ref, q_ref, tab_ref, t1_ref, b0_ref, b1_ref, b2_ref, s0_ref, s1_ref, p_ref,
    control_ref, image_ref, lam_ref, lhs_ref, x_ref, *, members, fine_rows, coarse_rows, scale,
):
    hits = hits_ref[...]
    v = state_ref[0]
    step = step_of(hits, v, state_ref[1])[0:1, 0:1]
    lam_ref[...] = state_ref[3] + step * v

    def v_of(d):
        return lam_ref[pl.ds(slot_ref[d], 1), :]

    scatter(q_ref, tab_ref, v_of, REACH - 1, REACH + 2, lhs_ref, x_ref, members, coarse_rows)
    control_ref[...] = scale * lon_filter(x_ref[...], t1_ref)

    b = s0_ref[0:1, 0:1] * b0_ref[...] + s1_ref[0:1, 0:1] * b1_ref[...] + step * b2_ref[...]
    half, cols = b.shape
    wide = 2 * half
    repeat = jnp.where(
        lax.broadcasted_iota(jnp.int32, (wide, half), 0) // 2 == lax.broadcasted_iota(jnp.int32, (wide, half), 1), 1.0, 0.0
    ).astype(jnp.bfloat16)
    hi, lo = split(jnp.concatenate([b, b[:, :EDGE]], axis=1))
    hi = dot(repeat, hi).astype(jnp.bfloat16)
    lo = dot(repeat, lo).astype(jnp.bfloat16)
    hat = jnp.maximum(1.0 - jnp.abs(0.5 * full((2 * EDGE, 2 * EDGE), 1) - full((2 * EDGE, 2 * EDGE), 0)), 0.0)
    hat = hat.astype(jnp.bfloat16)
    for f in range(cols // EDGE):
        at = slice(f * EDGE, f * EDGE + 2 * EDGE)
        fine = slice(2 * f * EDGE, 2 * (f + 1) * EDGE)
        field = dot(hi[:, at], hat) + dot(lo[:, at], hat)
        product = p_ref[:, fine].astype(jnp.float32) * field
        image_ref[:, fine] = (scale * scale) * jnp.sum(product.reshape(members, fine_rows, 2 * EDGE), axis=0)


def swap(a, axis, bit):
    count = lax.axis_size(axis)
    return lax.ppermute(a, axis, [(i, i ^ bit) for i in range(count)])


def gather_lat(a, dim):
    bit = 1
    while bit < lax.axis_size("lat"):
        a = jnp.concatenate([a, swap(a, "lat", bit)], axis=dim)
        bit *= 2
    return a


def sum_mem(a):
    bit = 1
    while bit < lax.axis_size("mem"):
        a = a + swap(a, "mem", bit)
        bit *= 2
    return a


def scatter_mem(a):
    bit = lax.axis_size("mem") // 2
    me = lax.axis_index("mem")
    while bit:
        width = a.shape[1] // 2
        low, high = a[:, :width], a[:, width:]
        upper = (me & bit) != 0
        a = jnp.where(upper, high, low) + swap(jnp.where(upper, low, high), "mem", bit)
        bit //= 2
    return a


def on_device(perturbation, obs_cells, obs_count, innovation, obs_scale):
    bands = lax.axis_size("lat")
    members, fine_rows, lon_cells = perturbation.shape
    coarse_rows = fine_rows // 2
    coarse_cols = lon_cells // 2
    slots = obs_cells.shape[1]
    half = members * coarse_rows
    scale = float((members * lax.axis_size("mem") - 1) ** (-0.5))
    band = lax.axis_index("lat")
    t1, t2 = lon_blocks(coarse_cols)
    tables = lax.dynamic_index_in_dim(jnp.asarray(lat_tables(bands, coarse_rows)), band, 0, keepdims=False)
    slot = (band ^ (band + jnp.arange(NREL, dtype=jnp.int32) - REACH)) & (bands - 1)

    smem = pl.BlockSpec(memory_space=pltpu.SMEM)
    vmem = pl.BlockSpec(memory_space=pltpu.VMEM)
    f32 = functools.partial(jax.ShapeDtypeStruct, dtype=jnp.float32)

    live = (jnp.arange(slots, dtype=jnp.int32)[None] < obs_count[0]).astype(jnp.float32)
    obs = gather_lat(jnp.stack([innovation, obs_scale, live]), 1)

    field = perturbation.reshape(members * fine_rows, lon_cells)
    meta = jnp.concatenate(
        [
            (obs_cells % lon_cells).astype(jnp.float32) * 0.5,
            (obs_cells // lon_cells).astype(jnp.float32),
            jnp.zeros((META - 2, slots), jnp.float32),
        ]
    )
    own = pl.pallas_call(
        functools.partial(pick_kernel, members=members, fine_rows=fine_rows, chunk=256),
        out_shape=f32((members + META, slots)),
        in_specs=[vmem, vmem],
        out_specs=vmem,
        cost_estimate=pl.CostEstimate(flops=4 * 10**9, bytes_accessed=2 * 10**6, transcendentals=0),
        name="pick",
    )(field, meta)
    near = []
    for d in range(-REACH, REACH + 1):
        near.append(lax.ppermute(own, "lat", [(s, s - d) for s in range(bands) if 0 <= s - d < bands]) if d else own)
    near = jnp.stack(near)

    scratch = [pltpu.VMEM((2 * half, slots), jnp.bfloat16), pltpu.VMEM((half, coarse_cols), jnp.float32)]
    state, hits, images, steps = None, None, [], []
    for iteration in range(ITERS):
        first = iteration == 0
        ins = [slot, obs, near, tables[0], t2] + ([] if first else [state, hits])
        outs = [f32((1, slots)), f32((half, coarse_cols)), f32((4, bands, slots))] + ([] if first else [f32((1, 128))])
        got = pl.pallas_call(
            functools.partial(iter_kernel, members=members, coarse_rows=coarse_rows, scale2=scale * scale, first=first),
            out_shape=outs,
            in_specs=[smem] + [vmem] * (len(ins) - 1),
            out_specs=[vmem] * len(outs),
            scratch_shapes=scratch + [pltpu.VMEM((2 * half, coarse_cols), jnp.bfloat16)],
            cost_estimate=pl.CostEstimate(flops=7 * 10**9, bytes_accessed=3 * 10**6, transcendentals=0),
            name="iterate",
        )(*ins)
        part, image, state = got[:3]
        images.append(image)
        steps += got[3:]
        hits = gather_lat(sum_mem(part), 0)
    control, image = pl.pallas_call(
        functools.partial(final_kernel, members=members, fine_rows=fine_rows, coarse_rows=coarse_rows, scale=scale),
        out_shape=[f32((half, coarse_cols)), f32((fine_rows, lon_cells))],
        in_specs=[smem] + [vmem] * 11,
        out_specs=[vmem] * 2,
        scratch_shapes=[pltpu.VMEM((bands, slots), jnp.float32)] + scratch,
        cost_estimate=pl.CostEstimate(flops=5 * 10**9, bytes_accessed=6 * 10**6, transcendentals=0),
        name="finish",
    )(slot, state, hits, near, tables[1], t1, *images, *steps, field)
    return control.reshape(members, coarse_rows, coarse_cols), scatter_mem(image)


def solution(mesh):
    in_specs = (P("mem", "lat", None), P("lat", None), P("lat"), P("lat", None), P("lat", None))
    out_specs = (P("mem", "lat", None), P("lat", "mem"))
    return jax.shard_map(on_device, mesh=mesh, in_specs=in_specs, out_specs=out_specs, check_vma=False)
```

time: 622 us -> 174 us (0.28); the launches traced: 613 us -> 174 us
  local copies, waits for them, and re-layouts: 169 us -> 3.37 us
  blocking collectives: 154 us -> 0 us
  Pallas kernels: 0 us -> 74.7 us
  other arithmetic: 74.9 us -> 8.1 us
  waiting for transfers between devices: 124 us -> 58.2 us
  matrix products: 33.7 us -> 0 us
  between operations: 21.7 us -> 1.63 us
  starting transfers between devices: 35.5 us -> 27.6 us
    psum x6 -> x0, blocking collectives: 154 us -> none  [the longest x3 136 us: on_device(): grad_norm = lax.psum(local_norm, ('mem', 'lat'))]
    pallas_call x0 -> x5, Pallas kernels: none -> 74.7 us  [the longest x3 56.8 us: on_device(): pl.pallas_call(functools.partial(iter_kernel, members=members, coarse_row...]
    gather x3 -> x0, local copies, waits for them, and re-layouts: 50 us -> none  [on_device(): hits = lax.psum(partial_image[row_index, col_index], 'mem')]
    ppermute x12 -> x24, waiting for transfers between devices: 105 us -> 58.2 us  [the longest x20 58.2 us: swap(): return lax.ppermute(a, axis, [(i, i ^ bit) for i in range(count)])]
    reshape x9 -> x0, local copies, waits for them, and re-layouts: 36.3 us -> none  [the longest x3 16.1 us: widen_lon(): jnp.stack([coarse, odd_part], axis=-1)]
    scatter-add x3 -> x0, other arithmetic: 34 us -> none  [on_device(): obs_field = jnp.zeros((fine_rows * lon_cells,), jnp.float32).at[obs_index...]
    dot_general x12 -> x0, matrix products: 33.7 us -> none  [the longest x3 13.1 us: on_device(): jnp.dot(folded, circulant, precision=lax.Precision.HIGHEST, preferred_ele...]
    slice x13 -> x0, local copies, waits for them, and re-layouts: 23.2 us -> none  [the longest x3 21.6 us: narrow_lon(): paired[..., 0] + 0.5 * odd_part + 0.5 * jnp.roll(odd_part, 1, axis=-1)]
  transfers between devices with their start and end apart: 13 -> 24, of which waited for: 7 -> 19; matrix products, arithmetic and copies ran while one was open for 2% -> 2% of each run, Pallas kernels for 0% -> 3%
where the time goes in v1:
time: 174 us
  Pallas kernels  74.7 us (43%)
  waiting for transfers between devices  58.2 us (33%)
  starting transfers between devices  27.6 us (16%)
  other arithmetic  8.1 us (5%)
  local copies, waits for them, and re-layouts  3.37 us (2%)
    ppermute x20, waiting for transfers between devices, swap(): return lax.ppermute(a, axis, [(i, i ^ bit) for i in range(count)])  58.2 us
    pallas_call x3, Pallas kernels, on_device(): pl.pallas_call(functools.partial(iter_kernel, members=members, coarse_row...  56.8 us
    ppermute x20, starting transfers between devices, swap(): return lax.ppermute(a, axis, [(i, i ^ bit) for i in range(count)])  19 us
    pallas_call x1, Pallas kernels, on_device(): pl.pallas_call(functools.partial(final_kernel, members=members, fine_rows...  12.4 us
    ppermute x4, starting transfers between devices, on_device(): lax.ppermute(own, 'lat', [(s, s - d) for s in range(bands) if 0 <= s - d...  8.56 us
    pallas_call x1, Pallas kernels, on_device(): pl.pallas_call(functools.partial(pick_kernel, members=members, fine_rows=...  5.54 us
  transfers between devices with their start and end apart: 24, of which 19 were waited for; matrix products, arithmetic and copies ran while one was open for 2% of the time, Pallas kernels for 3%

profile of v1, /device:TPU:0, one launch (start us, length us, event | category | flops | bytes accessed | tf_op | source)
XLA Modules:
  0.0 173.5 jit_solution(2730632922488794124)
XLA Ops:
  1.4 3.1 %collective-permute-start = (f32[3,1,2048]{2,1,0:T(1,128)S(1)}, f32[3,1,2048]{2,1,0:T(1,128)S(1)}, u32[]{:S(2)}, u32[]{:S(2)}) collective-permute-start(f32[3,1,2048]{2,1,0:T(1,128)S(1)} %pad_maximum_fusion.9), channel_id=1, source_target_pairs={{0,1},{1,0},{2,3},{3,2},{4,5},{5,4},{6,7},{7,6},{8,9},{9,8},{10,11... | collective-permute-start | bytes 73736 | tf_op jit(solution)/shard_map/ppermute | solution.py:229
  5.3 5.5 %pick.1 = f32[24,2048]{1,0:T(8,128)} custom-call(bf16[256,2048]{1,0:T(8,128)(2,1)} %bitcast.28, f32[8,2048]{1,0:T(8,128)} %maximum_maximum_fusion.meta_ref), custom_call_target="tpu_custom_call" | custom-call | flops 4000000000 | bytes 2000000 | tf_op jit(solution)/shard_map/pick/pallas_call | solution.py:288
  10.9 3.5 %collective-permute-start.3 = (f32[24,2048]{1,0:T(8,128)}, f32[24,2048]{1,0:T(8,128)S(1)}, u32[]{:S(2)}, u32[]{:S(2)}) collective-permute-start(f32[24,2048]{1,0:T(8,128)} %pick.1), channel_id=1, source_target_pairs={{0,2},{1,3},{2,4},{3,5},{4,6},{5,7},{8,10},{9,11},{10,12},{11,13},... | collective-permute-start | bytes 589832 | tf_op jit(solution)/shard_map/ppermute | solution.py:298
  14.4 2.5 %collective-permute-start.4 = (f32[24,2048]{1,0:T(8,128)}, f32[24,2048]{1,0:T(8,128)S(1)}, u32[]{:S(2)}, u32[]{:S(2)}) collective-permute-start(f32[24,2048]{1,0:T(8,128)} %pick.1), channel_id=1, source_target_pairs={{0,1},{1,2},{2,3},{3,4},{4,5},{5,6},{6,7},{8,9},{9,10},{10,11},{11... | collective-permute-start | bytes 589832 | tf_op jit(solution)/shard_map/ppermute | solution.py:298
  19.5 5.2 %collective-permute-start.1 = (f32[3,2,2048]{2,1,0:T(2,128)S(1)}, f32[3,2,2048]{2,1,0:T(2,128)S(1)}, u32[]{:S(2)}, u32[]{:S(2)}) collective-permute-start(f32[3,2,2048]{2,1,0:T(2,128)S(1)} %pad_maximum_fusion.5), channel_id=1, source_target_pairs={{0,2},{1,3},{2,0},{3,1},{4,6},{5,7},{6,4},{7,5},{8,10},{9,11},{10,... | collective-permute-start | bytes 147464 | tf_op jit(solution)/shard_map/ppermute | solution.py:229
  24.7 1.4 dynamic-slice_bitcast_fusion
  26.1 5.8 %collective-permute-done.1 = f32[3,2,2048]{2,1,0:T(2,128)S(1)} collective-permute-done((f32[3,2,2048]{2,1,0:T(2,128)S(1)}, f32[3,2,2048]{2,1,0:T(2,128)S(1)}, u32[]{:S(2)}, u32[]{:S(2)}) %collective-permute-start.1) | collective-permute-done | bytes 49184 | tf_op jit(solution)/shard_map/ppermute | solution.py:229
  33.4 4.2 %collective-permute-done.2 = f32[3,4,2048]{2,1,0:T(4,128)S(1)} collective-permute-done((f32[3,4,2048]{2,1,0:T(4,128)S(1)}, f32[3,4,2048]{2,1,0:T(4,128)S(1)}, u32[]{:S(2)}, u32[]{:S(2)}) %collective-permute-start.2) | collective-permute-done | bytes 98336 | tf_op jit(solution)/shard_map/ppermute | solution.py:229
  40.4 18.8 %iterate.3 = (f32[1,2048]{1,0:T(1,128)}, f32[128,1024]{1,0:T(8,128)}, f32[4,8,2048]{2,1,0:T(8,128)}) custom-call(s32[5]{0:T(128)} %xor_and_fusion.slot_ref, f32[3,8,2048]{2,1,0:T(8,128)} %pad_maximum_fusion.obs_ref, f32[5,24,2048]{2,1,0:T(8,128)} %copy-done.4, f32[5,8,128]{2,1,0:T(8,128)} %get-tuple-element.31.tab_ref, bf16[2,512,256]{2,1,0:T(8,128)(2,1)} %constant.73.t2_ref), custom_call_target="tpu_custom_call" | custom-call | flops 7000000000 | bytes 3000000 | tf_op jit(solution)/shard_map/iterate/pallas_call | solution.py:307
  59.2 1.4 collective-permute-done.7
  61.3 1.6 collective-permute-start.8
  62.8 2.2 %collective-permute-done.8 = f32[1,2048]{1,0:T(1,128)S(1)} collective-permute-done((f32[1,2048]{1,0:T(1,128)S(1)}, f32[1,2048]{1,0:T(1,128)S(1)}, u32[]{:S(2)}, u32[]{:S(2)}) %collective-permute-start.8) | collective-permute-done | bytes 8224 | tf_op jit(solution)/shard_map/ppermute | solution.py:229
  65.1 3.6 %collective-permute-done.9 = f32[1,2048]{1,0:T(1,128)S(1)} collective-permute-done((f32[1,2048]{1,0:T(1,128)S(1)}, f32[1,2048]{1,0:T(1,128)S(1)}, u32[]{:S(2)}, u32[]{:S(2)}) %collective-permute-start.9) | collective-permute-done | bytes 8224 | tf_op jit(solution)/shard_map/ppermute | solution.py:229
  68.8 3.7 %collective-permute-done.10 = f32[2,2048]{1,0:T(2,128)S(1)} collective-permute-done((f32[2,2048]{1,0:T(2,128)S(1)}, f32[2,2048]{1,0:T(2,128)S(1)}, u32[]{:S(2)}, u32[]{:S(2)}) %collective-permute-start.10) | collective-permute-done | bytes 16416 | tf_op jit(solution)/shard_map/ppermute | solution.py:229
  73.5 4.0 %collective-permute-done.11 = f32[4,2048]{1,0:T(4,128)S(1)} collective-permute-done((f32[4,2048]{1,0:T(4,128)S(1)}, f32[4,2048]{1,0:T(4,128)S(1)}, u32[]{:S(2)}, u32[]{:S(2)}) %collective-permute-start.11) | collective-permute-done | bytes 32800 | tf_op jit(solution)/shard_map/ppermute | solution.py:229
  78.1 19.0 %iterate.4 = (f32[1,2048]{1,0:T(1,128)}, f32[128,1024]{1,0:T(8,128)}, f32[4,8,2048]{2,1,0:T(8,128)}, f32[1,128]{1,0:T(1,128)}) custom-call(s32[5]{0:T(128)} %xor_and_fusion.slot_ref, f32[3,8,2048]{2,1,0:T(8,128)} %pad_maximum_fusion.obs_ref, f32[5,24,2048]{2,1,0:T(8,128)} %copy-done.4, f32[5,8,128]{2,1,0:T(8,128)} %get-tuple-element.31.tab_ref, ...), custom_call_target="tpu_custom_call" | custom-call | flops 7000000000 | bytes 3000000 | tf_op jit(solution)/shard_map/iterate/pallas_call | solution.py:307
  97.1 1.4 collective-permute-done.12
  99.2 1.6 collective-permute-start.13
  100.7 2.2 %collective-permute-done.13 = f32[1,2048]{1,0:T(1,128)S(1)} collective-permute-done((f32[1,2048]{1,0:T(1,128)S(1)}, f32[1,2048]{1,0:T(1,128)S(1)}, u32[]{:S(2)}, u32[]{:S(2)}) %collective-permute-start.13) | collective-permute-done | bytes 8224 | tf_op jit(solution)/shard_map/ppermute | solution.py:229
  103.0 3.6 %collective-permute-done.14 = f32[1,2048]{1,0:T(1,128)S(1)} collective-permute-done((f32[1,2048]{1,0:T(1,128)S(1)}, f32[1,2048]{1,0:T(1,128)S(1)}, u32[]{:S(2)}, u32[]{:S(2)}) %collective-permute-start.14) | collective-permute-done | bytes 8224 | tf_op jit(solution)/shard_map/ppermute | solution.py:229
  106.7 3.7 %collective-permute-done.15 = f32[2,2048]{1,0:T(2,128)S(1)} collective-permute-done((f32[2,2048]{1,0:T(2,128)S(1)}, f32[2,2048]{1,0:T(2,128)S(1)}, u32[]{:S(2)}, u32[]{:S(2)}) %collective-permute-start.15) | collective-permute-done | bytes 16416 | tf_op jit(solution)/shard_map/ppermute | solution.py:229
  111.6 3.8 %collective-permute-done.16 = f32[4,2048]{1,0:T(4,128)S(1)} collective-permute-done((f32[4,2048]{1,0:T(4,128)S(1)}, f32[4,2048]{1,0:T(4,128)S(1)}, u32[]{:S(2)}, u32[]{:S(2)}) %collective-permute-start.16) | collective-permute-done | bytes 32800 | tf_op jit(solution)/shard_map/ppermute | solution.py:229
  116.0 19.0 %iterate.5 = (f32[1,2048]{1,0:T(1,128)}, f32[128,1024]{1,0:T(8,128)}, f32[4,8,2048]{2,1,0:T(8,128)}, f32[1,128]{1,0:T(1,128)}) custom-call(s32[5]{0:T(128)} %xor_and_fusion.slot_ref, f32[3,8,2048]{2,1,0:T(8,128)} %pad_maximum_fusion.obs_ref, f32[5,24,2048]{2,1,0:T(8,128)} %copy-done.4, f32[5,8,128]{2,1,0:T(8,128)} %get-tuple-element.31.tab_ref, ...), custom_call_target="tpu_custom_call" | custom-call | flops 7000000000 | bytes 3000000 | tf_op jit(solution)/shard_map/iterate/pallas_call | solution.py:307
  135.0 1.4 collective-permute-done.17
  137.1 1.6 collective-permute-start.18
  138.7 2.2 %collective-permute-done.18 = f32[1,2048]{1,0:T(1,128)S(1)} collective-permute-done((f32[1,2048]{1,0:T(1,128)S(1)}, f32[1,2048]{1,0:T(1,128)S(1)}, u32[]{:S(2)}, u32[]{:S(2)}) %collective-permute-start.18) | collective-permute-done | bytes 8224 | tf_op jit(solution)/shard_map/ppermute | solution.py:229
  140.9 3.6 %collective-permute-done.19 = f32[1,2048]{1,0:T(1,128)S(1)} collective-permute-done((f32[1,2048]{1,0:T(1,128)S(1)}, f32[1,2048]{1,0:T(1,128)S(1)}, u32[]{:S(2)}, u32[]{:S(2)}) %collective-permute-start.19) | collective-permute-done | bytes 8224 | tf_op jit(solution)/shard_map/ppermute | solution.py:229
  144.7 3.7 %collective-permute-done.20 = f32[2,2048]{1,0:T(2,128)S(1)} collective-permute-done((f32[2,2048]{1,0:T(2,128)S(1)}, f32[2,2048]{1,0:T(2,128)S(1)}, u32[]{:S(2)}, u32[]{:S(2)}) %collective-permute-start.20) | collective-permute-done | bytes 16416 | tf_op jit(solution)/shard_map/ppermute | solution.py:229
  149.6 3.7 %collective-permute-done.21 = f32[4,2048]{1,0:T(4,128)S(1)} collective-permute-done((f32[4,2048]{1,0:T(4,128)S(1)}, f32[4,2048]{1,0:T(4,128)S(1)}, u32[]{:S(2)}, u32[]{:S(2)}) %collective-permute-start.21) | collective-permute-done | bytes 32800 | tf_op jit(solution)/shard_map/ppermute | solution.py:229
  154.0 12.4 %finish.1 = (f32[128,1024]{1,0:T(8,128)}, f32[16,2048]{1,0:T(8,128)}) custom-call(s32[5]{0:T(128)} %xor_and_fusion.slot_ref, f32[4,8,2048]{2,1,0:T(8,128)} %get-tuple-element.19.state_ref, f32[8,2048]{1,0:T(8,128)} %pad_maximum_fusion.4.hits_ref, f32[5,24,2048]{2,1,0:T(8,128)} %copy-done.4, f32[5,8,128]{2,1,0:T(8,128)} %get-tuple-element.30.tab_ref, ...), custom_call_target="tpu_custom_call" | custom-call | flops 5000000000 | bytes 6000000 | tf_op jit(solution)/shard_map/finish/pallas_call | solution.py:320
  167.3 1.6 collective-permute-start.22
  168.8 2.8 %collective-permute-done.22 = f32[16,1024]{1,0:T(8,128)S(1)} collective-permute-done((f32[16,1024]{1,0:T(8,128)S(1)}, f32[16,1024]{1,0:T(8,128)S(1)}, u32[]{:S(2)}, u32[]{:S(2)}) %collective-permute-start.22) | collective-permute-done | bytes 65568 | tf_op jit(solution)/shard_map/ppermute | solution.py:229
  (69 shorter events, 18.4 us)
Async XLA Ops:
  0.6 0.7 copy-start.3
  0.6 0.7 copy-start.2
  1.4 3.1 %copy-start.5 = (s32[1,2048]{1,0:T(1,128)S(1)}, s32[1,2048]{1,0:T(1,128)}, u32[]{:S(2)}) copy-start(s32[1,2048]{1,0:T(1,128)} %param.9) | copy-start | bytes 24580
  1.4 18.1 %collective-permute-start = (f32[3,1,2048]{2,1,0:T(1,128)S(1)}, f32[3,1,2048]{2,1,0:T(1,128)S(1)}, u32[]{:S(2)}, u32[]{:S(2)}) collective-permute-start(f32[3,1,2048]{2,1,0:T(1,128)S(1)} %pad_maximum_fusion.9), channel_id=1, source_target_pairs={{0,1},{1,0},{2,3},{3,2},{4,5},{5,4},{6,7},{7,6},{8,9},{9,8},{10,11... | collective-permute-start | bytes 73736 | tf_op jit(solution)/shard_map/ppermute | solution.py:229
  10.9 27.5 %collective-permute-start.3 = (f32[24,2048]{1,0:T(8,128)}, f32[24,2048]{1,0:T(8,128)S(1)}, u32[]{:S(2)}, u32[]{:S(2)}) collective-permute-start(f32[24,2048]{1,0:T(8,128)} %pick.1), channel_id=1, source_target_pairs={{0,2},{1,3},{2,4},{3,5},{4,6},{5,7},{8,10},{9,11},{10,12},{11,13},... | collective-permute-start | bytes 589832 | tf_op jit(solution)/shard_map/ppermute | solution.py:298
  14.4 24.1 %collective-permute-start.4 = (f32[24,2048]{1,0:T(8,128)}, f32[24,2048]{1,0:T(8,128)S(1)}, u32[]{:S(2)}, u32[]{:S(2)}) collective-permute-start(f32[24,2048]{1,0:T(8,128)} %pick.1), channel_id=1, source_target_pairs={{0,1},{1,2},{2,3},{3,4},{4,5},{5,6},{6,7},{8,9},{9,10},{10,11},{11... | collective-permute-start | bytes 589832 | tf_op jit(solution)/shard_map/ppermute | solution.py:298
  16.9 22.5 %collective-permute-start.5 = (f32[24,2048]{1,0:T(8,128)}, f32[24,2048]{1,0:T(8,128)S(1)}, u32[]{:S(2)}, u32[]{:S(2)}) collective-permute-start(f32[24,2048]{1,0:T(8,128)} %pick.1), channel_id=1, source_target_pairs={{1,0},{2,1},{3,2},{4,3},{5,4},{6,5},{7,6},{9,8},{10,9},{11,10},{12... | collective-permute-start | bytes 589832 | tf_op jit(solution)/shard_map/ppermute | solution.py:298
  18.2 21.2 %collective-permute-start.6 = (f32[24,2048]{1,0:T(8,128)}, f32[24,2048]{1,0:T(8,128)S(1)}, u32[]{:S(2)}, u32[]{:S(2)}) collective-permute-start(f32[24,2048]{1,0:T(8,128)} %pick.1), channel_id=1, source_target_pairs={{2,0},{3,1},{4,2},{5,3},{6,4},{7,5},{10,8},{11,9},{12,10},{13,11},... | collective-permute-start | bytes 589832 | tf_op jit(solution)/shard_map/ppermute | solution.py:298
  19.5 12.4 %collective-permute-start.1 = (f32[3,2,2048]{2,1,0:T(2,128)S(1)}, f32[3,2,2048]{2,1,0:T(2,128)S(1)}, u32[]{:S(2)}, u32[]{:S(2)}) collective-permute-start(f32[3,2,2048]{2,1,0:T(2,128)S(1)} %pad_maximum_fusion.5), channel_id=1, source_target_pairs={{0,2},{1,3},{2,0},{3,1},{4,6},{5,7},{6,4},{7,5},{8,10},{9,11},{10,... | collective-permute-start | bytes 147464 | tf_op jit(solution)/shard_map/ppermute | solution.py:229
  32.0 5.6 %collective-permute-start.2 = (f32[3,4,2048]{2,1,0:T(4,128)S(1)}, f32[3,4,2048]{2,1,0:T(4,128)S(1)}, u32[]{:S(2)}, u32[]{:S(2)}) collective-permute-start(f32[3,4,2048]{2,1,0:T(4,128)S(1)} %pad_maximum_fusion.1), channel_id=1, source_target_pairs={{0,4},{1,5},{2,6},{3,7},{4,0},{5,1},{6,2},{7,3},{8,12},{9,13},{10,... | collective-permute-start | bytes 294920 | tf_op jit(solution)/shard_map/ppermute | solution.py:229
  38.4 0.9 copy-start.1
  39.4 1.0 copy-start.4
  59.2 1.4 collective-permute-start.7
  61.3 3.7 %collective-permute-start.8 = (f32[1,2048]{1,0:T(1,128)S(1)}, f32[1,2048]{1,0:T(1,128)S(1)}, u32[]{:S(2)}, u32[]{:S(2)}) collective-permute-start(f32[1,2048]{1,0:T(1,128)S(1)} %add.43), channel_id=1, source_target_pairs={{0,16},{8,24},{16,0},{24,8},{1,17},{9,25},{17,1},{25,9},{2,18},{10... | collective-permute-start | bytes 24584 | tf_op jit(solution)/shard_map/ppermute | solution.py:229
  65.0 3.7 %collective-permute-start.9 = (f32[1,2048]{1,0:T(1,128)S(1)}, f32[1,2048]{1,0:T(1,128)S(1)}, u32[]{:S(2)}, u32[]{:S(2)}) collective-permute-start(f32[1,2048]{1,0:T(1,128)S(1)} %add.44), channel_id=1, source_target_pairs={{0,1},{1,0},{2,3},{3,2},{4,5},{5,4},{6,7},{7,6},{8,9},{9,8},{10,11... | collective-permute-start | bytes 24584 | tf_op jit(solution)/shard_map/ppermute | solution.py:229
  68.7 3.8 %collective-permute-start.10 = (f32[2,2048]{1,0:T(2,128)S(1)}, f32[2,2048]{1,0:T(2,128)S(1)}, u32[]{:S(2)}, u32[]{:S(2)}) collective-permute-start(f32[2,2048]{1,0:T(2,128)S(1)} %pad_maximum_fusion.10), channel_id=1, source_target_pairs={{0,2},{1,3},{2,0},{3,1},{4,6},{5,7},{6,4},{7,5},{8,10},{9,11},{10,... | collective-permute-start | bytes 49160 | tf_op jit(solution)/shard_map/ppermute | solution.py:229
  72.6 4.9 %collective-permute-start.11 = (f32[4,2048]{1,0:T(4,128)S(1)}, f32[4,2048]{1,0:T(4,128)S(1)}, u32[]{:S(2)}, u32[]{:S(2)}) collective-permute-start(f32[4,2048]{1,0:T(4,128)S(1)} %pad_maximum_fusion.6), channel_id=1, source_target_pairs={{0,4},{1,5},{2,6},{3,7},{4,0},{5,1},{6,2},{7,3},{8,12},{9,13},{10,... | collective-permute-start | bytes 98312 | tf_op jit(solution)/shard_map/ppermute | solution.py:229
  97.1 1.4 collective-permute-start.12
  99.2 3.7 %collective-permute-start.13 = (f32[1,2048]{1,0:T(1,128)S(1)}, f32[1,2048]{1,0:T(1,128)S(1)}, u32[]{:S(2)}, u32[]{:S(2)}) collective-permute-start(f32[1,2048]{1,0:T(1,128)S(1)} %add.45), channel_id=1, source_target_pairs={{0,16},{8,24},{16,0},{24,8},{1,17},{9,25},{17,1},{25,9},{2,18},{10... | collective-permute-start | bytes 24584 | tf_op jit(solution)/shard_map/ppermute | solution.py:229
  102.9 3.7 %collective-permute-start.14 = (f32[1,2048]{1,0:T(1,128)S(1)}, f32[1,2048]{1,0:T(1,128)S(1)}, u32[]{:S(2)}, u32[]{:S(2)}) collective-permute-start(f32[1,2048]{1,0:T(1,128)S(1)} %add.46), channel_id=1, source_target_pairs={{0,1},{1,0},{2,3},{3,2},{4,5},{5,4},{6,7},{7,6},{8,9},{9,8},{10,11... | collective-permute-start | bytes 24584 | tf_op jit(solution)/shard_map/ppermute | solution.py:229
  106.7 3.8 %collective-permute-start.15 = (f32[2,2048]{1,0:T(2,128)S(1)}, f32[2,2048]{1,0:T(2,128)S(1)}, u32[]{:S(2)}, u32[]{:S(2)}) collective-permute-start(f32[2,2048]{1,0:T(2,128)S(1)} %pad_maximum_fusion.11), channel_id=1, source_target_pairs={{0,2},{1,3},{2,0},{3,1},{4,6},{5,7},{6,4},{7,5},{8,10},{9,11},{10,... | collective-permute-start | bytes 49160 | tf_op jit(solution)/shard_map/ppermute | solution.py:229
  110.5 4.9 %collective-permute-start.16 = (f32[4,2048]{1,0:T(4,128)S(1)}, f32[4,2048]{1,0:T(4,128)S(1)}, u32[]{:S(2)}, u32[]{:S(2)}) collective-permute-start(f32[4,2048]{1,0:T(4,128)S(1)} %pad_maximum_fusion.7), channel_id=1, source_target_pairs={{0,4},{1,5},{2,6},{3,7},{4,0},{5,1},{6,2},{7,3},{8,12},{9,13},{10,... | collective-permute-start | bytes 98312 | tf_op jit(solution)/shard_map/ppermute | solution.py:229
  135.0 1.4 collective-permute-start.17
  137.1 3.7 %collective-permute-start.18 = (f32[1,2048]{1,0:T(1,128)S(1)}, f32[1,2048]{1,0:T(1,128)S(1)}, u32[]{:S(2)}, u32[]{:S(2)}) collective-permute-start(f32[1,2048]{1,0:T(1,128)S(1)} %add.47), channel_id=1, source_target_pairs={{0,16},{8,24},{16,0},{24,8},{1,17},{9,25},{17,1},{25,9},{2,18},{10... | collective-permute-start | bytes 24584 | tf_op jit(solution)/shard_map/ppermute | solution.py:229
  140.9 3.7 %collective-permute-start.19 = (f32[1,2048]{1,0:T(1,128)S(1)}, f32[1,2048]{1,0:T(1,128)S(1)}, u32[]{:S(2)}, u32[]{:S(2)}) collective-permute-start(f32[1,2048]{1,0:T(1,128)S(1)} %add.48), channel_id=1, source_target_pairs={{0,1},{1,0},{2,3},{3,2},{4,5},{5,4},{6,7},{7,6},{8,9},{9,8},{10,11... | collective-permute-start | bytes 24584 | tf_op jit(solution)/shard_map/ppermute | solution.py:229
  144.6 3.8 %collective-permute-start.20 = (f32[2,2048]{1,0:T(2,128)S(1)}, f32[2,2048]{1,0:T(2,128)S(1)}, u32[]{:S(2)}, u32[]{:S(2)}) collective-permute-start(f32[2,2048]{1,0:T(2,128)S(1)} %pad_maximum_fusion.12), channel_id=1, source_target_pairs={{0,2},{1,3},{2,0},{3,1},{4,6},{5,7},{6,4},{7,5},{8,10},{9,11},{10,... | collective-permute-start | bytes 49160 | tf_op jit(solution)/shard_map/ppermute | solution.py:229
  148.4 4.9 %collective-permute-start.21 = (f32[4,2048]{1,0:T(4,128)S(1)}, f32[4,2048]{1,0:T(4,128)S(1)}, u32[]{:S(2)}, u32[]{:S(2)}) collective-permute-start(f32[4,2048]{1,0:T(4,128)S(1)} %pad_maximum_fusion.8), channel_id=1, source_target_pairs={{0,4},{1,5},{2,6},{3,7},{4,0},{5,1},{6,2},{7,3},{8,12},{9,13},{10,... | collective-permute-start | bytes 98312 | tf_op jit(solution)/shard_map/ppermute | solution.py:229
  166.3 5.3 %copy-start = (f32[16,2048]{1,0:T(8,128)S(1)}, f32[16,2048]{1,0:T(8,128)}, u32[]{:S(2)}) copy-start(f32[16,2048]{1,0:T(8,128)} %get-tuple-element.27) | copy-start | bytes 393220
  167.3 4.3 %collective-permute-start.22 = (f32[16,1024]{1,0:T(8,128)S(1)}, f32[16,1024]{1,0:T(8,128)S(1)}, u32[]{:S(2)}, u32[]{:S(2)}) collective-permute-start(f32[16,1024]{1,0:T(8,128)S(1)} %slice_select_fusion), channel_id=1, source_target_pairs={{0,16},{8,24},{16,0},{24,8},{1,17},{9,25},{17,1},{25,9},{2,18},{10... | collective-permute-start | bytes 196616 | tf_op jit(solution)/shard_map/ppermute | solution.py:229
  171.6 1.3 collective-permute-start.23

commit v2 on v1

--- a/solution.py
+++ b/solution.py
@@ -65,6 +65,15 @@
     return lax.broadcasted_iota(jnp.int32, ref_shape, dim).astype(jnp.float32)
 
 
+def hat_of(x, count):
+    middle = 0.5 * (count - 1)
+    near = x - middle
+    near = jnp.where(jnp.abs(near) > middle + 0.75, float(count), near).astype(jnp.bfloat16)
+    j = (full((count, x.shape[1]), 0) - middle).astype(jnp.bfloat16)
+    one = jnp.asarray(1, jnp.bfloat16)
+    return jnp.maximum(one - jnp.abs(near - j), jnp.asarray(0, jnp.bfloat16))
+
+
 def pick_kernel(p_ref, meta_ref, out_ref, *, members, fine_rows, chunk):
     lon = p_ref.shape[1]
     slots = meta_ref.shape[1]
@@ -105,8 +114,7 @@
         def block(c, _):
             base = (c * BLK).astype(jnp.float32)
             near = jnp.where(jnp.logical_and(c == 0, at_col > cols - 1.0), at_col - float(cols), at_col)
-            hat = jnp.maximum(1.0 - jnp.abs((near - base) - full((BLK, slots), 0)), 0.0)
-            got = dot(lhs_ref[...], hat.astype(jnp.bfloat16), ((1,), (1,)))
+            got = dot(lhs_ref[...], hat_of(near - base, BLK), ((1,), (1,)))
             at = pl.ds(pl.multiple_of(c * BLK, BLK), BLK)
             x_ref[:, at] = x_ref[:, at] + (got[:half] + got[half:])
             return 0
@@ -128,41 +136,59 @@
 
 
 def step_of(hits, v, w):
-    gg = jnp.sum(v * hits)
-    cc = jnp.sum(w * hits * hits)
-    gg = jnp.full((1, 128), gg, jnp.float32)
-    cc = jnp.full((1, 128), cc, jnp.float32)
+    gg = jnp.full((1, 128), jnp.sum(v * hits), jnp.float32)
+    cc = jnp.full((1, 128), jnp.sum(w * hits * hits), jnp.float32)
     return gg / (gg + cc + 1e-6)
 
 
-def iter_kernel(slot_ref, obs_ref, q_ref, tab_ref, t2_ref, *refs, members, coarse_rows, scale2, first):
-    if first:
-        (part_ref, b_ref, state_ref, lhs_ref, x_ref, bhl_ref) = refs
+def sum_mem(parts):
+    return lambda bands: jnp.sum(parts.reshape(parts.shape[0] // bands, bands, parts.shape[1]), axis=0)
+
+
+def pull_of(target, saturation, live):
+    bounded = jnp.tanh(target / saturation)
+    return (
+        jnp.where(live > 0.5, saturation * bounded, 0.0),
+        jnp.where(live > 0.5, 1.0 - bounded * bounded, 0.0),
+    )
+
+
+def iter_kernel(slot_ref, q_ref, tab_ref, t2_ref, *refs, members, coarse_rows, scale2, order):
+    slots = q_ref.shape[2]
+    if order == 0:
+        part_ref, b_ref, lhs_ref, x_ref, bhl_ref = refs
+
+        def v_of(d):
+            rows = q_ref[d, members : members + META, :]
+            return pull_of(rows[2:3], rows[3:4], rows[4:5])[0]
+
     else:
-        (old_ref, hits_ref, part_ref, b_ref, state_ref, step_ref, lhs_ref, x_ref, bhl_ref) = refs
-    slots = q_ref.shape[2]
+        old_ref, hits_ref, part_ref, b_ref, state_ref, step_ref, lhs_ref, x_ref, bhl_ref = refs
+        bands = old_ref.shape[1]
+        hits = sum_mem(hits_ref[...])(bands)
+        if order == 1:
+            for b in range(bands):
+                state_ref[0:3, b : b + 1, :] = old_ref[:, pl.ds(slot_ref[1, b], 1), :]
+            v, w = pull_of(state_ref[0], state_ref[1], state_ref[2])
+            observed, lam = 0.0, 0.0
+        else:
+            state_ref[0:3] = old_ref[0:3]
+            v, w, observed, lam = old_ref[3], old_ref[4], old_ref[5], old_ref[6]
+        step = step_of(hits, v, w)
+        step_ref[...] = step
+        observed = observed + step[0:1, 0:1] * hits
+        lam = lam + step[0:1, 0:1] * v
+        pull, weight = pull_of(state_ref[0] - observed, state_ref[1], state_ref[2])
+        state_ref[3] = pull - lam
+        state_ref[4] = weight
+        state_ref[5] = observed
+        state_ref[6] = lam
+
+        def v_of(d):
+            return state_ref[3, pl.ds(slot_ref[0, d], 1), :]
+
     cols = x_ref.shape[1]
     half = members * coarse_rows
-    target, saturation, live = obs_ref[0], obs_ref[1], obs_ref[2]
-    if first:
-        observed = jnp.zeros_like(target)
-        lam = jnp.zeros_like(target)
-    else:
-        hits = hits_ref[...]
-        step = step_of(hits, old_ref[0], old_ref[1])
-        step_ref[...] = step
-        observed = old_ref[2] + step[0:1, 0:1] * hits
-        lam = old_ref[3] + step[0:1, 0:1] * old_ref[0]
-    bounded = jnp.tanh((target - observed) / saturation)
-    v = jnp.where(live > 0.5, saturation * bounded, 0.0) - lam
-    state_ref[0] = v
-    state_ref[1] = jnp.where(live > 0.5, 1.0 - bounded * bounded, 0.0)
-    state_ref[2] = observed
-    state_ref[3] = lam
-
-    def v_of(d):
-        return state_ref[0, pl.ds(slot_ref[d], 1), :]
-
     scatter(q_ref, tab_ref, v_of, 0, NREL, lhs_ref, x_ref, members, coarse_rows)
     b = lon_filter(x_ref[...], t2_ref)
     b_ref[...] = b
@@ -175,8 +201,9 @@
         at = pl.ds(pl.multiple_of(n * chunk, chunk), chunk)
         at_col = q_ref[REACH, members : members + 1, at]
         row = jnp.floor(q_ref[REACH, members + 1 : members + 2, at] * 0.5)
-        away = jnp.abs(at_col - full((cols, chunk), 0))
-        hat = jnp.maximum(1.0 - jnp.minimum(away, cols - away), 0.0).astype(jnp.bfloat16)
+        hats = [hat_of(jnp.where(at_col > cols - 1.0, at_col - float(cols), at_col), BLK)]
+        hats += [hat_of(at_col - float(c * BLK), BLK) for c in range(1, cols // BLK)]
+        hat = jnp.concatenate(hats, axis=0)
         got = dot(bhl_ref[...], hat)
         mask = jnp.where(full((coarse_rows, chunk), 0) == row, scale2, 0.0)
         total = jnp.zeros((coarse_rows, chunk), jnp.float32)
@@ -184,7 +211,7 @@
             r = slice(k * coarse_rows, (k + 1) * coarse_rows)
             r2 = slice(half + k * coarse_rows, half + (k + 1) * coarse_rows)
             total = total + q_ref[REACH, k : k + 1, at] * (got[r] + got[r2])
-        part_ref[:, at] = jnp.sum(total * mask, axis=0, keepdims=True)
+        part_ref[:, at] = jnp.broadcast_to(jnp.sum(total * mask, axis=0, keepdims=True), (part_ref.shape[0], chunk))
         return 0
 
     lax.fori_loop(0, slots // chunk, gather, 0)
@@ -194,13 +221,13 @@
     slot_ref, state_ref, hits_ref, q_ref, tab_ref, t1_ref, b0_ref, b1_ref, b2_ref, s0_ref, s1_ref, p_ref,
     control_ref, image_ref, lam_ref, lhs_ref, x_ref, *, members, fine_rows, coarse_rows, scale,
 ):
-    hits = hits_ref[...]
-    v = state_ref[0]
-    step = step_of(hits, v, state_ref[1])[0:1, 0:1]
-    lam_ref[...] = state_ref[3] + step * v
+    hits = sum_mem(hits_ref[...])(state_ref.shape[1])
+    v = state_ref[3]
+    step = step_of(hits, v, state_ref[4])[0:1, 0:1]
+    lam_ref[...] = state_ref[6] + step * v
 
     def v_of(d):
-        return lam_ref[pl.ds(slot_ref[d], 1), :]
+        return lam_ref[pl.ds(slot_ref[0, d], 1), :]
 
     scatter(q_ref, tab_ref, v_of, REACH - 1, REACH + 2, lhs_ref, x_ref, members, coarse_rows)
     control_ref[...] = scale * lon_filter(x_ref[...], t1_ref)
@@ -237,14 +264,6 @@
     return a
 
 
-def sum_mem(a):
-    bit = 1
-    while bit < lax.axis_size("mem"):
-        a = a + swap(a, "mem", bit)
-        bit *= 2
-    return a
-
-
 def scatter_mem(a):
     bit = lax.axis_size("mem") // 2
     me = lax.axis_index("mem")
@@ -268,7 +287,8 @@
     band = lax.axis_index("lat")
     t1, t2 = lon_blocks(coarse_cols)
     tables = lax.dynamic_index_in_dim(jnp.asarray(lat_tables(bands, coarse_rows)), band, 0, keepdims=False)
-    slot = (band ^ (band + jnp.arange(NREL, dtype=jnp.int32) - REACH)) & (bands - 1)
+    every = jnp.arange(max(NREL, bands), dtype=jnp.int32)
+    slot = jnp.stack([jnp.clip(band + every - REACH, 0, bands - 1), (band ^ every) & (bands - 1)])
 
     smem = pl.BlockSpec(memory_space=pltpu.SMEM)
     vmem = pl.BlockSpec(memory_space=pltpu.VMEM)
@@ -282,7 +302,10 @@
         [
             (obs_cells % lon_cells).astype(jnp.float32) * 0.5,
             (obs_cells // lon_cells).astype(jnp.float32),
-            jnp.zeros((META - 2, slots), jnp.float32),
+            innovation,
+            obs_scale,
+            live,
+            jnp.zeros((META - 5, slots), jnp.float32),
         ]
     )
     own = pl.pallas_call(
@@ -299,13 +322,15 @@
     near = jnp.stack(near)
 
     scratch = [pltpu.VMEM((2 * half, slots), jnp.bfloat16), pltpu.VMEM((half, coarse_cols), jnp.float32)]
-    state, hits, images, steps = None, None, [], []
+    state, hits, images, steps = obs, None, [], []
+    devices = bands * lax.axis_size("mem")
     for iteration in range(ITERS):
-        first = iteration == 0
-        ins = [slot, obs, near, tables[0], t2] + ([] if first else [state, hits])
-        outs = [f32((1, slots)), f32((half, coarse_cols)), f32((4, bands, slots))] + ([] if first else [f32((1, 128))])
+        ins = [slot, near, tables[0], t2] + ([state, hits] if iteration else [])
+        outs = [f32((devices, slots)), f32((half, coarse_cols))] + ([f32((7, bands, slots)), f32((1, 128))] if iteration else [])
         got = pl.pallas_call(
-            functools.partial(iter_kernel, members=members, coarse_rows=coarse_rows, scale2=scale * scale, first=first),
+            functools.partial(
+                iter_kernel, members=members, coarse_rows=coarse_rows, scale2=scale * scale, order=min(iteration, 2)
+            ),
             out_shape=outs,
             in_specs=[smem] + [vmem] * (len(ins) - 1),
             out_specs=[vmem] * len(outs),
@@ -313,10 +338,11 @@
             cost_estimate=pl.CostEstimate(flops=7 * 10**9, bytes_accessed=3 * 10**6, transcendentals=0),
             name="iterate",
         )(*ins)
-        part, image, state = got[:3]
-        images.append(image)
-        steps += got[3:]
-        hits = gather_lat(sum_mem(part), 0)
+        images.append(got[1])
+        if iteration:
+            state = got[2]
+            steps.append(got[3])
+        hits = lax.all_to_all(got[0], ("mem", "lat"), 0, 0, tiled=True)
     control, image = pl.pallas_call(
         functools.partial(final_kernel, members=members, fine_rows=fine_rows, coarse_rows=coarse_rows, scale=scale),
         out_shape=[f32((half, coarse_cols)), f32((fine_rows, lon_cells))],

time: 174 us -> 155 us (0.89)
  waiting for transfers between devices: 58.2 us -> 27.5 us
  blocking collectives: 0 us -> 13.9 us
  local copies, waits for them, and re-layouts: 3.37 us -> 12.1 us
  Pallas kernels: 74.7 us -> 67.2 us
  other arithmetic: 8.1 us -> 3.85 us
    ppermute x20 -> x5, waiting for transfers between devices: 58.2 us -> 17.1 us  [swap(): return lax.ppermute(a, axis, [(i, i ^ bit) for i in range(count)])]
    all_to_all x0 -> x1, blocking collectives: none -> 13.9 us  [on_device(): hits = lax.all_to_all(got[0], ('mem', 'lat'), 0, 0, tiled=True)]
    all_to_all x0 -> x2, waiting for transfers between devices: none -> 10.4 us  [on_device(): hits = lax.all_to_all(got[0], ('mem', 'lat'), 0, 0, tiled=True)]
    ppermute x20 -> x5, starting transfers between devices: 19 us -> 10.8 us  [swap(): return lax.ppermute(a, axis, [(i, i ^ bit) for i in range(count)])]
    pallas_call x3, Pallas kernels: 56.8 us -> 49.9 us  [on_device(): pl.pallas_call(functools.partial(iter_kernel, members=members, coarse_row...]
    all_to_all x0 -> x2, starting transfers between devices: none -> 6.36 us  [on_device(): hits = lax.all_to_all(got[0], ('mem', 'lat'), 0, 0, tiled=True)]
    all_to_all x0 -> x3, local copies, waits for them, and re-layouts: none -> 5.06 us  [on_device(): hits = lax.all_to_all(got[0], ('mem', 'lat'), 0, 0, tiled=True)]
    unnamed x16 -> x17, local copies, waits for them, and re-layouts: 1.92 us -> 4.96 us
  transfers between devices with their start and end apart: 24 -> 11, of which waited for: 19 -> 5; matrix products, arithmetic and copies ran while one was open for 2% -> 3% of each run, Pallas kernels for 3% -> 11%
where the time goes in v2:
time: 155 us; the launch traced here: 154 us
  Pallas kernels  67.2 us (43%)
  starting transfers between devices  28.1 us (18%)
  waiting for transfers between devices  27.5 us (18%)
  blocking collectives  13.9 us (9%)
  local copies, waits for them, and re-layouts  12.1 us (8%)
  other arithmetic  3.85 us (2%)
    pallas_call x3, Pallas kernels, on_device(): pl.pallas_call(functools.partial(iter_kernel, members=members, coarse_row...  49.9 us
    ppermute x5, waiting for transfers between devices, swap(): return lax.ppermute(a, axis, [(i, i ^ bit) for i in range(count)])  17.1 us
    all_to_all x1, blocking collectives, on_device(): hits = lax.all_to_all(got[0], ('mem', 'lat'), 0, 0, tiled=True)  13.9 us
    pallas_call x1, Pallas kernels, on_device(): pl.pallas_call(functools.partial(final_kernel, members=members, fine_rows...  11.7 us
    ppermute x4, starting transfers between devices, on_device(): lax.ppermute(own, 'lat', [(s, s - d) for s in range(bands) if 0 <= s - d...  11 us
    ppermute x5, starting transfers between devices, swap(): return lax.ppermute(a, axis, [(i, i ^ bit) for i in range(count)])  10.8 us
    all_to_all x2, waiting for transfers between devices, on_device(): hits = lax.all_to_all(got[0], ('mem', 'lat'), 0, 0, tiled=True)  10.4 us
    all_to_all x2, starting transfers between devices, on_device(): hits = lax.all_to_all(got[0], ('mem', 'lat'), 0, 0, tiled=True)  6.36 us
  transfers between devices with their start and end apart: 11, of which 5 were waited for; matrix products, arithmetic and copies ran while one was open for 3% of the time, Pallas kernels for 11%

profile of v2, /device:TPU:0, one launch (start us, length us, event | category | flops | bytes accessed | tf_op | source)
XLA Modules:
  0.0 154.1 jit_solution(7393363701621647479)
XLA Ops:
  1.3 0.7 fusion.2
  3.5 5.5 %pick.1 = f32[24,2048]{1,0:T(8,128)} custom-call(bf16[256,2048]{1,0:T(8,128)(2,1)} %bitcast.47, f32[8,2048]{1,0:T(8,128)} %concatenate.14.meta_ref), custom_call_target="tpu_custom_call" | custom-call | flops 4000000000 | bytes 2000000 | tf_op jit(solution)/shard_map/pick/pallas_call | solution.py:311
  9.0 5.0 %collective-permute-start = (f32[24,2048]{1,0:T(8,128)}, f32[24,2048]{1,0:T(8,128)S(1)}, u32[]{:S(2)}, u32[]{:S(2)}) collective-permute-start(f32[24,2048]{1,0:T(8,128)} %pick.1), channel_id=1, source_target_pairs={{0,2},{1,3},{2,4},{3,5},{4,6},{5,7},{8,10},{9,11},{10,12},{11,13},... | collective-permute-start | bytes 589832 | tf_op jit(solution)/shard_map/ppermute | solution.py:321
  14.0 3.4 %collective-permute-start.1 = (f32[24,2048]{1,0:T(8,128)}, f32[24,2048]{1,0:T(8,128)S(1)}, u32[]{:S(2)}, u32[]{:S(2)}) collective-permute-start(f32[24,2048]{1,0:T(8,128)} %pick.1), channel_id=1, source_target_pairs={{0,1},{1,2},{2,3},{3,4},{4,5},{5,6},{6,7},{8,9},{9,10},{10,11},{11... | collective-permute-start | bytes 589832 | tf_op jit(solution)/shard_map/ppermute | solution.py:321
  17.4 1.3 collective-permute-start.2
  18.7 1.3 collective-permute-start.3
  20.1 2.7 %collective-permute-start.4 = (f32[3,1,2048]{2,1,0:T(1,128)S(1)}, f32[3,1,2048]{2,1,0:T(1,128)S(1)}, u32[]{:S(2)}, u32[]{:S(2)}) collective-permute-start(f32[3,1,2048]{2,1,0:T(1,128)S(1)} %pad_maximum_fusion.3), channel_id=1, source_target_pairs={{0,1},{1,0},{2,3},{3,2},{4,5},{5,4},{6,7},{7,6},{8,9},{9,8},{10,11... | collective-permute-start | bytes 73736 | tf_op jit(solution)/shard_map/ppermute | solution.py:256
  22.8 1.4 dynamic-slice_bitcast_fusion
  24.7 1.4 collective-permute-done.4
  26.2 4.6 %collective-permute-start.5 = (f32[3,2,2048]{2,1,0:T(2,128)S(1)}, f32[3,2,2048]{2,1,0:T(2,128)S(1)}, u32[]{:S(2)}, u32[]{:S(2)}) collective-permute-start(f32[3,2,2048]{2,1,0:T(2,128)S(1)} %pad_maximum_fusion.2), channel_id=1, source_target_pairs={{0,2},{1,3},{2,0},{3,1},{4,6},{5,7},{6,4},{7,5},{8,10},{9,11},{10,... | collective-permute-start | bytes 147464 | tf_op jit(solution)/shard_map/ppermute | solution.py:256
  30.9 0.9 copy-done.3
  31.9 1.0 copy-done.4
  32.8 16.4 %iterate.3 = (f32[32,2048]{1,0:T(8,128)}, f32[128,1024]{1,0:T(8,128)}) custom-call(s32[2,8]{1,0:T(2,128)} %pad_add_fusion.slot_ref, f32[5,24,2048]{2,1,0:T(8,128)} %copy-done.4, f32[5,8,128]{2,1,0:T(8,128)} %get-tuple-element.29.tab_ref, bf16[2,512,256]{2,1,0:T(8,128)(2,1)} %constant.74.t2_ref), custom_call_target="tpu_custom_call" | custom-call | flops 7000000000 | bytes 3000000 | tf_op jit(solution)/shard_map/iterate/pallas_call | solution.py:330
  49.2 1.9 %copy.10 = f32[32,1,2048]{2,1,0:T(1,128)} copy(f32[32,1,2048]{2,0,1:T(8,128)} %bitcast.38) | data formatting | bytes 524288 | tf_op jit(solution)/shard_map/all_to_all | solution.py:345
  51.2 3.8 %all-to-all-start = ((f32[32,1,2048]{2,1,0:T(1,128)}), f32[32,1,2048]{2,1,0:T(1,128)S(1)}, u32[]{:S(2)}, u32[]{:S(2)}) async-start(f32[32,1,2048]{2,1,0:T(1,128)} %copy.10), calls=%async_computation | async-start | bytes 524288 | tf_op jit(solution)/shard_map/all_to_all | solution.py:345
  55.0 2.7 %collective-permute-start.6 = (f32[3,4,2048]{2,1,0:T(4,128)S(1)}, f32[3,4,2048]{2,1,0:T(4,128)S(1)}, u32[]{:S(2)}, u32[]{:S(2)}) collective-permute-start(f32[3,4,2048]{2,1,0:T(4,128)S(1)} %pad_maximum_fusion.1), channel_id=1, source_target_pairs={{0,4},{1,5},{2,6},{3,7},{4,0},{5,1},{6,2},{7,3},{8,12},{9,13},{10,... | collective-permute-start | bytes 294920 | tf_op jit(solution)/shard_map/ppermute | solution.py:256
  57.8 10.7 %collective-permute-done.6 = f32[3,4,2048]{2,1,0:T(4,128)S(1)} collective-permute-done((f32[3,4,2048]{2,1,0:T(4,128)S(1)}, f32[3,4,2048]{2,1,0:T(4,128)S(1)}, u32[]{:S(2)}, u32[]{:S(2)}) %collective-permute-start.6) | collective-permute-done | bytes 98336 | tf_op jit(solution)/shard_map/ppermute | solution.py:256
  68.5 0.8 pad_maximum_fusion.refs_0_
  69.3 0.8 copy.21
  70.1 16.8 %iterate.4 = (f32[32,2048]{1,0:T(8,128)}, f32[128,1024]{1,0:T(8,128)}, f32[7,8,2048]{2,1,0:T(8,128)}, f32[1,128]{1,0:T(1,128)}) custom-call(s32[2,8]{1,0:T(2,128)} %pad_add_fusion.slot_ref, f32[5,24,2048]{2,1,0:T(8,128)} %copy-done.4, f32[5,8,128]{2,1,0:T(8,128)} %get-tuple-element.29.tab_ref, bf16[2,512,256]{2,1,0:T(8,128)(2,1)} %constant.74.t2_ref, ...), custom_call_target="tpu_custom_call" | custom-call | flops 7000000000 | bytes 3000000 | tf_op jit(solution)/shard_map/iterate/pallas_call | solution.py:330
  86.9 1.2 copy.11
  88.1 13.9 %all_to_all.33 = f32[32,1,2048]{2,1,0:T(1,128)S(1)} all-to-all(f32[32,1,2048]{2,1,0:T(1,128)S(1)} %copy.11), channel_id=1, replica_groups=mesh['mem'=4,'lat'=8] {'mem','lat'}, dimensions={0} | all-to-all | bytes 524288 | tf_op jit(solution)/shard_map/all_to_all | solution.py:345
  102.0 0.8 copy.20
  102.8 16.8 %iterate.5 = (f32[32,2048]{1,0:T(8,128)}, f32[128,1024]{1,0:T(8,128)}, f32[7,8,2048]{2,1,0:T(8,128)}, f32[1,128]{1,0:T(1,128)}) custom-call(s32[2,8]{1,0:T(2,128)} %pad_add_fusion.slot_ref, f32[5,24,2048]{2,1,0:T(8,128)} %copy-done.4, f32[5,8,128]{2,1,0:T(8,128)} %get-tuple-element.29.tab_ref, bf16[2,512,256]{2,1,0:T(8,128)(2,1)} %constant.74.t2_ref, ...), custom_call_target="tpu_custom_call" | custom-call | flops 7000000000 | bytes 3000000 | tf_op jit(solution)/shard_map/iterate/pallas_call | solution.py:330
  119.5 1.9 %copy.12 = f32[32,1,2048]{2,1,0:T(1,128)} copy(f32[32,1,2048]{2,0,1:T(8,128)} %bitcast.35) | data formatting | bytes 524288 | tf_op jit(solution)/shard_map/all_to_all | solution.py:345
  121.5 2.6 %all-to-all-start.2 = ((f32[32,1,2048]{2,1,0:T(1,128)}), f32[32,1,2048]{2,1,0:T(1,128)S(1)}, u32[]{:S(2)}, u32[]{:S(2)}) async-start(f32[32,1,2048]{2,1,0:T(1,128)} %copy.12), calls=%async_computation.2 | async-start | bytes 524288 | tf_op jit(solution)/shard_map/all_to_all | solution.py:345
  124.1 10.4 %all-to-all-done.2 = f32[32,1,2048]{2,1,0:T(1,128)S(1)} async-done(((f32[32,1,2048]{2,1,0:T(1,128)}), f32[32,1,2048]{2,1,0:T(1,128)S(1)}, u32[]{:S(2)}, u32[]{:S(2)}) %all-to-all-start.2) | async-done | bytes 262176 | tf_op jit(solution)/shard_map/all_to_all | solution.py:345
  134.5 0.8 copy.19
  135.3 11.7 %finish.1 = (f32[128,1024]{1,0:T(8,128)}, f32[16,2048]{1,0:T(8,128)}) custom-call(s32[2,8]{1,0:T(2,128)} %pad_add_fusion.slot_ref, f32[7,8,2048]{2,1,0:T(8,128)} %get-tuple-element.17.state_ref, f32[32,2048]{1,0:T(8,128)} %bitcast.33, f32[5,24,2048]{2,1,0:T(8,128)} %copy-done.4, f32[5,8,128]{2,1,0:T(8,128)} %get-tuple-element.28.tab_ref, ...), custom_call_target="tpu_custom_call" | custom-call | flops 5000000000 | bytes 6000000 | tf_op jit(solution)/shard_map/finish/pallas_call | solution.py:346
  147.0 0.9 slice_select_fusion
  148.5 3.7 %collective-permute-done.7 = f32[16,1024]{1,0:T(8,128)S(1)} collective-permute-done((f32[16,1024]{1,0:T(8,128)S(1)}, f32[16,1024]{1,0:T(8,128)S(1)}, u32[]{:S(2)}, u32[]{:S(2)}) %collective-permute-start.7) | collective-permute-done | bytes 65568 | tf_op jit(solution)/shard_map/ppermute | solution.py:256
  152.3 1.2 collective-permute-done.8
  (34 shorter events, 3.6 us)
Async XLA Ops:
  2.1 0.7 copy-start.1
  2.1 0.7 copy-start.2
  9.0 21.8 %collective-permute-start = (f32[24,2048]{1,0:T(8,128)}, f32[24,2048]{1,0:T(8,128)S(1)}, u32[]{:S(2)}, u32[]{:S(2)}) collective-permute-start(f32[24,2048]{1,0:T(8,128)} %pick.1), channel_id=1, source_target_pairs={{0,2},{1,3},{2,4},{3,5},{4,6},{5,7},{8,10},{9,11},{10,12},{11,13},... | collective-permute-start | bytes 589832 | tf_op jit(solution)/shard_map/ppermute | solution.py:321
  14.0 16.9 %collective-permute-start.1 = (f32[24,2048]{1,0:T(8,128)}, f32[24,2048]{1,0:T(8,128)S(1)}, u32[]{:S(2)}, u32[]{:S(2)}) collective-permute-start(f32[24,2048]{1,0:T(8,128)} %pick.1), channel_id=1, source_target_pairs={{0,1},{1,2},{2,3},{3,4},{4,5},{5,6},{6,7},{8,9},{9,10},{10,11},{11... | collective-permute-start | bytes 589832 | tf_op jit(solution)/shard_map/ppermute | solution.py:321
  17.4 14.4 %collective-permute-start.2 = (f32[24,2048]{1,0:T(8,128)}, f32[24,2048]{1,0:T(8,128)S(1)}, u32[]{:S(2)}, u32[]{:S(2)}) collective-permute-start(f32[24,2048]{1,0:T(8,128)} %pick.1), channel_id=1, source_target_pairs={{1,0},{2,1},{3,2},{4,3},{5,4},{6,5},{7,6},{9,8},{10,9},{11,10},{12... | collective-permute-start | bytes 589832 | tf_op jit(solution)/shard_map/ppermute | solution.py:321
  18.7 13.1 %collective-permute-start.3 = (f32[24,2048]{1,0:T(8,128)}, f32[24,2048]{1,0:T(8,128)S(1)}, u32[]{:S(2)}, u32[]{:S(2)}) collective-permute-start(f32[24,2048]{1,0:T(8,128)} %pick.1), channel_id=1, source_target_pairs={{2,0},{3,1},{4,2},{5,3},{6,4},{7,5},{10,8},{11,9},{12,10},{13,11},... | collective-permute-start | bytes 589832 | tf_op jit(solution)/shard_map/ppermute | solution.py:321
  20.1 6.1 %collective-permute-start.4 = (f32[3,1,2048]{2,1,0:T(1,128)S(1)}, f32[3,1,2048]{2,1,0:T(1,128)S(1)}, u32[]{:S(2)}, u32[]{:S(2)}) collective-permute-start(f32[3,1,2048]{2,1,0:T(1,128)S(1)} %pad_maximum_fusion.3), channel_id=1, source_target_pairs={{0,1},{1,0},{2,3},{3,2},{4,5},{5,4},{6,7},{7,6},{8,9},{9,8},{10,11... | collective-permute-start | bytes 73736 | tf_op jit(solution)/shard_map/ppermute | solution.py:256
  26.2 28.8 %collective-permute-start.5 = (f32[3,2,2048]{2,1,0:T(2,128)S(1)}, f32[3,2,2048]{2,1,0:T(2,128)S(1)}, u32[]{:S(2)}, u32[]{:S(2)}) collective-permute-start(f32[3,2,2048]{2,1,0:T(2,128)S(1)} %pad_maximum_fusion.2), channel_id=1, source_target_pairs={{0,2},{1,3},{2,0},{3,1},{4,6},{5,7},{6,4},{7,5},{8,10},{9,11},{10,... | collective-permute-start | bytes 147464 | tf_op jit(solution)/shard_map/ppermute | solution.py:256
  30.9 0.9 copy-start.3
  31.9 1.0 copy-start.4
  51.2 18.1 %all-to-all-start = ((f32[32,1,2048]{2,1,0:T(1,128)}), f32[32,1,2048]{2,1,0:T(1,128)S(1)}, u32[]{:S(2)}, u32[]{:S(2)}) async-start(f32[32,1,2048]{2,1,0:T(1,128)} %copy.10), calls=%async_computation | async-start | bytes 524288 | tf_op jit(solution)/shard_map/all_to_all | solution.py:345
  55.0 13.5 %collective-permute-start.6 = (f32[3,4,2048]{2,1,0:T(4,128)S(1)}, f32[3,4,2048]{2,1,0:T(4,128)S(1)}, u32[]{:S(2)}, u32[]{:S(2)}) collective-permute-start(f32[3,4,2048]{2,1,0:T(4,128)S(1)} %pad_maximum_fusion.1), channel_id=1, source_target_pairs={{0,4},{1,5},{2,6},{3,7},{4,0},{5,1},{6,2},{7,3},{8,12},{9,13},{10,... | collective-permute-start | bytes 294920 | tf_op jit(solution)/shard_map/ppermute | solution.py:256
  121.5 13.0 %all-to-all-start.2 = ((f32[32,1,2048]{2,1,0:T(1,128)}), f32[32,1,2048]{2,1,0:T(1,128)S(1)}, u32[]{:S(2)}, u32[]{:S(2)}) async-start(f32[32,1,2048]{2,1,0:T(1,128)} %copy.12), calls=%async_computation.2 | async-start | bytes 524288 | tf_op jit(solution)/shard_map/all_to_all | solution.py:345
  146.9 5.3 %copy-start = (f32[16,2048]{1,0:T(8,128)S(1)}, f32[16,2048]{1,0:T(8,128)}, u32[]{:S(2)}) copy-start(f32[16,2048]{1,0:T(8,128)} %get-tuple-element.25) | copy-start | bytes 393220
  147.9 4.3 %collective-permute-start.7 = (f32[16,1024]{1,0:T(8,128)S(1)}, f32[16,1024]{1,0:T(8,128)S(1)}, u32[]{:S(2)}, u32[]{:S(2)}) collective-permute-start(f32[16,1024]{1,0:T(8,128)S(1)} %slice_select_fusion), channel_id=1, source_target_pairs={{0,16},{8,24},{16,0},{24,8},{1,17},{9,25},{17,1},{25,9},{2,18},{10... | collective-permute-start | bytes 196616 | tf_op jit(solution)/shard_map/ppermute | solution.py:256
  152.2 1.3 collective-permute-start.8

commit v3 on v2

--- a/solution.py
+++ b/solution.py
@@ -103,8 +103,9 @@
         row = jnp.floor(q_ref[d, members + 1 : members + 2, :] * 0.5)
         v = v_of(d)
         weights = jnp.zeros((coarse_rows, slots), jnp.float32)
+        taps = tab(d)
         for r in range(coarse_rows):
-            weights = jnp.where(row == float(r), tab[d, :, r : r + 1], weights)
+            weights = jnp.where(row == float(r), taps[:, r : r + 1], weights)
         weights = weights * v
         for k in range(members):
             hi, lo = split(weights * q_ref[d, k : k + 1, :])
@@ -141,61 +142,70 @@
     return gg / (gg + cc + 1e-6)
 
 
-def sum_mem(parts):
-    return lambda bands: jnp.sum(parts.reshape(parts.shape[0] // bands, bands, parts.shape[1]), axis=0)
-
-
-def pull_of(target, saturation, live):
-    bounded = jnp.tanh(target / saturation)
-    return (
-        jnp.where(live > 0.5, saturation * bounded, 0.0),
-        jnp.where(live > 0.5, 1.0 - bounded * bounded, 0.0),
-    )
-
-
-def iter_kernel(slot_ref, q_ref, tab_ref, t2_ref, *refs, members, coarse_rows, scale2, order):
+def sum_mem(parts, bands):
+    return jnp.sum(parts.reshape((parts.shape[0] // bands, bands) + parts.shape[1:]), axis=0)
+
+
+def pull_of(target, signed):
+    bounded = jnp.tanh(target / jnp.abs(signed))
+    return jnp.where(signed > 0.0, signed * bounded, 0.0), jnp.where(signed > 0.0, 1.0 - bounded * bounded, 0.0)
+
+
+def lay_rows(rows_ref, tile_of, bands):
+    for d in range(NREL):
+        tile = tile_of(jnp.clip(bands[0] + d - REACH, 0, bands[1] - 1))
+        for i in range(tile.shape[0]):
+            rows_ref[d : d + 1, i * 128 : (i + 1) * 128] = tile[i : i + 1, :]
+
+
+def iter_kernel(place_ref, q_ref, tab_ref, t2_ref, *refs, members, coarse_rows, scale2, order, bands, groups):
     slots = q_ref.shape[2]
+    tiles = slots // 128
+    share = tiles // groups
+    band = place_ref[1]
     if order == 0:
-        part_ref, b_ref, lhs_ref, x_ref, bhl_ref = refs
-
-        def v_of(d):
-            rows = q_ref[d, members : members + META, :]
-            return pull_of(rows[2:3], rows[3:4], rows[4:5])[0]
-
+        part_ref, b_ref, lhs_ref, x_ref, bhl_ref, rows_ref = refs
+        for d in range(NREL):
+            rows_ref[d : d + 1, :] = pull_of(q_ref[d, members + 2 : members + 3, :], q_ref[d, members + 3 : members + 4, :])[0]
     else:
-        old_ref, hits_ref, part_ref, b_ref, state_ref, step_ref, lhs_ref, x_ref, bhl_ref = refs
-        bands = old_ref.shape[1]
-        hits = sum_mem(hits_ref[...])(bands)
+        old_ref, hits_ref, part_ref, b_ref, state_ref, step_ref, lhs_ref, x_ref, bhl_ref, rows_ref = refs
+        hits = sum_mem(hits_ref[:, :tiles, :], bands)
         if order == 1:
-            for b in range(bands):
-                state_ref[0:3, b : b + 1, :] = old_ref[:, pl.ds(slot_ref[1, b], 1), :]
-            v, w = pull_of(state_ref[0], state_ref[1], state_ref[2])
+            for g in range(groups):
+                mine = slice(g * bands, (g + 1) * bands)
+                at = slice(g * share, (g + 1) * share)
+                state_ref[0, :, at, :] = hits_ref[mine, tiles : tiles + share, :]
+                state_ref[1, :, at, :] = hits_ref[mine, tiles + share : tiles + 2 * share, :]
+            v, w = pull_of(state_ref[0], state_ref[1])
             observed, lam = 0.0, 0.0
         else:
-            state_ref[0:3] = old_ref[0:3]
-            v, w, observed, lam = old_ref[3], old_ref[4], old_ref[5], old_ref[6]
+            state_ref[0:2] = old_ref[0:2]
+            v, w, observed, lam = old_ref[2], old_ref[3], old_ref[4], old_ref[5]
         step = step_of(hits, v, w)
         step_ref[...] = step
-        observed = observed + step[0:1, 0:1] * hits
-        lam = lam + step[0:1, 0:1] * v
-        pull, weight = pull_of(state_ref[0] - observed, state_ref[1], state_ref[2])
-        state_ref[3] = pull - lam
-        state_ref[4] = weight
-        state_ref[5] = observed
-        state_ref[6] = lam
-
-        def v_of(d):
-            return state_ref[3, pl.ds(slot_ref[0, d], 1), :]
+        step = step[0:1, 0:1][None]
+        observed = observed + step * hits
+        lam = lam + step * v
+        pull, weight = pull_of(state_ref[0] - observed, state_ref[1])
+        state_ref[2] = pull - lam
+        state_ref[3] = weight
+        state_ref[4] = observed
+        state_ref[5] = lam
+        lay_rows(rows_ref, lambda b: state_ref[2, b], (band, bands))
+
+    def v_of(d):
+        return rows_ref[pl.ds(d, 1), :]
 
     cols = x_ref.shape[1]
     half = members * coarse_rows
-    scatter(q_ref, tab_ref, v_of, 0, NREL, lhs_ref, x_ref, members, coarse_rows)
+    scatter(q_ref, lambda d: tab_ref[band, 0, d], v_of, 0, NREL, lhs_ref, x_ref, members, coarse_rows)
     b = lon_filter(x_ref[...], t2_ref)
     b_ref[...] = b
     hi, lo = split(b)
     bhl_ref[:half] = hi
     bhl_ref[half:] = lo
     chunk = 512
+    per = chunk // 128
 
     def gather(n, _):
         at = pl.ds(pl.multiple_of(n * chunk, chunk), chunk)
@@ -211,25 +221,37 @@
             r = slice(k * coarse_rows, (k + 1) * coarse_rows)
             r2 = slice(half + k * coarse_rows, half + (k + 1) * coarse_rows)
             total = total + q_ref[REACH, k : k + 1, at] * (got[r] + got[r2])
-        part_ref[:, at] = jnp.broadcast_to(jnp.sum(total * mask, axis=0, keepdims=True), (part_ref.shape[0], chunk))
+        part = jnp.sum(total * mask, axis=0, keepdims=True)
+        for i in range(per):
+            part_ref[0, pl.ds(n * per + i, 1), :] = part[:, i * 128 : (i + 1) * 128]
         return 0
 
     lax.fori_loop(0, slots // chunk, gather, 0)
+    if order == 0:
+        for r in range(2):
+            mine = pl.ds(pl.multiple_of(place_ref[0] * (share * 128), 128), share * 128)
+            row = q_ref[REACH, members + 2 + r : members + 3 + r, mine]
+            for i in range(share):
+                to = tiles + r * share + i
+                part_ref[0, to : to + 1, :] = row[:, i * 128 : (i + 1) * 128]
+    part_ref[1:] = jnp.broadcast_to(part_ref[0][None], (part_ref.shape[0] - 1,) + part_ref.shape[1:])
 
 
 def final_kernel(
-    slot_ref, state_ref, hits_ref, q_ref, tab_ref, t1_ref, b0_ref, b1_ref, b2_ref, s0_ref, s1_ref, p_ref,
-    control_ref, image_ref, lam_ref, lhs_ref, x_ref, *, members, fine_rows, coarse_rows, scale,
+    place_ref, state_ref, hits_ref, q_ref, tab_ref, t1_ref, b0_ref, b1_ref, b2_ref, s0_ref, s1_ref, p_ref,
+    control_ref, image_ref, lam_ref, lhs_ref, x_ref, rows_ref, *, members, fine_rows, coarse_rows, scale,
 ):
-    hits = sum_mem(hits_ref[...])(state_ref.shape[1])
-    v = state_ref[3]
-    step = step_of(hits, v, state_ref[4])[0:1, 0:1]
-    lam_ref[...] = state_ref[6] + step * v
+    bands = state_ref.shape[1]
+    hits = sum_mem(hits_ref[...], bands)
+    v = state_ref[2]
+    step = step_of(hits, v, state_ref[3])[0:1, 0:1]
+    lam_ref[...] = state_ref[5] + step[None] * v
+    lay_rows(rows_ref, lambda b: lam_ref[b], (place_ref[1], bands))
 
     def v_of(d):
-        return lam_ref[pl.ds(slot_ref[0, d], 1), :]
-
-    scatter(q_ref, tab_ref, v_of, REACH - 1, REACH + 2, lhs_ref, x_ref, members, coarse_rows)
+        return rows_ref[pl.ds(d, 1), :]
+
+    scatter(q_ref, lambda d: tab_ref[place_ref[1], 1, d], v_of, REACH - 1, REACH + 2, lhs_ref, x_ref, members, coarse_rows)
     control_ref[...] = scale * lon_filter(x_ref[...], t1_ref)
 
     b = s0_ref[0:1, 0:1] * b0_ref[...] + s1_ref[0:1, 0:1] * b1_ref[...] + step * b2_ref[...]
@@ -256,14 +278,6 @@
     return lax.ppermute(a, axis, [(i, i ^ bit) for i in range(count)])
 
 
-def gather_lat(a, dim):
-    bit = 1
-    while bit < lax.axis_size("lat"):
-        a = jnp.concatenate([a, swap(a, "lat", bit)], axis=dim)
-        bit *= 2
-    return a
-
-
 def scatter_mem(a):
     bit = lax.axis_size("mem") // 2
     me = lax.axis_index("mem")
@@ -284,28 +298,24 @@
     slots = obs_cells.shape[1]
     half = members * coarse_rows
     scale = float((members * lax.axis_size("mem") - 1) ** (-0.5))
-    band = lax.axis_index("lat")
     t1, t2 = lon_blocks(coarse_cols)
-    tables = lax.dynamic_index_in_dim(jnp.asarray(lat_tables(bands, coarse_rows)), band, 0, keepdims=False)
-    every = jnp.arange(max(NREL, bands), dtype=jnp.int32)
-    slot = jnp.stack([jnp.clip(band + every - REACH, 0, bands - 1), (band ^ every) & (bands - 1)])
+    tables = jnp.asarray(lat_tables(bands, coarse_rows))
+    groups = lax.axis_size("mem")
+    place = jnp.stack([lax.axis_index("mem"), lax.axis_index("lat")]).astype(jnp.int32)
 
     smem = pl.BlockSpec(memory_space=pltpu.SMEM)
     vmem = pl.BlockSpec(memory_space=pltpu.VMEM)
     f32 = functools.partial(jax.ShapeDtypeStruct, dtype=jnp.float32)
 
-    live = (jnp.arange(slots, dtype=jnp.int32)[None] < obs_count[0]).astype(jnp.float32)
-    obs = gather_lat(jnp.stack([innovation, obs_scale, live]), 1)
-
+    live = jnp.arange(slots, dtype=jnp.int32)[None] < obs_count[0]
     field = perturbation.reshape(members * fine_rows, lon_cells)
     meta = jnp.concatenate(
         [
             (obs_cells % lon_cells).astype(jnp.float32) * 0.5,
             (obs_cells // lon_cells).astype(jnp.float32),
             innovation,
-            obs_scale,
-            live,
-            jnp.zeros((META - 5, slots), jnp.float32),
+            jnp.where(live, obs_scale, -obs_scale),
+            jnp.zeros((META - 4, slots), jnp.float32),
         ]
     )
     own = pl.pallas_call(
@@ -321,20 +331,23 @@
         near.append(lax.ppermute(own, "lat", [(s, s - d) for s in range(bands) if 0 <= s - d < bands]) if d else own)
     near = jnp.stack(near)
 
+    rows = pltpu.VMEM((8, slots), jnp.float32)
     scratch = [pltpu.VMEM((2 * half, slots), jnp.bfloat16), pltpu.VMEM((half, coarse_cols), jnp.float32)]
-    state, hits, images, steps = obs, None, [], []
-    devices = bands * lax.axis_size("mem")
+    tiles = slots // 128
+    state, hits, images, steps = None, None, [], []
     for iteration in range(ITERS):
-        ins = [slot, near, tables[0], t2] + ([state, hits] if iteration else [])
-        outs = [f32((devices, slots)), f32((half, coarse_cols))] + ([f32((7, bands, slots)), f32((1, 128))] if iteration else [])
+        order = min(iteration, 2)
+        ins = [place, near, tables, t2] + [[], [obs_cells, hits], [state, hits]][order]
+        block = (groups * bands, tiles + (0 if iteration else 2 * (tiles // groups)), 128)
+        outs = [f32(block), f32((half, coarse_cols))] + ([f32((6, bands, tiles, 128)), f32((1, 128))] if iteration else [])
         got = pl.pallas_call(
             functools.partial(
-                iter_kernel, members=members, coarse_rows=coarse_rows, scale2=scale * scale, order=min(iteration, 2)
+                iter_kernel, members=members, coarse_rows=coarse_rows, scale2=scale * scale, order=order, bands=bands, groups=groups
             ),
             out_shape=outs,
             in_specs=[smem] + [vmem] * (len(ins) - 1),
             out_specs=[vmem] * len(outs),
-            scratch_shapes=scratch + [pltpu.VMEM((2 * half, coarse_cols), jnp.bfloat16)],
+            scratch_shapes=scratch + [pltpu.VMEM((2 * half, coarse_cols), jnp.bfloat16), rows],
             cost_estimate=pl.CostEstimate(flops=7 * 10**9, bytes_accessed=3 * 10**6, transcendentals=0),
             name="iterate",
         )(*ins)
@@ -348,10 +361,10 @@
         out_shape=[f32((half, coarse_cols)), f32((fine_rows, lon_cells))],
         in_specs=[smem] + [vmem] * 11,
         out_specs=[vmem] * 2,
-        scratch_shapes=[pltpu.VMEM((bands, slots), jnp.float32)] + scratch,
+        scratch_shapes=[pltpu.VMEM((bands, tiles, 128), jnp.float32)] + scratch + [rows],
         cost_estimate=pl.CostEstimate(flops=5 * 10**9, bytes_accessed=6 * 10**6, transcendentals=0),
         name="finish",
-    )(slot, state, hits, near, tables[1], t1, *images, *steps, field)
+    )(place, state, hits, near, tables, t1, *images, *steps, field)
     return control.reshape(members, coarse_rows, coarse_cols), scatter_mem(image)
 
 

time: 155 us -> 146 us (0.942)
  blocking collectives: 13.9 us -> 30.4 us
  starting transfers between devices: 28.1 us -> 14.2 us
  local copies, waits for them, and re-layouts: 12.1 us -> 3.11 us
  waiting for transfers between devices: 27.5 us -> 25.4 us
    all_to_all x1 -> x2, blocking collectives: 13.9 us -> 30.4 us  [on_device(): hits = lax.all_to_all(got[0], ('mem', 'lat'), 0, 0, tiled=True)]
    ppermute x5 -> x2, waiting for transfers between devices: 17.1 us -> 4.91 us  [swap(): return lax.ppermute(a, axis, [(i, i ^ bit) for i in range(count)])]
    ppermute x5 -> x2, starting transfers between devices: 10.8 us -> 0.68 us  [swap(): return lax.ppermute(a, axis, [(i, i ^ bit) for i in range(count)])]
    ppermute x4, waiting for transfers between devices: 0.01 us -> 10.1 us  [on_device(): lax.ppermute(own, 'lat', [(s, s - d) for s in range(bands) if 0 <= s - d...]
    all_to_all x3 -> x0, local copies, waits for them, and re-layouts: 5.06 us -> none  [on_device(): hits = lax.all_to_all(got[0], ('mem', 'lat'), 0, 0, tiled=True)]
    all_to_all x2 -> x1, starting transfers between devices: 6.36 us -> 2.58 us  [on_device(): hits = lax.all_to_all(got[0], ('mem', 'lat'), 0, 0, tiled=True)]
    unnamed x17 -> x16, local copies, waits for them, and re-layouts: 4.96 us -> 2.4 us
    all_to_all x2 -> x1, waiting for transfers between devices: 10.4 us -> 10.4 us  [on_device(): hits = lax.all_to_all(got[0], ('mem', 'lat'), 0, 0, tiled=True)]
  transfers between devices with their start and end apart: 11 -> 7, of which waited for: 5 -> 6; matrix products, arithmetic and copies ran while one was open for 3% -> 0% of each run, Pallas kernels for 11% -> 0%
where the time goes in v3:
time: 146 us; the launch traced here: 145 us
  Pallas kernels  67.5 us (46%)
  blocking collectives  30.4 us (21%)
  waiting for transfers between devices  25.4 us (17%)
  starting transfers between devices  14.2 us (10%)
  local copies, waits for them, and re-layouts  3.11 us (2%)
  other arithmetic  2.93 us (2%)
    pallas_call x3, Pallas kernels, on_device(): pl.pallas_call(functools.partial(iter_kernel, members=members, coarse_row...  50.2 us
    all_to_all x2, blocking collectives, on_device(): hits = lax.all_to_all(got[0], ('mem', 'lat'), 0, 0, tiled=True)  30.4 us
    pallas_call x1, Pallas kernels, on_device(): pl.pallas_call(functools.partial(final_kernel, members=members, fine_rows...  11.7 us
    ppermute x4, starting transfers between devices, on_device(): lax.ppermute(own, 'lat', [(s, s - d) for s in range(bands) if 0 <= s - d...  11 us
    all_to_all x1, waiting for transfers between devices, on_device(): hits = lax.all_to_all(got[0], ('mem', 'lat'), 0, 0, tiled=True)  10.4 us
    ppermute x4, waiting for transfers between devices, on_device(): lax.ppermute(own, 'lat', [(s, s - d) for s in range(bands) if 0 <= s - d...  10.1 us
    pallas_call x1, Pallas kernels, on_device(): pl.pallas_call(functools.partial(pick_kernel, members=members, fine_rows=...  5.54 us
    ppermute x2, waiting for transfers between devices, swap(): return lax.ppermute(a, axis, [(i, i ^ bit) for i in range(count)])  4.91 us
  transfers between devices with their start and end apart: 7, of which 6 were waited for; matrix products, arithmetic and copies ran while one was open for 0% of the time, Pallas kernels for 0%

profile of v3, /device:TPU:0, one launch (start us, length us, event | category | flops | bytes accessed | tf_op | source)
XLA Modules:
  0.0 145.1 jit_solution(12667160604296565032)
XLA Ops:
  0.6 0.7 fusion.2
  2.1 0.0 copy-start.4
  2.1 0.7 copy-done.4
  2.8 0.7 concatenate.3.meta_ref
  3.5 5.5 %pick.1 = f32[24,2048]{1,0:T(8,128)} custom-call(bf16[256,2048]{1,0:T(8,128)(2,1)} %bitcast.16, f32[8,2048]{1,0:T(8,128)} %concatenate.3.meta_ref), custom_call_target="tpu_custom_call" | custom-call | flops 4000000000 | bytes 2000000 | tf_op jit(solution)/shard_map/pick/pallas_call | solution.py:321
  9.0 5.0 %collective-permute-start = (f32[24,2048]{1,0:T(8,128)}, f32[24,2048]{1,0:T(8,128)S(1)}, u32[]{:S(2)}, u32[]{:S(2)}) collective-permute-start(f32[24,2048]{1,0:T(8,128)} %pick.1), channel_id=1, source_target_pairs={{0,2},{1,3},{2,4},{3,5},{4,6},{5,7},{8,10},{9,11},{10,12},{11,13},... | collective-permute-start | bytes 589832 | tf_op jit(solution)/shard_map/ppermute | solution.py:331
  14.0 3.4 %collective-permute-start.1 = (f32[24,2048]{1,0:T(8,128)}, f32[24,2048]{1,0:T(8,128)S(1)}, u32[]{:S(2)}, u32[]{:S(2)}) collective-permute-start(f32[24,2048]{1,0:T(8,128)} %pick.1), channel_id=1, source_target_pairs={{0,1},{1,2},{2,3},{3,4},{4,5},{5,6},{6,7},{8,9},{9,10},{10,11},{11... | collective-permute-start | bytes 589832 | tf_op jit(solution)/shard_map/ppermute | solution.py:331
  17.4 1.3 collective-permute-start.2
  18.7 1.3 collective-permute-start.3
  20.0 0.6 pad_add_fusion.place_ref
  20.6 0.0 collective-permute-done
  20.6 0.0 copy-start.2
  20.7 1.0 collective-permute-done.1
  21.6 0.0 copy-done.2
  21.7 3.9 %collective-permute-done.2 = f32[24,2048]{1,0:T(8,128)S(1)} collective-permute-done((f32[24,2048]{1,0:T(8,128)}, f32[24,2048]{1,0:T(8,128)S(1)}, u32[]{:S(2)}, u32[]{:S(2)}) %collective-permute-start.2) | collective-permute-done | bytes 196640 | tf_op jit(solution)/shard_map/ppermute | solution.py:331
  25.6 5.2 %collective-permute-done.3 = f32[24,2048]{1,0:T(8,128)S(1)} collective-permute-done((f32[24,2048]{1,0:T(8,128)}, f32[24,2048]{1,0:T(8,128)S(1)}, u32[]{:S(2)}, u32[]{:S(2)}) %collective-permute-start.3) | collective-permute-done | bytes 196640 | tf_op jit(solution)/shard_map/ppermute | solution.py:331
  30.8 1.0 copy-done.3
  31.8 16.6 %iterate.3 = (f32[32,24,128]{2,1,0:T(8,128)}, f32[128,1024]{1,0:T(8,128)}) custom-call(s32[2]{0:T(128)} %pad_add_fusion.place_ref, f32[5,24,2048]{2,1,0:T(8,128)} %copy-done.3, f32[8,2,5,8,128]{4,3,2,1,0:T(8,128)} %constant.52.clone.tab_ref, bf16[2,512,256]{2,1,0:T(8,128)(2,1)} %constant.63.t2_ref), custom_call_target="tpu_custom_call" | custom-call | flops 7000000000 | bytes 3000000 | tf_op jit(solution)/shard_map/iterate/pallas_call | solution.py:343
  48.3 16.7 %all_to_all.15.refs_1_ = f32[32,24,128]{2,1,0:T(8,128)} all-to-all(f32[32,24,128]{2,1,0:T(8,128)} %get-tuple-element.14), channel_id=1, replica_groups=mesh['mem'=4,'lat'=8] {'mem','lat'}, dimensions={0} | all-to-all | bytes 786432 | tf_op jit(solution)/shard_map/all_to_all | solution.py:358
  65.1 16.8 %iterate.4 = (f32[32,16,128]{2,1,0:T(8,128)}, f32[128,1024]{1,0:T(8,128)}, f32[6,8,16,128]{3,2,1,0:T(8,128)}, f32[1,128]{1,0:T(1,128)}) custom-call(s32[2]{0:T(128)} %pad_add_fusion.place_ref, f32[5,24,2048]{2,1,0:T(8,128)} %copy-done.3, f32[8,2,5,8,128]{4,3,2,1,0:T(8,128)} %constant.52.clone.tab_ref, bf16[2,512,256]{2,1,0:T(8,128)(2,1)} %constant.63.t2_ref, ...), custom_call_target="tpu_custom_call" | custom-call | flops 7000000000 | bytes 3000000 | tf_op jit(solution)/shard_map/iterate/pallas_call | solution.py:343
  81.9 13.7 %all_to_all.16.refs_1_ = f32[32,16,128]{2,1,0:T(8,128)} all-to-all(f32[32,16,128]{2,1,0:T(8,128)} %get-tuple-element.16), channel_id=1, replica_groups=mesh['mem'=4,'lat'=8] {'mem','lat'}, dimensions={0} | all-to-all | bytes 524288 | tf_op jit(solution)/shard_map/all_to_all | solution.py:358
  95.6 16.8 %iterate.5 = (f32[32,16,128]{2,1,0:T(8,128)}, f32[128,1024]{1,0:T(8,128)}, f32[6,8,16,128]{3,2,1,0:T(8,128)}, f32[1,128]{1,0:T(1,128)}) custom-call(s32[2]{0:T(128)} %pad_add_fusion.place_ref, f32[5,24,2048]{2,1,0:T(8,128)} %copy-done.3, f32[8,2,5,8,128]{4,3,2,1,0:T(8,128)} %constant.52.clone.tab_ref, bf16[2,512,256]{2,1,0:T(8,128)(2,1)} %constant.63.t2_ref, ...), custom_call_target="tpu_custom_call" | custom-call | flops 7000000000 | bytes 3000000 | tf_op jit(solution)/shard_map/iterate/pallas_call | solution.py:343
  112.5 2.6 %all-to-all-start.2 = ((f32[32,16,128]{2,1,0:T(8,128)}), f32[32,16,128]{2,1,0:T(8,128)S(1)}, u32[]{:S(2)}, u32[]{:S(2)}) async-start(f32[32,16,128]{2,1,0:T(8,128)} %get-tuple-element.18), calls=%async_computation.2 | async-start | bytes 524288 | tf_op jit(solution)/shard_map/all_to_all | solution.py:358
  115.0 10.4 %all-to-all-done.2.hits_ref = f32[32,16,128]{2,1,0:T(8,128)S(1)} async-done(((f32[32,16,128]{2,1,0:T(8,128)}), f32[32,16,128]{2,1,0:T(8,128)S(1)}, u32[]{:S(2)}, u32[]{:S(2)}) %all-to-all-start.2) | async-done | bytes 262176 | tf_op jit(solution)/shard_map/all_to_all | solution.py:358
  125.5 0.7 copy-done.1
  126.2 11.7 %finish.1 = (f32[128,1024]{1,0:T(8,128)}, f32[16,2048]{1,0:T(8,128)}) custom-call(s32[2]{0:T(128)} %pad_add_fusion.place_ref, f32[6,8,16,128]{3,2,1,0:T(8,128)} %get-tuple-element.17.state_ref, f32[32,16,128]{2,1,0:T(8,128)} %copy-done.1, f32[5,24,2048]{2,1,0:T(8,128)} %copy-done.3, f32[8,2,5,8,128]{4,3,2,1,0:T(8,128)} %constant.52.clone.tab_ref, ...), custom_call_target="tpu_custom_call" | custom-call | flops 5000000000 | bytes 6000000 | tf_op jit(solution)/shard_map/finish/pallas_call | solution.py:359
  137.9 0.9 slice_select_fusion
  138.9 0.6 collective-permute-start.4
  139.5 3.7 %collective-permute-done.4 = f32[16,1024]{1,0:T(8,128)S(1)} collective-permute-done((f32[16,1024]{1,0:T(8,128)S(1)}, f32[16,1024]{1,0:T(8,128)S(1)}, u32[]{:S(2)}, u32[]{:S(2)}) %collective-permute-start.4) | collective-permute-done | bytes 65568 | tf_op jit(solution)/shard_map/ppermute | solution.py:278
  143.2 0.1 collective-permute-start.5
  143.3 1.2 collective-permute-done.5
  144.5 0.6 select_add_fusion.1
  (15 shorter events, 0.1 us)
Async XLA Ops:
  0.6 1.4 copy-start.5
  2.1 0.7 copy-start.4
  9.0 11.6 %collective-permute-start = (f32[24,2048]{1,0:T(8,128)}, f32[24,2048]{1,0:T(8,128)S(1)}, u32[]{:S(2)}, u32[]{:S(2)}) collective-permute-start(f32[24,2048]{1,0:T(8,128)} %pick.1), channel_id=1, source_target_pairs={{0,2},{1,3},{2,4},{3,5},{4,6},{5,7},{8,10},{9,11},{10,12},{11,13},... | collective-permute-start | bytes 589832 | tf_op jit(solution)/shard_map/ppermute | solution.py:331
  14.0 7.7 %collective-permute-start.1 = (f32[24,2048]{1,0:T(8,128)}, f32[24,2048]{1,0:T(8,128)S(1)}, u32[]{:S(2)}, u32[]{:S(2)}) collective-permute-start(f32[24,2048]{1,0:T(8,128)} %pick.1), channel_id=1, source_target_pairs={{0,1},{1,2},{2,3},{3,4},{4,5},{5,6},{6,7},{8,9},{9,10},{10,11},{11... | collective-permute-start | bytes 589832 | tf_op jit(solution)/shard_map/ppermute | solution.py:331
  17.4 8.2 %collective-permute-start.2 = (f32[24,2048]{1,0:T(8,128)}, f32[24,2048]{1,0:T(8,128)S(1)}, u32[]{:S(2)}, u32[]{:S(2)}) collective-permute-start(f32[24,2048]{1,0:T(8,128)} %pick.1), channel_id=1, source_target_pairs={{1,0},{2,1},{3,2},{4,3},{5,4},{6,5},{7,6},{9,8},{10,9},{11,10},{12... | collective-permute-start | bytes 589832 | tf_op jit(solution)/shard_map/ppermute | solution.py:331
  18.7 12.1 %collective-permute-start.3 = (f32[24,2048]{1,0:T(8,128)}, f32[24,2048]{1,0:T(8,128)S(1)}, u32[]{:S(2)}, u32[]{:S(2)}) collective-permute-start(f32[24,2048]{1,0:T(8,128)} %pick.1), channel_id=1, source_target_pairs={{2,0},{3,1},{4,2},{5,3},{6,4},{7,5},{10,8},{11,9},{12,10},{13,11},... | collective-permute-start | bytes 589832 | tf_op jit(solution)/shard_map/ppermute | solution.py:331
  20.6 1.0 copy-start.2
  30.8 1.0 copy-start.3
  112.5 13.0 %all-to-all-start.2 = ((f32[32,16,128]{2,1,0:T(8,128)}), f32[32,16,128]{2,1,0:T(8,128)S(1)}, u32[]{:S(2)}, u32[]{:S(2)}) async-start(f32[32,16,128]{2,1,0:T(8,128)} %get-tuple-element.18), calls=%async_computation.2 | async-start | bytes 524288 | tf_op jit(solution)/shard_map/all_to_all | solution.py:358
  125.5 0.7 copy-start.1
  137.9 5.3 %copy-start = (f32[16,2048]{1,0:T(8,128)S(1)}, f32[16,2048]{1,0:T(8,128)}, u32[]{:S(2)}) copy-start(f32[16,2048]{1,0:T(8,128)} %get-tuple-element.25) | copy-start | bytes 393220
  138.9 4.3 %collective-permute-start.4 = (f32[16,1024]{1,0:T(8,128)S(1)}, f32[16,1024]{1,0:T(8,128)S(1)}, u32[]{:S(2)}, u32[]{:S(2)}) collective-permute-start(f32[16,1024]{1,0:T(8,128)S(1)} %slice_select_fusion), channel_id=1, source_target_pairs={{0,16},{8,24},{16,0},{24,8},{1,17},{9,25},{17,1},{25,9},{2,18},{10... | collective-permute-start | bytes 196616 | tf_op jit(solution)/shard_map/ppermute | solution.py:278
  143.2 1.3 collective-permute-start.5

commit v4 on v3

--- a/solution.py
+++ b/solution.py
@@ -16,6 +16,7 @@
 BLK = 256
 EDGE = 128
 META = 8
+WINDOW = 768
 
 
 def lat_tables(bands, coarse_rows):
@@ -74,34 +75,113 @@
     return jnp.maximum(one - jnp.abs(near - j), jnp.asarray(0, jnp.bfloat16))
 
 
-def pick_kernel(p_ref, meta_ref, out_ref, *, members, fine_rows, chunk):
+def pieces(a):
+    out = []
+    for _ in range(3):
+        out.append(a.astype(jnp.bfloat16))
+        a = a - out[-1].astype(jnp.float32)
+    return out
+
+
+def count(mask):
+    return jnp.sum(jnp.where(mask, 1.0, 0.0)).astype(jnp.int32)
+
+
+def prepare_kernel(p_ref, meta_ref, out_ref, key_ref, kcol_ref, srt_ref, *, members, fine_rows):
     lon = p_ref.shape[1]
     slots = meta_ref.shape[1]
-
-    def body(n, _):
-        at = pl.ds(pl.multiple_of(n * chunk, chunk), chunk)
-        col = 2.0 * meta_ref[0:1, at]
-        row = meta_ref[1:2, at]
-        one = jnp.where(full((lon, chunk), 0) == col, 1.0, 0.0).astype(jnp.bfloat16)
-        got = dot(p_ref[...], one).reshape(members, fine_rows, chunk)
-        mask = jnp.where(full((fine_rows, chunk), 0) == row, 1.0, 0.0)
-        out_ref[0:members, at] = jnp.sum(got * mask[None], axis=1)
-        out_ref[members : members + META, at] = meta_ref[:, at]
+    col = 2.0 * meta_ref[0:1, :]
+    dead = meta_ref[3:4, :] < 0.0
+    key = jnp.where(dead, col + float(lon), col) * float(slots) + full((1, slots), 1)
+    key_ref[0:1, :] = key
+    top = jnp.floor(key / 65536.0)
+    low = key - top * 65536.0
+    mid = jnp.floor(low / 256.0)
+    parts = jnp.concatenate([top, mid, low - mid * 256.0, jnp.zeros((13, slots), jnp.float32)], axis=0).astype(jnp.bfloat16)
+    r = full((16, 128), 0)
+    base = jnp.where(r == 0.0, 65536.0, jnp.where(r == 1.0, 256.0, jnp.where(r == 2.0, 1.0, 0.0))).astype(jnp.bfloat16)
+    kcol_ref[...] = dot(parts, base, ((0,), (0,)))
+
+    def rank(n, _):
+        at = pl.ds(pl.multiple_of(n * 128, 128), 128)
+        below = jnp.where(kcol_ref[...] < key_ref[0:1, at], 1.0, 0.0)
+        key_ref[1:2, at] = jnp.sum(below, axis=0, keepdims=True)
         return 0
 
-    lax.fori_loop(0, slots // chunk, body, 0)
-
-
-def scatter(q_ref, tab, v_of, first, last, lhs_ref, x_ref, members, coarse_rows):
-    cols = x_ref.shape[1]
+    lax.fori_loop(0, slots // 128, rank, 0)
+
+    srt_ref[...] = jnp.zeros_like(srt_ref)
+    high = jnp.floor(col / 256.0)
+    rows = [high.astype(jnp.bfloat16), (col - high * 256.0).astype(jnp.bfloat16), meta_ref[1:2, :].astype(jnp.bfloat16)]
+    rows += pieces(meta_ref[2:3, :]) + pieces(meta_ref[3:4, :])
+    rows.append(jnp.zeros((16 - len(rows), slots), jnp.bfloat16))
+    rows = jnp.concatenate([a.astype(jnp.float32) for a in rows], axis=0).astype(jnp.bfloat16)
+
+    def permute(n, _):
+        at = pl.ds(pl.multiple_of(n * BLK, BLK), BLK)
+        place = key_ref[1:2, :] - (n * BLK).astype(jnp.float32)
+        one = jnp.where(full((BLK, slots), 0) == place, 1.0, 0.0).astype(jnp.bfloat16)
+        got = dot(rows, one, ((1,), (1,)))
+        srt_ref[members : members + 1, at] = 128.0 * got[0:1] + 0.5 * got[1:2]
+        srt_ref[members + 1 : members + 2, at] = got[2:3]
+        srt_ref[members + 2 : members + 3, at] = got[3:4] + got[4:5] + got[5:6]
+        srt_ref[members + 3 : members + 4, at] = got[6:7] + got[7:8] + got[8:9]
+        return 0
+
+    lax.fori_loop(0, slots // BLK, permute, 0)
+
+    lane = full((1, 128), 1)
+    bounds = jnp.zeros((1, 128), jnp.float32)
+    blocks = lon // (2 * BLK)
+    for c in range(blocks + 1):
+        first = jnp.where(jnp.logical_and(jnp.logical_not(dead), col <= 2.0 * BLK * c - 2.0), 1.0, 0.0)
+        last = jnp.where(jnp.logical_and(jnp.logical_not(dead), col < 2.0 * BLK * (c + 1)), 1.0, 0.0)
+        bounds = jnp.where(lane == float(c), jnp.sum(first, axis=1, keepdims=True), bounds)
+        bounds = jnp.where(lane == float(64 + c), jnp.sum(last, axis=1, keepdims=True), bounds)
+    srt_ref[members + 4 : members + 5, 0:128] = bounds
+
+    def pick(c, _):
+        edge = (c * BLK).astype(jnp.float32)
+        live = jnp.logical_not(dead)
+        s = count(jnp.logical_and(live, col < edge))
+        e = count(jnp.logical_and(live, col < edge + BLK))
+        start = s // 128 * 128
+        trips = jnp.where(e > s, (e - start + 511) // 512, 0)
+
+        def window(i, _):
+            at = pl.ds(pl.multiple_of(start + i * 512, 128), 512)
+            cols = 2.0 * srt_ref[members : members + 1, at] - edge
+            one = jnp.where(full((BLK, 512), 0) == cols, 1.0, 0.0).astype(jnp.bfloat16)
+            field = p_ref[:, pl.ds(pl.multiple_of(c * BLK, BLK), BLK)]
+            got = dot(field, one).reshape(members, fine_rows, 512)
+            mask = jnp.where(full((fine_rows, 512), 0) == srt_ref[members + 1 : members + 2, at], 1.0, 0.0)
+            srt_ref[0:members, at] = srt_ref[0:members, at] + jnp.sum(got * mask[None], axis=1)
+            return 0
+
+        return lax.fori_loop(0, trips, window, 0)
+
+    lax.fori_loop(0, lon // BLK, pick, 0)
+    out_ref[...] = srt_ref[:, :slots]
+
+
+def windows(bound_ref, d, c):
+    s, e = bound_ref[d, c], bound_ref[d, 64 + c]
+    start = s // 128 * 128
+    return start, jnp.where(e > s, (e - start + WINDOW - 1) // WINDOW, 0)
+
+
+def scatter(bound_ref, q_ref, tab, v_of, first, last, lhs_ref, at_ref, x_ref, members, coarse_rows):
     slots = q_ref.shape[2]
     half = members * coarse_rows
+    blocks = x_ref.shape[1] // BLK - 1
     x_ref[...] = jnp.zeros_like(x_ref)
+    lhs_ref[:, slots:] = jnp.zeros((2 * half, WINDOW), jnp.bfloat16)
+    at_ref[...] = jnp.zeros_like(at_ref)
 
     def band(d, _):
-        at_col = q_ref[d, members : members + 1, :]
         row = jnp.floor(q_ref[d, members + 1 : members + 2, :] * 0.5)
         v = v_of(d)
+        at_ref[0:1, :slots] = q_ref[d, members : members + 1, :]
         weights = jnp.zeros((coarse_rows, slots), jnp.float32)
         taps = tab(d)
         for r in range(coarse_rows):
@@ -109,20 +189,33 @@
         weights = weights * v
         for k in range(members):
             hi, lo = split(weights * q_ref[d, k : k + 1, :])
-            lhs_ref[k * coarse_rows : (k + 1) * coarse_rows, :] = hi
-            lhs_ref[half + k * coarse_rows : half + (k + 1) * coarse_rows, :] = lo
-
-        def block(c, _):
-            base = (c * BLK).astype(jnp.float32)
-            near = jnp.where(jnp.logical_and(c == 0, at_col > cols - 1.0), at_col - float(cols), at_col)
-            got = dot(lhs_ref[...], hat_of(near - base, BLK), ((1,), (1,)))
-            at = pl.ds(pl.multiple_of(c * BLK, BLK), BLK)
-            x_ref[:, at] = x_ref[:, at] + (got[:half] + got[half:])
-            return 0
-
-        return lax.fori_loop(0, cols // BLK, block, 0)
+            lhs_ref[k * coarse_rows : (k + 1) * coarse_rows, :slots] = hi
+            lhs_ref[half + k * coarse_rows : half + (k + 1) * coarse_rows, :slots] = lo
+
+        def one(c, start):
+            at = pl.ds(pl.multiple_of(start, 128), WINDOW)
+            hat = hat_of(at_ref[0:1, at] - c * float(BLK), BLK)
+            got = dot(lhs_ref[:, at], hat, ((1,), (1,)))
+            return got[:half] + got[half:]
+
+        for c in range(blocks):
+            to = slice(c * BLK, (c + 1) * BLK)
+            x_ref[:, to] = x_ref[:, to] + one(float(c), windows(bound_ref, d, c)[0])
+
+        def rest(c, _):
+            start, trips = windows(bound_ref, d, c)
+            to = pl.ds(pl.multiple_of(c * BLK, BLK), BLK)
+
+            def more(i, _):
+                x_ref[:, to] = x_ref[:, to] + one(c.astype(jnp.float32), start + i * WINDOW)
+                return 0
+
+            return lax.fori_loop(jnp.where(c < blocks, 1, 0), trips, more, 0)
+
+        return lax.fori_loop(0, blocks + 1, rest, 0)
 
     lax.fori_loop(first, last, band, 0)
+    x_ref[:, :EDGE] = x_ref[:, :EDGE] + x_ref[:, blocks * BLK : blocks * BLK + EDGE]
 
 
 def lon_filter(x, t_ref):
@@ -158,17 +251,17 @@
             rows_ref[d : d + 1, i * 128 : (i + 1) * 128] = tile[i : i + 1, :]
 
 
-def iter_kernel(place_ref, q_ref, tab_ref, t2_ref, *refs, members, coarse_rows, scale2, order, bands, groups):
+def iter_kernel(place_ref, bound_ref, q_ref, tab_ref, t2_ref, *refs, members, coarse_rows, scale2, order, bands, groups):
     slots = q_ref.shape[2]
     tiles = slots // 128
     share = tiles // groups
     band = place_ref[1]
     if order == 0:
-        part_ref, b_ref, lhs_ref, x_ref, bhl_ref, rows_ref = refs
+        part_ref, b_ref, lhs_ref, at_ref, x_ref, rows_ref, bhl_ref, own_ref = refs
         for d in range(NREL):
-            rows_ref[d : d + 1, :] = pull_of(q_ref[d, members + 2 : members + 3, :], q_ref[d, members + 3 : members + 4, :])[0]
+            rows_ref[d : d + 1, :slots] = pull_of(q_ref[d, members + 2 : members + 3, :], q_ref[d, members + 3 : members + 4, :])[0]
     else:
-        old_ref, hits_ref, part_ref, b_ref, state_ref, step_ref, lhs_ref, x_ref, bhl_ref, rows_ref = refs
+        old_ref, hits_ref, part_ref, b_ref, state_ref, step_ref, lhs_ref, at_ref, x_ref, rows_ref, bhl_ref, own_ref = refs
         hits = sum_mem(hits_ref[:, :tiles, :], bands)
         if order == 1:
             for g in range(groups):
@@ -194,39 +287,50 @@
         lay_rows(rows_ref, lambda b: state_ref[2, b], (band, bands))
 
     def v_of(d):
-        return rows_ref[pl.ds(d, 1), :]
-
-    cols = x_ref.shape[1]
+        return rows_ref[pl.ds(d, 1), :slots]
+
     half = members * coarse_rows
-    scatter(q_ref, lambda d: tab_ref[band, 0, d], v_of, 0, NREL, lhs_ref, x_ref, members, coarse_rows)
-    b = lon_filter(x_ref[...], t2_ref)
+    blocks = x_ref.shape[1] // BLK - 1
+    cols = blocks * BLK
+    scatter(bound_ref, q_ref, lambda d: tab_ref[band, 0, d], v_of, 0, NREL, lhs_ref, at_ref, x_ref, members, coarse_rows)
+    b = lon_filter(x_ref[:, :cols], t2_ref)
     b_ref[...] = b
     hi, lo = split(b)
-    bhl_ref[:half] = hi
-    bhl_ref[half:] = lo
-    chunk = 512
-    per = chunk // 128
-
-    def gather(n, _):
-        at = pl.ds(pl.multiple_of(n * chunk, chunk), chunk)
-        at_col = q_ref[REACH, members : members + 1, at]
-        row = jnp.floor(q_ref[REACH, members + 1 : members + 2, at] * 0.5)
-        hats = [hat_of(jnp.where(at_col > cols - 1.0, at_col - float(cols), at_col), BLK)]
-        hats += [hat_of(at_col - float(c * BLK), BLK) for c in range(1, cols // BLK)]
-        hat = jnp.concatenate(hats, axis=0)
-        got = dot(bhl_ref[...], hat)
-        mask = jnp.where(full((coarse_rows, chunk), 0) == row, scale2, 0.0)
-        total = jnp.zeros((coarse_rows, chunk), jnp.float32)
+    bhl_ref[:half, :cols] = hi
+    bhl_ref[half:, :cols] = lo
+    bhl_ref[:, cols:] = bhl_ref[:, :BLK]
+    own_ref[:, :slots] = q_ref[REACH]
+    own_ref[:, slots:] = jnp.zeros((members + META, WINDOW), jnp.float32)
+    rows_ref[...] = jnp.zeros_like(rows_ref)
+
+    def gather(c, start):
+        at = pl.ds(pl.multiple_of(start, 128), WINDOW)
+        row = jnp.floor(own_ref[members + 1 : members + 2, at] * 0.5)
+        hat = hat_of(own_ref[members : members + 1, at] - jnp.float32(c) * float(BLK), BLK)
+        got = dot(bhl_ref[:, pl.ds(pl.multiple_of(c * BLK, BLK), BLK)], hat)
+        mask = jnp.where(full((coarse_rows, WINDOW), 0) == row, scale2, 0.0)
+        total = jnp.zeros((coarse_rows, WINDOW), jnp.float32)
         for k in range(members):
             r = slice(k * coarse_rows, (k + 1) * coarse_rows)
             r2 = slice(half + k * coarse_rows, half + (k + 1) * coarse_rows)
-            total = total + q_ref[REACH, k : k + 1, at] * (got[r] + got[r2])
-        part = jnp.sum(total * mask, axis=0, keepdims=True)
-        for i in range(per):
-            part_ref[0, pl.ds(n * per + i, 1), :] = part[:, i * 128 : (i + 1) * 128]
-        return 0
-
-    lax.fori_loop(0, slots // chunk, gather, 0)
+            total = total + own_ref[k : k + 1, at] * (got[r] + got[r2])
+        rows_ref[0:1, at] = rows_ref[0:1, at] + jnp.sum(total * mask, axis=0, keepdims=True)
+
+    for c in range(blocks):
+        gather(c, windows(bound_ref, REACH, c)[0])
+
+    def rest(c, _):
+        start, trips = windows(bound_ref, REACH, c)
+
+        def more(i, _):
+            gather(c, start + i * WINDOW)
+            return 0
+
+        return lax.fori_loop(jnp.where(c < blocks, 1, 0), trips, more, 0)
+
+    lax.fori_loop(0, blocks + 1, rest, 0)
+    for i in range(tiles):
+        part_ref[0, i : i + 1, :] = rows_ref[0:1, i * 128 : (i + 1) * 128]
     if order == 0:
         for r in range(2):
             mine = pl.ds(pl.multiple_of(place_ref[0] * (share * 128), 128), share * 128)
@@ -238,10 +342,11 @@
 
 
 def final_kernel(
-    place_ref, state_ref, hits_ref, q_ref, tab_ref, t1_ref, b0_ref, b1_ref, b2_ref, s0_ref, s1_ref, p_ref,
-    control_ref, image_ref, lam_ref, lhs_ref, x_ref, rows_ref, *, members, fine_rows, coarse_rows, scale,
+    place_ref, bound_ref, state_ref, hits_ref, q_ref, tab_ref, t1_ref, b0_ref, b1_ref, b2_ref, s0_ref, s1_ref, p_ref,
+    control_ref, image_ref, lam_ref, lhs_ref, at_ref, x_ref, rows_ref, *, members, fine_rows, coarse_rows, scale,
 ):
     bands = state_ref.shape[1]
+    slots = q_ref.shape[2]
     hits = sum_mem(hits_ref[...], bands)
     v = state_ref[2]
     step = step_of(hits, v, state_ref[3])[0:1, 0:1]
@@ -249,10 +354,11 @@
     lay_rows(rows_ref, lambda b: lam_ref[b], (place_ref[1], bands))
 
     def v_of(d):
-        return rows_ref[pl.ds(d, 1), :]
-
-    scatter(q_ref, lambda d: tab_ref[place_ref[1], 1, d], v_of, REACH - 1, REACH + 2, lhs_ref, x_ref, members, coarse_rows)
-    control_ref[...] = scale * lon_filter(x_ref[...], t1_ref)
+        return rows_ref[pl.ds(d, 1), :slots]
+
+    tab = lambda d: tab_ref[place_ref[1], 1, d]
+    scatter(bound_ref, q_ref, tab, v_of, REACH - 1, REACH + 2, lhs_ref, at_ref, x_ref, members, coarse_rows)
+    control_ref[...] = scale * lon_filter(x_ref[:, : b0_ref.shape[1]], t1_ref)
 
     b = s0_ref[0:1, 0:1] * b0_ref[...] + s1_ref[0:1, 0:1] * b1_ref[...] + step * b2_ref[...]
     half, cols = b.shape
@@ -319,25 +425,36 @@
         ]
     )
     own = pl.pallas_call(
-        functools.partial(pick_kernel, members=members, fine_rows=fine_rows, chunk=256),
+        functools.partial(prepare_kernel, members=members, fine_rows=fine_rows),
         out_shape=f32((members + META, slots)),
         in_specs=[vmem, vmem],
         out_specs=vmem,
+        scratch_shapes=[
+            pltpu.VMEM((8, slots), jnp.float32),
+            pltpu.VMEM((slots, 128), jnp.float32),
+            pltpu.VMEM((members + META, slots + 512), jnp.float32),
+        ],
         cost_estimate=pl.CostEstimate(flops=4 * 10**9, bytes_accessed=2 * 10**6, transcendentals=0),
-        name="pick",
+        name="prepare",
     )(field, meta)
     near = []
     for d in range(-REACH, REACH + 1):
         near.append(lax.ppermute(own, "lat", [(s, s - d) for s in range(bands) if 0 <= s - d < bands]) if d else own)
     near = jnp.stack(near)
-
-    rows = pltpu.VMEM((8, slots), jnp.float32)
-    scratch = [pltpu.VMEM((2 * half, slots), jnp.bfloat16), pltpu.VMEM((half, coarse_cols), jnp.float32)]
+    bound = near[:, members + 4, :128].astype(jnp.int32)
+
+    padded = slots + WINDOW
+    scratch = [
+        pltpu.VMEM((2 * half, padded), jnp.bfloat16),
+        pltpu.VMEM((8, padded), jnp.float32),
+        pltpu.VMEM((half, coarse_cols + BLK), jnp.float32),
+        pltpu.VMEM((8, padded), jnp.float32),
+    ]
     tiles = slots // 128
     state, hits, images, steps = None, None, [], []
     for iteration in range(ITERS):
         order = min(iteration, 2)
-        ins = [place, near, tables, t2] + [[], [obs_cells, hits], [state, hits]][order]
+        ins = [place, bound, near, tables, t2] + [[], [obs_cells, hits], [state, hits]][order]
         block = (groups * bands, tiles + (0 if iteration else 2 * (tiles // groups)), 128)
         outs = [f32(block), f32((half, coarse_cols))] + ([f32((6, bands, tiles, 128)), f32((1, 128))] if iteration else [])
         got = pl.pallas_call(
@@ -345,9 +462,10 @@
                 iter_kernel, members=members, coarse_rows=coarse_rows, scale2=scale * scale, order=order, bands=bands, groups=groups
             ),
             out_shape=outs,
-            in_specs=[smem] + [vmem] * (len(ins) - 1),
+            in_specs=[smem] * 2 + [vmem] * (len(ins) - 2),
             out_specs=[vmem] * len(outs),
-            scratch_shapes=scratch + [pltpu.VMEM((2 * half, coarse_cols), jnp.bfloat16), rows],
+            scratch_shapes=scratch
+            + [pltpu.VMEM((2 * half, coarse_cols + BLK), jnp.bfloat16), pltpu.VMEM((members + META, padded), jnp.float32)],
             cost_estimate=pl.CostEstimate(flops=7 * 10**9, bytes_accessed=3 * 10**6, transcendentals=0),
             name="iterate",
         )(*ins)
@@ -359,12 +477,12 @@
     control, image = pl.pallas_call(
         functools.partial(final_kernel, members=members, fine_rows=fine_rows, coarse_rows=coarse_rows, scale=scale),
         out_shape=[f32((half, coarse_cols)), f32((fine_rows, lon_cells))],
-        in_specs=[smem] + [vmem] * 11,
+        in_specs=[smem] * 2 + [vmem] * 11,
         out_specs=[vmem] * 2,
-        scratch_shapes=[pltpu.VMEM((bands, tiles, 128), jnp.float32)] + scratch + [rows],
+        scratch_shapes=[pltpu.VMEM((bands, tiles, 128), jnp.float32)] + scratch,
         cost_estimate=pl.CostEstimate(flops=5 * 10**9, bytes_accessed=6 * 10**6, transcendentals=0),
         name="finish",
-    )(place, state, hits, near, tables, t1, *images, *steps, field)
+    )(place, bound, state, hits, near, tables, t1, *images, *steps, field)
     return control.reshape(members, coarse_rows, coarse_cols), scatter_mem(image)
 
 

time: 146 us -> 134 us (0.918)
  Pallas kernels: 67.5 us -> 55.8 us
    pallas_call x3, Pallas kernels: 50.2 us -> 31.7 us  [on_device(): pl.pallas_call(functools.partial(iter_kernel, members=members, coarse_row...]
    pallas_call x1, Pallas kernels: 5.54 us -> 15.6 us  [on_device(): pl.pallas_call(functools.partial(prepare_kernel, members=members, fine_ro...]
    pallas_call x1, Pallas kernels: 11.7 us -> 8.63 us  [on_device(): pl.pallas_call(functools.partial(final_kernel, members=members, fine_rows...]
where the time goes in v4:
time: 134 us
  Pallas kernels  55.8 us (42%)
  blocking collectives  30.8 us (23%)
  waiting for transfers between devices  25.3 us (19%)
  starting transfers between devices  14.4 us (11%)
  local copies, waits for them, and re-layouts  3.1 us (2%)
  other arithmetic  2.94 us (2%)
  between operations  1.46 us (1%)
    pallas_call x3, Pallas kernels, on_device(): pl.pallas_call(functools.partial(iter_kernel, members=members, coarse_row...  31.7 us
    all_to_all x2, blocking collectives, on_device(): hits = lax.all_to_all(got[0], ('mem', 'lat'), 0, 0, tiled=True)  30.8 us
    pallas_call x1, Pallas kernels, on_device(): pl.pallas_call(functools.partial(prepare_kernel, members=members, fine_ro...  15.6 us
    ppermute x4, starting transfers between devices, on_device(): lax.ppermute(own, 'lat', [(s, s - d) for s in range(bands) if 0 <= s - d...  11 us
    all_to_all x1, waiting for transfers between devices, on_device(): hits = lax.all_to_all(got[0], ('mem', 'lat'), 0, 0, tiled=True)  10.3 us
    ppermute x4, waiting for transfers between devices, on_device(): lax.ppermute(own, 'lat', [(s, s - d) for s in range(bands) if 0 <= s - d...  10.1 us
    pallas_call x1, Pallas kernels, on_device(): pl.pallas_call(functools.partial(final_kernel, members=members, fine_rows...  8.63 us
    ppermute x2, waiting for transfers between devices, swap(): return lax.ppermute(a, axis, [(i, i ^ bit) for i in range(count)])  4.91 us
  transfers between devices with their start and end apart: 7, of which 6 were waited for; matrix products, arithmetic and copies ran while one was open for 0% of the time, Pallas kernels for 0%

profile of v4, /device:TPU:0, one launch (start us, length us, event | category | flops | bytes accessed | tf_op | source)
XLA Modules:
  0.0 133.8 jit_solution(9210029803091273292)
XLA Ops:
  0.6 0.7 fusion.2
  2.1 0.0 copy-start.4
  2.1 0.7 copy-done.4
  2.8 0.7 concatenate.3.meta_ref
  3.5 15.6 %prepare.1 = f32[24,2048]{1,0:T(8,128)} custom-call(bf16[256,2048]{1,0:T(8,128)(2,1)} %bitcast.23, f32[8,2048]{1,0:T(8,128)} %concatenate.3.meta_ref), custom_call_target="tpu_custom_call" | custom-call | flops 4000000000 | bytes 2000000 | tf_op jit(solution)/shard_map/prepare/pallas_call | solution.py:427
  19.0 5.0 %collective-permute-start = (f32[24,2048]{1,0:T(8,128)}, f32[24,2048]{1,0:T(8,128)S(1)}, u32[]{:S(2)}, u32[]{:S(2)}) collective-permute-start(f32[24,2048]{1,0:T(8,128)} %prepare.1), channel_id=1, source_target_pairs={{0,2},{1,3},{2,4},{3,5},{4,6},{5,7},{8,10},{9,11},{10,12},{11,13},... | collective-permute-start | bytes 589832 | tf_op jit(solution)/shard_map/ppermute | solution.py:442
  24.0 3.4 %collective-permute-start.1 = (f32[24,2048]{1,0:T(8,128)}, f32[24,2048]{1,0:T(8,128)S(1)}, u32[]{:S(2)}, u32[]{:S(2)}) collective-permute-start(f32[24,2048]{1,0:T(8,128)} %prepare.1), channel_id=1, source_target_pairs={{0,1},{1,2},{2,3},{3,4},{4,5},{5,6},{6,7},{8,9},{9,10},{10,11},{11... | collective-permute-start | bytes 589832 | tf_op jit(solution)/shard_map/ppermute | solution.py:442
  27.4 1.3 collective-permute-start.2
  28.7 1.3 collective-permute-start.3
  30.0 0.6 pad_add_fusion.place_ref
  30.6 0.0 collective-permute-done
  30.7 0.0 copy-start.2
  30.7 1.0 collective-permute-done.1
  31.7 3.9 %collective-permute-done.2 = f32[24,2048]{1,0:T(8,128)S(1)} collective-permute-done((f32[24,2048]{1,0:T(8,128)}, f32[24,2048]{1,0:T(8,128)S(1)}, u32[]{:S(2)}, u32[]{:S(2)}) %collective-permute-start.2) | collective-permute-done | bytes 196640 | tf_op jit(solution)/shard_map/ppermute | solution.py:442
  35.6 5.2 %collective-permute-done.3 = f32[24,2048]{1,0:T(8,128)S(1)} collective-permute-done((f32[24,2048]{1,0:T(8,128)}, f32[24,2048]{1,0:T(8,128)S(1)}, u32[]{:S(2)}, u32[]{:S(2)}) %collective-permute-start.3) | collective-permute-done | bytes 196640 | tf_op jit(solution)/shard_map/ppermute | solution.py:442
  40.9 0.6 copy.12
  41.5 0.3 copy-done.3
  41.8 10.3 %iterate.3 = (f32[32,24,128]{2,1,0:T(8,128)}, f32[128,1024]{1,0:T(8,128)}) custom-call(s32[2]{0:T(128)} %pad_add_fusion.place_ref, s32[5,128]{1,0:T(8,128)} %bitcast.19, f32[5,24,2048]{2,1,0:T(8,128)} %copy-done.3, f32[8,2,5,8,128]{4,3,2,1,0:T(8,128)} %constant.52.clone.tab_ref, bf16[2,512,256]{2,1,0:T(8,128)(2,1)} %constant.63.t2_ref), custom_call_target="tpu_custom_call" | custom-call | flops 7000000000 | bytes 3000000 | tf_op jit(solution)/shard_map/iterate/pallas_call | solution.py:460
  52.1 17.1 %all_to_all.15.refs_1_ = f32[32,24,128]{2,1,0:T(8,128)} all-to-all(f32[32,24,128]{2,1,0:T(8,128)} %get-tuple-element.14), channel_id=1, replica_groups=mesh['mem'=4,'lat'=8] {'mem','lat'}, dimensions={0} | all-to-all | bytes 786432 | tf_op jit(solution)/shard_map/all_to_all | solution.py:476
  69.1 10.7 %iterate.4 = (f32[32,16,128]{2,1,0:T(8,128)}, f32[128,1024]{1,0:T(8,128)}, f32[6,8,16,128]{3,2,1,0:T(8,128)}, f32[1,128]{1,0:T(1,128)}) custom-call(s32[2]{0:T(128)} %pad_add_fusion.place_ref, s32[5,128]{1,0:T(8,128)} %bitcast.20, f32[5,24,2048]{2,1,0:T(8,128)} %copy-done.3, f32[8,2,5,8,128]{4,3,2,1,0:T(8,128)} %constant.52.clone.tab_ref, ...), custom_call_target="tpu_custom_call" | custom-call | flops 7000000000 | bytes 3000000 | tf_op jit(solution)/shard_map/iterate/pallas_call | solution.py:460
  79.8 13.7 %all_to_all.16.refs_1_ = f32[32,16,128]{2,1,0:T(8,128)} all-to-all(f32[32,16,128]{2,1,0:T(8,128)} %get-tuple-element.16), channel_id=1, replica_groups=mesh['mem'=4,'lat'=8] {'mem','lat'}, dimensions={0} | all-to-all | bytes 524288 | tf_op jit(solution)/shard_map/all_to_all | solution.py:476
  93.5 10.7 %iterate.5 = (f32[32,16,128]{2,1,0:T(8,128)}, f32[128,1024]{1,0:T(8,128)}, f32[6,8,16,128]{3,2,1,0:T(8,128)}, f32[1,128]{1,0:T(1,128)}) custom-call(s32[2]{0:T(128)} %pad_add_fusion.place_ref, s32[5,128]{1,0:T(8,128)} %bitcast.21, f32[5,24,2048]{2,1,0:T(8,128)} %copy-done.3, f32[8,2,5,8,128]{4,3,2,1,0:T(8,128)} %constant.52.clone.tab_ref, ...), custom_call_target="tpu_custom_call" | custom-call | flops 7000000000 | bytes 3000000 | tf_op jit(solution)/shard_map/iterate/pallas_call | solution.py:460
  104.2 2.8 %all-to-all-start.2 = ((f32[32,16,128]{2,1,0:T(8,128)}), f32[32,16,128]{2,1,0:T(8,128)S(1)}, u32[]{:S(2)}, u32[]{:S(2)}) async-start(f32[32,16,128]{2,1,0:T(8,128)} %get-tuple-element.18), calls=%async_computation.2 | async-start | bytes 524288 | tf_op jit(solution)/shard_map/all_to_all | solution.py:476
  107.0 10.3 %all-to-all-done.2.hits_ref = f32[32,16,128]{2,1,0:T(8,128)S(1)} async-done(((f32[32,16,128]{2,1,0:T(8,128)}), f32[32,16,128]{2,1,0:T(8,128)S(1)}, u32[]{:S(2)}, u32[]{:S(2)}) %all-to-all-start.2) | async-done | bytes 262176 | tf_op jit(solution)/shard_map/all_to_all | solution.py:476
  117.3 0.7 copy-done.1
  118.0 8.6 %finish.1 = (f32[128,1024]{1,0:T(8,128)}, f32[16,2048]{1,0:T(8,128)}) custom-call(s32[2]{0:T(128)} %pad_add_fusion.place_ref, s32[5,128]{1,0:T(8,128)} %bitcast.22, f32[6,8,16,128]{3,2,1,0:T(8,128)} %get-tuple-element.17.state_ref, f32[32,16,128]{2,1,0:T(8,128)} %copy-done.1, f32[5,24,2048]{2,1,0:T(8,128)} %copy-done.3, ...), custom_call_target="tpu_custom_call" | custom-call | flops 5000000000 | bytes 6000000 | tf_op jit(solution)/shard_map/finish/pallas_call | solution.py:477
  126.6 0.9 slice_select_fusion
  127.5 0.6 collective-permute-start.4
  128.1 3.7 %collective-permute-done.4 = f32[16,1024]{1,0:T(8,128)S(1)} collective-permute-done((f32[16,1024]{1,0:T(8,128)S(1)}, f32[16,1024]{1,0:T(8,128)S(1)}, u32[]{:S(2)}, u32[]{:S(2)}) %collective-permute-start.4) | collective-permute-done | bytes 65568 | tf_op jit(solution)/shard_map/ppermute | solution.py:384
  131.9 0.1 collective-permute-start.5
  132.0 1.2 collective-permute-done.5
  133.2 0.6 select_add_fusion.1
  (17 shorter events, 0.2 us)
Async XLA Ops:
  0.6 1.4 %copy-start.5 = (f32[1,2048]{1,0:T(1,128)S(1)}, f32[1,2048]{1,0:T(1,128)}, u32[]{:S(2)}) copy-start(f32[1,2048]{1,0:T(1,128)} %param.12) | copy-start | bytes 24580
  2.1 0.7 copy-start.4
  19.0 11.6 %collective-permute-start = (f32[24,2048]{1,0:T(8,128)}, f32[24,2048]{1,0:T(8,128)S(1)}, u32[]{:S(2)}, u32[]{:S(2)}) collective-permute-start(f32[24,2048]{1,0:T(8,128)} %prepare.1), channel_id=1, source_target_pairs={{0,2},{1,3},{2,4},{3,5},{4,6},{5,7},{8,10},{9,11},{10,12},{11,13},... | collective-permute-start | bytes 589832 | tf_op jit(solution)/shard_map/ppermute | solution.py:442
  24.0 7.7 %collective-permute-start.1 = (f32[24,2048]{1,0:T(8,128)}, f32[24,2048]{1,0:T(8,128)S(1)}, u32[]{:S(2)}, u32[]{:S(2)}) collective-permute-start(f32[24,2048]{1,0:T(8,128)} %prepare.1), channel_id=1, source_target_pairs={{0,1},{1,2},{2,3},{3,4},{4,5},{5,6},{6,7},{8,9},{9,10},{10,11},{11... | collective-permute-start | bytes 589832 | tf_op jit(solution)/shard_map/ppermute | solution.py:442
  27.4 8.2 %collective-permute-start.2 = (f32[24,2048]{1,0:T(8,128)}, f32[24,2048]{1,0:T(8,128)S(1)}, u32[]{:S(2)}, u32[]{:S(2)}) collective-permute-start(f32[24,2048]{1,0:T(8,128)} %prepare.1), channel_id=1, source_target_pairs={{1,0},{2,1},{3,2},{4,3},{5,4},{6,5},{7,6},{9,8},{10,9},{11,10},{12... | collective-permute-start | bytes 589832 | tf_op jit(solution)/shard_map/ppermute | solution.py:442
  28.7 12.1 %collective-permute-start.3 = (f32[24,2048]{1,0:T(8,128)}, f32[24,2048]{1,0:T(8,128)S(1)}, u32[]{:S(2)}, u32[]{:S(2)}) collective-permute-start(f32[24,2048]{1,0:T(8,128)} %prepare.1), channel_id=1, source_target_pairs={{2,0},{3,1},{4,2},{5,3},{6,4},{7,5},{10,8},{11,9},{12,10},{13,11},... | collective-permute-start | bytes 589832 | tf_op jit(solution)/shard_map/ppermute | solution.py:442
  30.7 1.0 copy-start.2
  40.8 1.0 copy-start.3
  104.2 13.0 %all-to-all-start.2 = ((f32[32,16,128]{2,1,0:T(8,128)}), f32[32,16,128]{2,1,0:T(8,128)S(1)}, u32[]{:S(2)}, u32[]{:S(2)}) async-start(f32[32,16,128]{2,1,0:T(8,128)} %get-tuple-element.18), calls=%async_computation.2 | async-start | bytes 524288 | tf_op jit(solution)/shard_map/all_to_all | solution.py:476
  117.3 0.7 copy-start.1
  126.6 5.3 %copy-start = (f32[16,2048]{1,0:T(8,128)S(1)}, f32[16,2048]{1,0:T(8,128)}, u32[]{:S(2)}) copy-start(f32[16,2048]{1,0:T(8,128)} %get-tuple-element.25) | copy-start | bytes 393220
  127.5 4.3 %collective-permute-start.4 = (f32[16,1024]{1,0:T(8,128)S(1)}, f32[16,1024]{1,0:T(8,128)S(1)}, u32[]{:S(2)}, u32[]{:S(2)}) collective-permute-start(f32[16,1024]{1,0:T(8,128)S(1)} %slice_select_fusion), channel_id=1, source_target_pairs={{0,16},{8,24},{16,0},{24,8},{1,17},{9,25},{17,1},{25,9},{2,18},{10... | collective-permute-start | bytes 196616 | tf_op jit(solution)/shard_map/ppermute | solution.py:384
  131.9 1.3 collective-permute-start.5

commit v5 on v4

--- a/solution.py
+++ b/solution.py
@@ -87,11 +87,14 @@
     return jnp.sum(jnp.where(mask, 1.0, 0.0)).astype(jnp.int32)
 
 
-def prepare_kernel(p_ref, meta_ref, out_ref, key_ref, kcol_ref, srt_ref, *, members, fine_rows):
+def prepare_kernel(count_ref, p_ref, cell_ref, innovation_ref, scale_ref, out_ref, key_ref, kcol_ref, srt_ref, *, members, fine_rows):
     lon = p_ref.shape[1]
-    slots = meta_ref.shape[1]
-    col = 2.0 * meta_ref[0:1, :]
-    dead = meta_ref[3:4, :] < 0.0
+    slots = cell_ref.shape[1]
+    cell = cell_ref[...].astype(jnp.float32)
+    row = jnp.floor((cell + 0.5) / float(lon))
+    col = cell - row * float(lon)
+    dead = full((1, slots), 1) >= count_ref[0].astype(jnp.float32)
+    signed = jnp.where(dead, -scale_ref[...], scale_ref[...])
     key = jnp.where(dead, col + float(lon), col) * float(slots) + full((1, slots), 1)
     key_ref[0:1, :] = key
     top = jnp.floor(key / 65536.0)
@@ -105,6 +108,7 @@
     def rank(n, _):
         at = pl.ds(pl.multiple_of(n * 128, 128), 128)
         below = jnp.where(kcol_ref[...] < key_ref[0:1, at], 1.0, 0.0)
+        below = jnp.sum(below.reshape(slots // 64, 64, 128), axis=0)
         key_ref[1:2, at] = jnp.sum(below, axis=0, keepdims=True)
         return 0
 
@@ -112,8 +116,8 @@
 
     srt_ref[...] = jnp.zeros_like(srt_ref)
     high = jnp.floor(col / 256.0)
-    rows = [high.astype(jnp.bfloat16), (col - high * 256.0).astype(jnp.bfloat16), meta_ref[1:2, :].astype(jnp.bfloat16)]
-    rows += pieces(meta_ref[2:3, :]) + pieces(meta_ref[3:4, :])
+    rows = [high.astype(jnp.bfloat16), (col - high * 256.0).astype(jnp.bfloat16), row.astype(jnp.bfloat16)]
+    rows += pieces(innovation_ref[...]) + pieces(signed)
     rows.append(jnp.zeros((16 - len(rows), slots), jnp.bfloat16))
     rows = jnp.concatenate([a.astype(jnp.float32) for a in rows], axis=0).astype(jnp.bfloat16)
 
@@ -140,27 +144,27 @@
         bounds = jnp.where(lane == float(64 + c), jnp.sum(last, axis=1, keepdims=True), bounds)
     srt_ref[members + 4 : members + 5, 0:128] = bounds
 
-    def pick(c, _):
-        edge = (c * BLK).astype(jnp.float32)
-        live = jnp.logical_not(dead)
-        s = count(jnp.logical_and(live, col < edge))
-        e = count(jnp.logical_and(live, col < edge + BLK))
-        start = s // 128 * 128
-        trips = jnp.where(e > s, (e - start + 511) // 512, 0)
-
-        def window(i, _):
-            at = pl.ds(pl.multiple_of(start + i * 512, 128), 512)
-            cols = 2.0 * srt_ref[members : members + 1, at] - edge
-            one = jnp.where(full((BLK, 512), 0) == cols, 1.0, 0.0).astype(jnp.bfloat16)
-            field = p_ref[:, pl.ds(pl.multiple_of(c * BLK, BLK), BLK)]
-            got = dot(field, one).reshape(members, fine_rows, 512)
-            mask = jnp.where(full((fine_rows, 512), 0) == srt_ref[members + 1 : members + 2, at], 1.0, 0.0)
-            srt_ref[0:members, at] = srt_ref[0:members, at] + jnp.sum(got * mask[None], axis=1)
+    live = jnp.logical_not(dead)
+    edges = [count(jnp.logical_and(live, col < float(c * BLK))) for c in range(lon // BLK + 1)]
+
+    def window(c, start):
+        at = pl.ds(pl.multiple_of(start, 128), 512)
+        cols = 2.0 * srt_ref[members : members + 1, at] - float(c * BLK)
+        one = jnp.where(full((BLK, 512), 0) == cols, 1.0, 0.0).astype(jnp.bfloat16)
+        got = dot(p_ref[:, c * BLK : (c + 1) * BLK], one).reshape(members, fine_rows, 512)
+        mask = jnp.where(full((fine_rows, 512), 0) == srt_ref[members + 1 : members + 2, at], 1.0, 0.0)
+        srt_ref[0:members, at] = srt_ref[0:members, at] + jnp.sum(got * mask[None], axis=1)
+
+    starts = [s // 128 * 128 for s in edges[:-1]]
+    for c, start in enumerate(starts):
+        window(c, start)
+    for c, start in enumerate(starts):
+
+        def more(i, _, c=c, start=start):
+            window(c, start + i * 512)
             return 0
 
-        return lax.fori_loop(0, trips, window, 0)
-
-    lax.fori_loop(0, lon // BLK, pick, 0)
+        lax.fori_loop(1, (edges[c + 1] - start + 511) // 512, more, 0)
     out_ref[...] = srt_ref[:, :slots]
 
 
@@ -219,7 +223,7 @@
 
 
 def lon_filter(x, t_ref):
-    half, cols = x.shape
+    _, cols = x.shape
     ext = jnp.concatenate([x[:, cols - EDGE :], x, x[:, :EDGE]], axis=1)
     hi, lo = split(ext)
     parts = []
@@ -257,11 +261,11 @@
     share = tiles // groups
     band = place_ref[1]
     if order == 0:
-        part_ref, b_ref, lhs_ref, at_ref, x_ref, rows_ref, bhl_ref, own_ref = refs
+        part_ref, b_ref, vrow_ref, lhs_ref, at_ref, x_ref, rows_ref, bhl_ref, own_ref = refs
         for d in range(NREL):
-            rows_ref[d : d + 1, :slots] = pull_of(q_ref[d, members + 2 : members + 3, :], q_ref[d, members + 3 : members + 4, :])[0]
+            vrow_ref[d : d + 1, :] = pull_of(q_ref[d, members + 2 : members + 3, :], q_ref[d, members + 3 : members + 4, :])[0]
     else:
-        old_ref, hits_ref, part_ref, b_ref, state_ref, step_ref, lhs_ref, at_ref, x_ref, rows_ref, bhl_ref, own_ref = refs
+        old_ref, hits_ref, part_ref, b_ref, vrow_ref, state_ref, step_ref, lhs_ref, at_ref, x_ref, rows_ref, bhl_ref, own_ref = refs
         hits = sum_mem(hits_ref[:, :tiles, :], bands)
         if order == 1:
             for g in range(groups):
@@ -284,10 +288,10 @@
         state_ref[3] = weight
         state_ref[4] = observed
         state_ref[5] = lam
-        lay_rows(rows_ref, lambda b: state_ref[2, b], (band, bands))
+        lay_rows(vrow_ref, lambda b: state_ref[2, b], (band, bands))
 
     def v_of(d):
-        return rows_ref[pl.ds(d, 1), :slots]
+        return vrow_ref[pl.ds(d, 1), :]
 
     half = members * coarse_rows
     blocks = x_ref.shape[1] // BLK - 1
@@ -341,26 +345,18 @@
     part_ref[1:] = jnp.broadcast_to(part_ref[0][None], (part_ref.shape[0] - 1,) + part_ref.shape[1:])
 
 
-def final_kernel(
-    place_ref, bound_ref, state_ref, hits_ref, q_ref, tab_ref, t1_ref, b0_ref, b1_ref, b2_ref, s0_ref, s1_ref, p_ref,
-    control_ref, image_ref, lam_ref, lhs_ref, at_ref, x_ref, rows_ref, *, members, fine_rows, coarse_rows, scale,
+def side_kernel(
+    place_ref, bound_ref, vrow_ref, q_ref, tab_ref, t1_ref, b_ref, p_ref, control_ref, image_ref, lhs_ref, at_ref, x_ref,
+    *, members, fine_rows, coarse_rows, scale,
 ):
-    bands = state_ref.shape[1]
-    slots = q_ref.shape[2]
-    hits = sum_mem(hits_ref[...], bands)
-    v = state_ref[2]
-    step = step_of(hits, v, state_ref[3])[0:1, 0:1]
-    lam_ref[...] = state_ref[5] + step[None] * v
-    lay_rows(rows_ref, lambda b: lam_ref[b], (place_ref[1], bands))
-
     def v_of(d):
-        return rows_ref[pl.ds(d, 1), :slots]
+        return vrow_ref[pl.ds(d, 1), :]
 
     tab = lambda d: tab_ref[place_ref[1], 1, d]
     scatter(bound_ref, q_ref, tab, v_of, REACH - 1, REACH + 2, lhs_ref, at_ref, x_ref, members, coarse_rows)
-    control_ref[...] = scale * lon_filter(x_ref[:, : b0_ref.shape[1]], t1_ref)
-
-    b = s0_ref[0:1, 0:1] * b0_ref[...] + s1_ref[0:1, 0:1] * b1_ref[...] + step * b2_ref[...]
+    control_ref[...] = scale * lon_filter(x_ref[:, : b_ref.shape[1]], t1_ref)
+
+    b = b_ref[...]
     half, cols = b.shape
     wide = 2 * half
     repeat = jnp.where(
@@ -376,22 +372,32 @@
         fine = slice(2 * f * EDGE, 2 * (f + 1) * EDGE)
         field = dot(hi[:, at], hat) + dot(lo[:, at], hat)
         product = p_ref[:, fine].astype(jnp.float32) * field
-        image_ref[:, fine] = (scale * scale) * jnp.sum(product.reshape(members, fine_rows, 2 * EDGE), axis=0)
-
-
-def swap(a, axis, bit):
-    count = lax.axis_size(axis)
-    return lax.ppermute(a, axis, [(i, i ^ bit) for i in range(count)])
+        part = (scale * scale) * jnp.sum(product.reshape(members, fine_rows, 2 * EDGE), axis=0)
+        width = image_ref.shape[2]
+        for start in range(0, 2 * EDGE, min(width, 2 * EDGE)):
+            stop = start + min(width, 2 * EDGE)
+            group, to = divmod(2 * f * EDGE + start, width)
+            image_ref[group, :, to : to + stop - start] = part[:, start:stop]
+
+
+def combine_kernel(state_ref, hits_ref, *refs):
+    steps, controls, images = refs[: ITERS - 1], refs[ITERS - 1 : 2 * ITERS - 1], refs[2 * ITERS - 1 : 3 * ITERS - 1]
+    control_ref, image_ref = refs[3 * ITERS - 1 :]
+    last = step_of(sum_mem(hits_ref[...], state_ref.shape[1]), state_ref[2], state_ref[3])[0:1, 0:1]
+    steps = [s[0:1, 0:1] for s in steps] + [last]
+    control_ref[...] = sum(s * c[...] for s, c in zip(steps, controls))
+    image_ref[...] = sum(s * i[...] for s, i in zip(steps, images))
 
 
 def scatter_mem(a):
-    bit = lax.axis_size("mem") // 2
+    count = lax.axis_size("mem")
     me = lax.axis_index("mem")
+    bit = count // 2
     while bit:
-        width = a.shape[1] // 2
-        low, high = a[:, :width], a[:, width:]
+        low, high = a[: a.shape[0] // 2], a[a.shape[0] // 2 :]
         upper = (me & bit) != 0
-        a = jnp.where(upper, high, low) + swap(jnp.where(upper, low, high), "mem", bit)
+        away = lax.ppermute(jnp.where(upper, low, high), "mem", [(i, i ^ bit) for i in range(count)])
+        a = jnp.where(upper, high, low) + away
         bit //= 2
     return a
 
@@ -413,21 +419,11 @@
     vmem = pl.BlockSpec(memory_space=pltpu.VMEM)
     f32 = functools.partial(jax.ShapeDtypeStruct, dtype=jnp.float32)
 
-    live = jnp.arange(slots, dtype=jnp.int32)[None] < obs_count[0]
     field = perturbation.reshape(members * fine_rows, lon_cells)
-    meta = jnp.concatenate(
-        [
-            (obs_cells % lon_cells).astype(jnp.float32) * 0.5,
-            (obs_cells // lon_cells).astype(jnp.float32),
-            innovation,
-            jnp.where(live, obs_scale, -obs_scale),
-            jnp.zeros((META - 4, slots), jnp.float32),
-        ]
-    )
     own = pl.pallas_call(
         functools.partial(prepare_kernel, members=members, fine_rows=fine_rows),
         out_shape=f32((members + META, slots)),
-        in_specs=[vmem, vmem],
+        in_specs=[smem] + [vmem] * 4,
         out_specs=vmem,
         scratch_shapes=[
             pltpu.VMEM((8, slots), jnp.float32),
@@ -436,7 +432,7 @@
         ],
         cost_estimate=pl.CostEstimate(flops=4 * 10**9, bytes_accessed=2 * 10**6, transcendentals=0),
         name="prepare",
-    )(field, meta)
+    )(obs_count, field, obs_cells, innovation, obs_scale)
     near = []
     for d in range(-REACH, REACH + 1):
         near.append(lax.ppermute(own, "lat", [(s, s - d) for s in range(bands) if 0 <= s - d < bands]) if d else own)
@@ -448,15 +444,16 @@
         pltpu.VMEM((2 * half, padded), jnp.bfloat16),
         pltpu.VMEM((8, padded), jnp.float32),
         pltpu.VMEM((half, coarse_cols + BLK), jnp.float32),
-        pltpu.VMEM((8, padded), jnp.float32),
     ]
     tiles = slots // 128
-    state, hits, images, steps = None, None, [], []
+    width = lon_cells // groups
+    state, hits, steps, controls, images = None, None, [], [], []
     for iteration in range(ITERS):
         order = min(iteration, 2)
         ins = [place, bound, near, tables, t2] + [[], [obs_cells, hits], [state, hits]][order]
         block = (groups * bands, tiles + (0 if iteration else 2 * (tiles // groups)), 128)
-        outs = [f32(block), f32((half, coarse_cols))] + ([f32((6, bands, tiles, 128)), f32((1, 128))] if iteration else [])
+        outs = [f32(block), f32((half, coarse_cols)), f32((8, slots))]
+        outs += [f32((6, bands, tiles, 128)), f32((1, 128))] if iteration else []
         got = pl.pallas_call(
             functools.partial(
                 iter_kernel, members=members, coarse_rows=coarse_rows, scale2=scale * scale, order=order, bands=bands, groups=groups
@@ -465,25 +462,36 @@
             in_specs=[smem] * 2 + [vmem] * (len(ins) - 2),
             out_specs=[vmem] * len(outs),
             scratch_shapes=scratch
+            + [pltpu.VMEM((8, padded), jnp.float32)]
             + [pltpu.VMEM((2 * half, coarse_cols + BLK), jnp.bfloat16), pltpu.VMEM((members + META, padded), jnp.float32)],
             cost_estimate=pl.CostEstimate(flops=7 * 10**9, bytes_accessed=3 * 10**6, transcendentals=0),
             name="iterate",
         )(*ins)
-        images.append(got[1])
         if iteration:
-            state = got[2]
-            steps.append(got[3])
+            state = got[3]
+            steps.append(got[4])
         hits = lax.all_to_all(got[0], ("mem", "lat"), 0, 0, tiled=True)
+        side = pl.pallas_call(
+            functools.partial(side_kernel, members=members, fine_rows=fine_rows, coarse_rows=coarse_rows, scale=scale),
+            out_shape=[f32((half, coarse_cols)), f32((groups, fine_rows, width))],
+            in_specs=[smem] * 2 + [vmem] * 6,
+            out_specs=[vmem] * 2,
+            scratch_shapes=scratch,
+            cost_estimate=pl.CostEstimate(flops=4 * 10**9, bytes_accessed=6 * 10**6, transcendentals=0),
+            name="side",
+        )
+        control, image = side(place, bound, got[2], near, tables, t1, got[1], field)
+        controls.append(control)
+        images.append(scatter_mem(image)[0])
     control, image = pl.pallas_call(
-        functools.partial(final_kernel, members=members, fine_rows=fine_rows, coarse_rows=coarse_rows, scale=scale),
-        out_shape=[f32((half, coarse_cols)), f32((fine_rows, lon_cells))],
-        in_specs=[smem] * 2 + [vmem] * 11,
+        combine_kernel,
+        out_shape=[f32((half, coarse_cols)), f32((fine_rows, width))],
+        in_specs=[vmem] * (3 * ITERS + 1),
         out_specs=[vmem] * 2,
-        scratch_shapes=[pltpu.VMEM((bands, tiles, 128), jnp.float32)] + scratch,
-        cost_estimate=pl.CostEstimate(flops=5 * 10**9, bytes_accessed=6 * 10**6, transcendentals=0),
-        name="finish",
-    )(place, bound, state, hits, near, tables, t1, *images, *steps, field)
-    return control.reshape(members, coarse_rows, coarse_cols), scatter_mem(image)
+        cost_estimate=pl.CostEstimate(flops=10**7, bytes_accessed=4 * 10**6, transcendentals=0),
+        name="combine",
+    )(state, hits, *steps, *controls, *images)
+    return control.reshape(members, coarse_rows, coarse_cols), image
 
 
 def solution(mesh):

time: 134 us -> 134 us (level)
  blocking collectives: 30.8 us -> 0 us
  starting transfers between devices: 14.4 us -> 33 us
  Pallas kernels: 55.8 us -> 66.8 us
  other arithmetic: 2.94 us -> 5.28 us
  waiting for transfers between devices: 25.3 us -> 23.6 us
    all_to_all x2 -> x0, blocking collectives: 30.8 us -> none  [on_device(): hits = lax.all_to_all(got[0], ('mem', 'lat'), 0, 0, tiled=True)]
    pallas_call x1 -> x4, Pallas kernels: 8.63 us -> 25.7 us  [the longest x3 23.1 us: on_device(): control, image = side(place, bound, got[2], near, tables, t1, got[1], field)]
    all_to_all x1 -> x3, starting transfers between devices: 2.76 us -> 16.1 us  [on_device(): hits = lax.all_to_all(got[0], ('mem', 'lat'), 0, 0, tiled=True)]
    ppermute x2 -> x6, starting transfers between devices: 0.68 us -> 5.89 us  [scatter_mem(): lax.ppermute(jnp.where(upper, low, high), 'mem', [(i, i ^ bit) for i in r...]
    pallas_call x1, Pallas kernels: 15.6 us -> 11.2 us  [on_device(): pl.pallas_call(functools.partial(prepare_kernel, members=members, fine_ro...]
    squeeze x0 -> x3, other arithmetic: none -> 1.86 us  [on_device(): images.append(scatter_mem(image)[0])]
    select_n x2 -> x6, other arithmetic: 0.93 us -> 2.75 us  [scatter_mem(): jnp.where(upper, low, high)]
    pallas_call x3, Pallas kernels: 31.7 us -> 29.9 us  [on_device(): pl.pallas_call(functools.partial(iter_kernel, members=members, coarse_row...]
  transfers between devices with their start and end apart: 7 -> 13, of which waited for: 6 -> 7; matrix products, arithmetic and copies ran while one was open for 0% -> 3% of each run, Pallas kernels for 0% -> 19%
where the time goes in v5:
time: 134 us; the launch traced here: 133 us
  Pallas kernels  66.8 us (50%)
  starting transfers between devices  33 us (25%)
  waiting for transfers between devices  23.6 us (18%)
  other arithmetic  5.28 us (4%)
  local copies, waits for them, and re-layouts  3.22 us (2%)
  between operations  1.52 us (1%)
    pallas_call x3, Pallas kernels, on_device(): pl.pallas_call(functools.partial(iter_kernel, members=members, coarse_row...  29.9 us
    pallas_call x3, Pallas kernels, on_device(): control, image = side(place, bound, got[2], near, tables, t1, got[1], field)  23.1 us
    all_to_all x3, starting transfers between devices, on_device(): hits = lax.all_to_all(got[0], ('mem', 'lat'), 0, 0, tiled=True)  16.1 us
    pallas_call x1, Pallas kernels, on_device(): pl.pallas_call(functools.partial(prepare_kernel, members=members, fine_ro...  11.2 us
    ppermute x4, starting transfers between devices, on_device(): lax.ppermute(own, 'lat', [(s, s - d) for s in range(bands) if 0 <= s - d...  11 us
    ppermute x4, waiting for transfers between devices, on_device(): lax.ppermute(own, 'lat', [(s, s - d) for s in range(bands) if 0 <= s - d...  10.1 us
    all_to_all x3, waiting for transfers between devices, on_device(): hits = lax.all_to_all(got[0], ('mem', 'lat'), 0, 0, tiled=True)  8.5 us
    ppermute x6, starting transfers between devices, scatter_mem(): lax.ppermute(jnp.where(upper, low, high), 'mem', [(i, i ^ bit) for i in r...  5.89 us
  transfers between devices with their start and end apart: 13, of which 7 were waited for; matrix products, arithmetic and copies ran while one was open for 3% of the time, Pallas kernels for 19%

profile of v5, /device:TPU:0, one launch (start us, length us, event | category | flops | bytes accessed | tf_op | source)
XLA Modules:
  0.0 133.4 jit_solution(8570060862861927333)
XLA Ops:
  1.3 11.2 %prepare.1 = f32[24,2048]{1,0:T(8,128)} custom-call(s32[1]{0:T(128)S(6)} %copy.17.count_ref, bf16[256,2048]{1,0:T(8,128)(2,1)} %bitcast.29, s32[1,2048]{1,0:T(1,128)} %refs_0_.1, f32[1,2048]{1,0:T(1,128)} %innovation_ref.1, f32[1,2048]{1,0:T(1,128)} %scale_ref.1), custom_call_target="tpu_custom_call" | custom-call | flops 4000000000 | bytes 2000000 | tf_op jit(solution)/shard_map/prepare/pallas_call | solution.py:423
  12.5 5.0 %collective-permute-start = (f32[24,2048]{1,0:T(8,128)}, f32[24,2048]{1,0:T(8,128)S(1)}, u32[]{:S(2)}, u32[]{:S(2)}) collective-permute-start(f32[24,2048]{1,0:T(8,128)} %prepare.1), channel_id=1, source_target_pairs={{0,2},{1,3},{2,4},{3,5},{4,6},{5,7},{8,10},{9,11},{10,12},{11,13},... | collective-permute-start | bytes 589832 | tf_op jit(solution)/shard_map/ppermute | solution.py:438
  17.5 3.4 %collective-permute-start.1 = (f32[24,2048]{1,0:T(8,128)}, f32[24,2048]{1,0:T(8,128)S(1)}, u32[]{:S(2)}, u32[]{:S(2)}) collective-permute-start(f32[24,2048]{1,0:T(8,128)} %prepare.1), channel_id=1, source_target_pairs={{0,1},{1,2},{2,3},{3,4},{4,5},{5,6},{6,7},{8,9},{9,10},{10,11},{11... | collective-permute-start | bytes 589832 | tf_op jit(solution)/shard_map/ppermute | solution.py:438
  20.9 1.3 collective-permute-start.2
  22.2 1.3 collective-permute-start.3
  24.1 1.0 collective-permute-done.1
  25.2 3.9 %collective-permute-done.2 = f32[24,2048]{1,0:T(8,128)S(1)} collective-permute-done((f32[24,2048]{1,0:T(8,128)}, f32[24,2048]{1,0:T(8,128)S(1)}, u32[]{:S(2)}, u32[]{:S(2)}) %collective-permute-start.2) | collective-permute-done | bytes 196640 | tf_op jit(solution)/shard_map/ppermute | solution.py:438
  29.1 5.2 %collective-permute-done.3 = f32[24,2048]{1,0:T(8,128)S(1)} collective-permute-done((f32[24,2048]{1,0:T(8,128)}, f32[24,2048]{1,0:T(8,128)S(1)}, u32[]{:S(2)}, u32[]{:S(2)}) %collective-permute-start.3) | collective-permute-done | bytes 196640 | tf_op jit(solution)/shard_map/ppermute | solution.py:438
  34.3 0.7 copy.12
  35.3 9.7 %iterate.3 = (f32[32,24,128]{2,1,0:T(8,128)}, f32[128,1024]{1,0:T(8,128)}, f32[8,2048]{1,0:T(8,128)}) custom-call(s32[2]{0:T(128)} %pad_add_fusion.place_ref, s32[5,128]{1,0:T(8,128)} %bitcast.23, f32[5,24,2048]{2,1,0:T(8,128)} %copy-done.7, f32[8,2,5,8,128]{4,3,2,1,0:T(8,128)} %constant.22.clone.tab_ref, bf16[2,512,256]{2,1,0:T(8,128)(2,1)} %constant.33.t2_ref), custom_call_target="tpu_custom_call" | custom-call | flops 7000000000 | bytes 3000000 | tf_op jit(solution)/shard_map/iterate/pallas_call | solution.py:457
  45.0 3.6 %all-to-all-start = ((f32[32,24,128]{2,1,0:T(8,128)}), f32[32,24,128]{2,1,0:T(8,128)S(1)}, u32[]{:S(2)}, u32[]{:S(2)}) async-start(f32[32,24,128]{2,1,0:T(8,128)} %get-tuple-element.23), calls=%async_computation | async-start | bytes 786432 | tf_op jit(solution)/shard_map/all_to_all | solution.py:473
  48.6 7.7 %side.3 = (f32[128,1024]{1,0:T(8,128)}, f32[4,16,512]{2,1,0:T(8,128)}) custom-call(s32[2]{0:T(128)} %pad_add_fusion.place_ref, s32[5,128]{1,0:T(8,128)} %bitcast.24, f32[8,2048]{1,0:T(8,128)} %get-tuple-element.30.vrow_ref, f32[5,24,2048]{2,1,0:T(8,128)} %copy-done.7, f32[8,2,5,8,128]{4,3,2,1,0:T(8,128)} %constant.22.clone.tab_ref, ...), custom_call_target="tpu_custom_call" | custom-call | flops 4000000000 | bytes 6000000 | tf_op jit(solution)/shard_map/side/pallas_call | solution.py:483
  56.3 0.9 slice_select_fusion.2
  57.2 1.8 %collective-permute-start.4 = (f32[2,16,512]{2,1,0:T(8,128)S(1)}, f32[2,16,512]{2,1,0:T(8,128)S(1)}, u32[]{:S(2)}, u32[]{:S(2)}) collective-permute-start(f32[2,16,512]{2,1,0:T(8,128)S(1)} %slice_select_fusion.2), channel_id=1, source_target_pairs={{0,16},{8,24},{16,0},{24,8},{1,17},{9,25},{17,1},{25,9},{2,18},{10... | collective-permute-start | bytes 196616 | tf_op jit(solution)/shard_map/ppermute | solution.py:399
  59.1 2.9 %collective-permute-done.4 = f32[2,16,512]{2,1,0:T(8,128)S(1)} collective-permute-done((f32[2,16,512]{2,1,0:T(8,128)S(1)}, f32[2,16,512]{2,1,0:T(8,128)S(1)}, u32[]{:S(2)}, u32[]{:S(2)}) %collective-permute-start.4) | collective-permute-done | bytes 65568 | tf_op jit(solution)/shard_map/ppermute | solution.py:399
  62.1 0.8 copy-done.4
  62.8 10.1 %iterate.4 = (f32[32,16,128]{2,1,0:T(8,128)}, f32[128,1024]{1,0:T(8,128)}, f32[8,2048]{1,0:T(8,128)}, f32[6,8,16,128]{3,2,1,0:T(8,128)}, f32[1,128]{1,0:T(1,128)}) custom-call(s32[2]{0:T(128)} %pad_add_fusion.place_ref, s32[5,128]{1,0:T(8,128)} %bitcast.25, f32[5,24,2048]{2,1,0:T(8,128)} %copy-done.7, f32[8,2,5,8,128]{4,3,2,1,0:T(8,128)} %constant.22.clone.tab_ref, ...), custom_call_target="tpu_custom_call" | custom-call | flops 7000000000 | bytes 3000000 | tf_op jit(solution)/shard_map/iterate/pallas_call | solution.py:457
  72.9 6.5 %all-to-all-start.1 = ((f32[32,16,128]{2,1,0:T(8,128)}), f32[32,16,128]{2,1,0:T(8,128)S(1)}, u32[]{:S(2)}, u32[]{:S(2)}) async-start(f32[32,16,128]{2,1,0:T(8,128)} %get-tuple-element.25), calls=%async_computation.1 | async-start | bytes 524288 | tf_op jit(solution)/shard_map/all_to_all | solution.py:473
  79.4 7.7 %side.4 = (f32[128,1024]{1,0:T(8,128)}, f32[4,16,512]{2,1,0:T(8,128)}) custom-call(s32[2]{0:T(128)} %pad_add_fusion.place_ref, s32[5,128]{1,0:T(8,128)} %bitcast.26, f32[8,2048]{1,0:T(8,128)} %get-tuple-element.33.vrow_ref, f32[5,24,2048]{2,1,0:T(8,128)} %copy-done.7, f32[8,2,5,8,128]{4,3,2,1,0:T(8,128)} %constant.22.clone.tab_ref, ...), custom_call_target="tpu_custom_call" | custom-call | flops 4000000000 | bytes 6000000 | tf_op jit(solution)/shard_map/side/pallas_call | solution.py:483
  87.1 0.9 slice_select_fusion.1
  88.0 1.8 %collective-permute-start.6 = (f32[2,16,512]{2,1,0:T(8,128)S(1)}, f32[2,16,512]{2,1,0:T(8,128)S(1)}, u32[]{:S(2)}, u32[]{:S(2)}) collective-permute-start(f32[2,16,512]{2,1,0:T(8,128)S(1)} %slice_select_fusion.1), channel_id=1, source_target_pairs={{0,16},{8,24},{16,0},{24,8},{1,17},{9,25},{17,1},{25,9},{2,18},{10... | collective-permute-start | bytes 196616 | tf_op jit(solution)/shard_map/ppermute | solution.py:399
  90.5 1.9 %collective-permute-done.6 = f32[2,16,512]{2,1,0:T(8,128)S(1)} collective-permute-done((f32[2,16,512]{2,1,0:T(8,128)S(1)}, f32[2,16,512]{2,1,0:T(8,128)S(1)}, u32[]{:S(2)}, u32[]{:S(2)}) %collective-permute-start.6) | collective-permute-done | bytes 65568 | tf_op jit(solution)/shard_map/ppermute | solution.py:399
  92.4 0.7 copy-done.5
  93.1 10.1 %iterate.5 = (f32[32,16,128]{2,1,0:T(8,128)}, f32[128,1024]{1,0:T(8,128)}, f32[8,2048]{1,0:T(8,128)}, f32[6,8,16,128]{3,2,1,0:T(8,128)}, f32[1,128]{1,0:T(1,128)}) custom-call(s32[2]{0:T(128)} %pad_add_fusion.place_ref, s32[5,128]{1,0:T(8,128)} %bitcast.27, f32[5,24,2048]{2,1,0:T(8,128)} %copy-done.7, f32[8,2,5,8,128]{4,3,2,1,0:T(8,128)} %constant.22.clone.tab_ref, ...), custom_call_target="tpu_custom_call" | custom-call | flops 7000000000 | bytes 3000000 | tf_op jit(solution)/shard_map/iterate/pallas_call | solution.py:457
  103.2 7.7 %side.5 = (f32[128,1024]{1,0:T(8,128)}, f32[4,16,512]{2,1,0:T(8,128)}) custom-call(s32[2]{0:T(128)} %pad_add_fusion.place_ref, s32[5,128]{1,0:T(8,128)} %bitcast.28, f32[8,2048]{1,0:T(8,128)} %get-tuple-element.36.vrow_ref, f32[5,24,2048]{2,1,0:T(8,128)} %copy-done.7, f32[8,2,5,8,128]{4,3,2,1,0:T(8,128)} %constant.22.clone.tab_ref, ...), custom_call_target="tpu_custom_call" | custom-call | flops 4000000000 | bytes 6000000 | tf_op jit(solution)/shard_map/side/pallas_call | solution.py:483
  110.9 0.9 slice_select_fusion
  111.7 1.8 %collective-permute-start.8 = (f32[2,16,512]{2,1,0:T(8,128)S(1)}, f32[2,16,512]{2,1,0:T(8,128)S(1)}, u32[]{:S(2)}, u32[]{:S(2)}) collective-permute-start(f32[2,16,512]{2,1,0:T(8,128)S(1)} %slice_select_fusion), channel_id=1, source_target_pairs={{0,16},{8,24},{16,0},{24,8},{1,17},{9,25},{17,1},{25,9},{2,18},{10... | collective-permute-start | bytes 196616 | tf_op jit(solution)/shard_map/ppermute | solution.py:399
  113.6 6.0 %all-to-all-start.2 = ((f32[32,16,128]{2,1,0:T(8,128)}), f32[32,16,128]{2,1,0:T(8,128)S(1)}, u32[]{:S(2)}, u32[]{:S(2)}) async-start(f32[32,16,128]{2,1,0:T(8,128)} %get-tuple-element.27), calls=%async_computation.2 | async-start | bytes 524288 | tf_op jit(solution)/shard_map/all_to_all | solution.py:473
  120.0 0.6 add_bitcast_fusion.1.refs_6_
  121.6 8.5 %all-to-all-done.2.hits_ref = f32[32,16,128]{2,1,0:T(8,128)S(1)} async-done(((f32[32,16,128]{2,1,0:T(8,128)}), f32[32,16,128]{2,1,0:T(8,128)S(1)}, u32[]{:S(2)}, u32[]{:S(2)}) %all-to-all-start.2) | async-done | bytes 262176 | tf_op jit(solution)/shard_map/all_to_all | solution.py:473
  130.1 0.7 copy-done
  130.8 2.6 %combine.1 = (f32[128,1024]{1,0:T(8,128)}, f32[16,512]{1,0:T(8,128)}) custom-call(f32[6,8,16,128]{3,2,1,0:T(8,128)} %get-tuple-element.26.state_ref, f32[32,16,128]{2,1,0:T(8,128)} %copy-done, f32[1,128]{1,0:T(1,128)} %get-tuple-element.28.refs_0_, f32[1,128]{1,0:T(1,128)} %get-tuple-element.29.refs_1_, f32[128,1024]{1,0:T(8,128)} %get-tuple-element.32.refs_2_, ...), custom_call_target="tpu_custom_call" | custom-call | flops 10000000 | bytes 4000000 | tf_op jit(solution)/shard_map/combine/pallas_call | solution.py:486
  (38 shorter events, 3.1 us)
Async XLA Ops:
  12.5 11.6 %collective-permute-start = (f32[24,2048]{1,0:T(8,128)}, f32[24,2048]{1,0:T(8,128)S(1)}, u32[]{:S(2)}, u32[]{:S(2)}) collective-permute-start(f32[24,2048]{1,0:T(8,128)} %prepare.1), channel_id=1, source_target_pairs={{0,2},{1,3},{2,4},{3,5},{4,6},{5,7},{8,10},{9,11},{10,12},{11,13},... | collective-permute-start | bytes 589832 | tf_op jit(solution)/shard_map/ppermute | solution.py:438
  17.5 7.7 %collective-permute-start.1 = (f32[24,2048]{1,0:T(8,128)}, f32[24,2048]{1,0:T(8,128)S(1)}, u32[]{:S(2)}, u32[]{:S(2)}) collective-permute-start(f32[24,2048]{1,0:T(8,128)} %prepare.1), channel_id=1, source_target_pairs={{0,1},{1,2},{2,3},{3,4},{4,5},{5,6},{6,7},{8,9},{9,10},{10,11},{11... | collective-permute-start | bytes 589832 | tf_op jit(solution)/shard_map/ppermute | solution.py:438
  20.9 8.2 %collective-permute-start.2 = (f32[24,2048]{1,0:T(8,128)}, f32[24,2048]{1,0:T(8,128)S(1)}, u32[]{:S(2)}, u32[]{:S(2)}) collective-permute-start(f32[24,2048]{1,0:T(8,128)} %prepare.1), channel_id=1, source_target_pairs={{1,0},{2,1},{3,2},{4,3},{5,4},{6,5},{7,6},{9,8},{10,9},{11,10},{12... | collective-permute-start | bytes 589832 | tf_op jit(solution)/shard_map/ppermute | solution.py:438
  22.2 12.1 %collective-permute-start.3 = (f32[24,2048]{1,0:T(8,128)}, f32[24,2048]{1,0:T(8,128)S(1)}, u32[]{:S(2)}, u32[]{:S(2)}) collective-permute-start(f32[24,2048]{1,0:T(8,128)} %prepare.1), channel_id=1, source_target_pairs={{2,0},{3,1},{4,2},{5,3},{6,4},{7,5},{10,8},{11,9},{12,10},{13,11},... | collective-permute-start | bytes 589832 | tf_op jit(solution)/shard_map/ppermute | solution.py:438
  24.1 1.0 copy-start.6
  34.3 1.0 copy-start.7
  45.0 17.1 %all-to-all-start = ((f32[32,24,128]{2,1,0:T(8,128)}), f32[32,24,128]{2,1,0:T(8,128)S(1)}, u32[]{:S(2)}, u32[]{:S(2)}) async-start(f32[32,24,128]{2,1,0:T(8,128)} %get-tuple-element.23), calls=%async_computation | async-start | bytes 786432 | tf_op jit(solution)/shard_map/all_to_all | solution.py:473
  56.3 5.6 %copy-start.3 = (f32[4,16,512]{2,1,0:T(8,128)S(1)}, f32[4,16,512]{2,1,0:T(8,128)}, u32[]{:S(2)}) copy-start(f32[4,16,512]{2,1,0:T(8,128)} %get-tuple-element.39) | copy-start | bytes 393220
  57.2 4.7 %collective-permute-start.4 = (f32[2,16,512]{2,1,0:T(8,128)S(1)}, f32[2,16,512]{2,1,0:T(8,128)S(1)}, u32[]{:S(2)}, u32[]{:S(2)}) collective-permute-start(f32[2,16,512]{2,1,0:T(8,128)S(1)} %slice_select_fusion.2), channel_id=1, source_target_pairs={{0,16},{8,24},{16,0},{24,8},{1,17},{9,25},{17,1},{25,9},{2,18},{10... | collective-permute-start | bytes 196616 | tf_op jit(solution)/shard_map/ppermute | solution.py:399
  62.0 27.9 %collective-permute-start.5 = (f32[1,16,512]{2,1,0:T(8,128)S(1)}, f32[1,16,512]{2,1,0:T(8,128)S(1)}, u32[]{:S(2)}, u32[]{:S(2)}) collective-permute-start(f32[1,16,512]{2,1,0:T(8,128)S(1)} %slice_select_fusion.5), channel_id=1, source_target_pairs={{0,8},{8,0},{16,24},{24,16},{1,9},{9,1},{17,25},{25,17},{2,10},{10... | collective-permute-start | bytes 98312 | tf_op jit(solution)/shard_map/ppermute | solution.py:399
  62.1 0.8 copy-start.4
  72.9 19.5 %all-to-all-start.1 = ((f32[32,16,128]{2,1,0:T(8,128)}), f32[32,16,128]{2,1,0:T(8,128)S(1)}, u32[]{:S(2)}, u32[]{:S(2)}) async-start(f32[32,16,128]{2,1,0:T(8,128)} %get-tuple-element.25), calls=%async_computation.1 | async-start | bytes 524288 | tf_op jit(solution)/shard_map/all_to_all | solution.py:473
  87.1 5.3 %copy-start.2 = (f32[4,16,512]{2,1,0:T(8,128)S(1)}, f32[4,16,512]{2,1,0:T(8,128)}, u32[]{:S(2)}) copy-start(f32[4,16,512]{2,1,0:T(8,128)} %get-tuple-element.40) | copy-start | bytes 393220
  88.0 4.3 %collective-permute-start.6 = (f32[2,16,512]{2,1,0:T(8,128)S(1)}, f32[2,16,512]{2,1,0:T(8,128)S(1)}, u32[]{:S(2)}, u32[]{:S(2)}) collective-permute-start(f32[2,16,512]{2,1,0:T(8,128)S(1)} %slice_select_fusion.1), channel_id=1, source_target_pairs={{0,16},{8,24},{16,0},{24,8},{1,17},{9,25},{17,1},{25,9},{2,18},{10... | collective-permute-start | bytes 196616 | tf_op jit(solution)/shard_map/ppermute | solution.py:399
  92.4 0.7 copy-start.5
  111.7 7.9 %collective-permute-start.8 = (f32[2,16,512]{2,1,0:T(8,128)S(1)}, f32[2,16,512]{2,1,0:T(8,128)S(1)}, u32[]{:S(2)}, u32[]{:S(2)}) collective-permute-start(f32[2,16,512]{2,1,0:T(8,128)S(1)} %slice_select_fusion), channel_id=1, source_target_pairs={{0,16},{8,24},{16,0},{24,8},{1,17},{9,25},{17,1},{25,9},{2,18},{10... | collective-permute-start | bytes 196616 | tf_op jit(solution)/shard_map/ppermute | solution.py:399
  113.6 6.4 %collective-permute-start.7 = (f32[1,16,512]{2,1,0:T(8,128)S(1)}, f32[1,16,512]{2,1,0:T(8,128)S(1)}, u32[]{:S(2)}, u32[]{:S(2)}) collective-permute-start(f32[1,16,512]{2,1,0:T(8,128)S(1)} %slice_select_fusion.4), channel_id=1, source_target_pairs={{0,8},{8,0},{16,24},{24,16},{1,9},{9,1},{17,25},{25,17},{2,10},{10... | collective-permute-start | bytes 98312 | tf_op jit(solution)/shard_map/ppermute | solution.py:399
  113.6 6.1 %copy-start.1 = (f32[4,16,512]{2,1,0:T(8,128)S(1)}, f32[4,16,512]{2,1,0:T(8,128)}, u32[]{:S(2)}) copy-start(f32[4,16,512]{2,1,0:T(8,128)} %get-tuple-element.41) | copy-start | bytes 393220
  113.6 16.5 %all-to-all-start.2 = ((f32[32,16,128]{2,1,0:T(8,128)}), f32[32,16,128]{2,1,0:T(8,128)S(1)}, u32[]{:S(2)}, u32[]{:S(2)}) async-start(f32[32,16,128]{2,1,0:T(8,128)} %get-tuple-element.27), calls=%async_computation.2 | async-start | bytes 524288 | tf_op jit(solution)/shard_map/all_to_all | solution.py:473
  119.7 1.3 collective-permute-start.9
  130.1 0.7 copy-start

commit v6 on v5

--- a/solution.py
+++ b/solution.py
@@ -380,26 +380,14 @@
             image_ref[group, :, to : to + stop - start] = part[:, start:stop]
 
 
-def combine_kernel(state_ref, hits_ref, *refs):
+def combine_kernel(place_ref, state_ref, hits_ref, *refs):
     steps, controls, images = refs[: ITERS - 1], refs[ITERS - 1 : 2 * ITERS - 1], refs[2 * ITERS - 1 : 3 * ITERS - 1]
-    control_ref, image_ref = refs[3 * ITERS - 1 :]
+    control_ref, block_refs = refs[3 * ITERS - 1], refs[3 * ITERS :]
     last = step_of(sum_mem(hits_ref[...], state_ref.shape[1]), state_ref[2], state_ref[3])[0:1, 0:1]
     steps = [s[0:1, 0:1] for s in steps] + [last]
+    for away, block_ref in enumerate(block_refs):
+        block_ref[...] = sum(s * i[place_ref[0] ^ away] for s, i in zip(steps, images))
     control_ref[...] = sum(s * c[...] for s, c in zip(steps, controls))
-    image_ref[...] = sum(s * i[...] for s, i in zip(steps, images))
-
-
-def scatter_mem(a):
-    count = lax.axis_size("mem")
-    me = lax.axis_index("mem")
-    bit = count // 2
-    while bit:
-        low, high = a[: a.shape[0] // 2], a[a.shape[0] // 2 :]
-        upper = (me & bit) != 0
-        away = lax.ppermute(jnp.where(upper, low, high), "mem", [(i, i ^ bit) for i in range(count)])
-        a = jnp.where(upper, high, low) + away
-        bit //= 2
-    return a
 
 
 def on_device(perturbation, obs_cells, obs_count, innovation, obs_scale):
@@ -482,15 +470,17 @@
         )
         control, image = side(place, bound, got[2], near, tables, t1, got[1], field)
         controls.append(control)
-        images.append(scatter_mem(image)[0])
-    control, image = pl.pallas_call(
+        images.append(image)
+    control, image, *away = pl.pallas_call(
         combine_kernel,
-        out_shape=[f32((half, coarse_cols)), f32((fine_rows, width))],
-        in_specs=[vmem] * (3 * ITERS + 1),
-        out_specs=[vmem] * 2,
+        out_shape=[f32((half, coarse_cols))] + [f32((fine_rows, width))] * groups,
+        in_specs=[smem] + [vmem] * (3 * ITERS + 1),
+        out_specs=[vmem] * (1 + groups),
         cost_estimate=pl.CostEstimate(flops=10**7, bytes_accessed=4 * 10**6, transcendentals=0),
         name="combine",
-    )(state, hits, *steps, *controls, *images)
+    )(place, state, hits, *steps, *controls, *images)
+    for n, block in enumerate(away):
+        image = image + lax.ppermute(block, "mem", [(i, i ^ (n + 1)) for i in range(groups)])
     return control.reshape(members, coarse_rows, coarse_cols), image
 
 

time: 134 us -> 129 us (0.963)
  blocking collectives: 0 us -> 20.7 us
  starting transfers between devices: 33 us -> 21.5 us
  waiting for transfers between devices: 23.6 us -> 13.3 us
  other arithmetic: 5.28 us -> 1.99 us
    all_to_all x0 -> x1, blocking collectives: none -> 20.7 us  [on_device(): hits = lax.all_to_all(got[0], ('mem', 'lat'), 0, 0, tiled=True)]
    all_to_all x3 -> x2, starting transfers between devices: 16.1 us -> 7.52 us  [on_device(): hits = lax.all_to_all(got[0], ('mem', 'lat'), 0, 0, tiled=True)]
    all_to_all x3 -> x2, waiting for transfers between devices: 8.5 us -> 2.58 us  [on_device(): hits = lax.all_to_all(got[0], ('mem', 'lat'), 0, 0, tiled=True)]
    ppermute x6 -> x3, starting transfers between devices: 5.89 us -> 1.88 us  [on_device(): lax.ppermute(block, 'mem', [(i, i ^ n + 1) for i in range(groups)])]
    ppermute x4, waiting for transfers between devices: 10.1 us -> 7.12 us  [on_device(): lax.ppermute(own, 'lat', [(s, s - d) for s in range(bands) if 0 <= s - d...]
    select_n x6 -> x0, other arithmetic: 2.75 us -> none  [scatter_mem(): jnp.where(upper, low, high)]
    squeeze x3 -> x0, other arithmetic: 1.86 us -> none  [on_device(): images.append(scatter_mem(image)[0])]
    ppermute x6 -> x3, waiting for transfers between devices: 5.08 us -> 3.62 us  [on_device(): lax.ppermute(block, 'mem', [(i, i ^ n + 1) for i in range(groups)])]
  transfers between devices with their start and end apart: 13 -> 9, of which waited for: 7 -> 4; matrix products, arithmetic and copies ran while one was open for 3% -> 1% of each run, Pallas kernels for 19% -> 18%
where the time goes in v6:
time: 129 us; the launch traced here: 128 us
  Pallas kernels  66.8 us (52%)
  starting transfers between devices  21.5 us (17%)
  blocking collectives  20.7 us (16%)
  waiting for transfers between devices  13.3 us (10%)
  local copies, waits for them, and re-layouts  2.42 us (2%)
  other arithmetic  1.99 us (2%)
  between operations  1.42 us (1%)
    pallas_call x3, Pallas kernels, on_device(): pl.pallas_call(functools.partial(iter_kernel, members=members, coarse_row...  29.8 us
    pallas_call x3, Pallas kernels, on_device(): control, image = side(place, bound, got[2], near, tables, t1, got[1], field)  23.1 us
    all_to_all x1, blocking collectives, on_device(): hits = lax.all_to_all(got[0], ('mem', 'lat'), 0, 0, tiled=True)  20.7 us
    ppermute x4, starting transfers between devices, on_device(): lax.ppermute(own, 'lat', [(s, s - d) for s in range(bands) if 0 <= s - d...  12.1 us
    pallas_call x1, Pallas kernels, on_device(): pl.pallas_call(functools.partial(prepare_kernel, members=members, fine_ro...  11.2 us
    all_to_all x2, starting transfers between devices, on_device(): hits = lax.all_to_all(got[0], ('mem', 'lat'), 0, 0, tiled=True)  7.52 us
    ppermute x4, waiting for transfers between devices, on_device(): lax.ppermute(own, 'lat', [(s, s - d) for s in range(bands) if 0 <= s - d...  7.12 us
    ppermute x3, waiting for transfers between devices, on_device(): lax.ppermute(block, 'mem', [(i, i ^ n + 1) for i in range(groups)])  3.62 us
  transfers between devices with their start and end apart: 9, of which 4 were waited for; matrix products, arithmetic and copies ran while one was open for 1% of the time, Pallas kernels for 18%

profile of v6, /device:TPU:0, one launch (start us, length us, event | category | flops | bytes accessed | tf_op | source)
XLA Modules:
  0.0 128.2 jit_solution(10701769779437416293)
XLA Ops:
  1.3 11.2 %prepare.1 = f32[24,2048]{1,0:T(8,128)} custom-call(s32[1]{0:T(128)S(6)} %copy.17.count_ref, bf16[256,2048]{1,0:T(8,128)(2,1)} %bitcast.23, s32[1,2048]{1,0:T(1,128)} %refs_0_.1, f32[1,2048]{1,0:T(1,128)} %innovation_ref.1, f32[1,2048]{1,0:T(1,128)} %scale_ref.1), custom_call_target="tpu_custom_call" | custom-call | flops 4000000000 | bytes 2000000 | tf_op jit(solution)/shard_map/prepare/pallas_call | solution.py:411
  12.5 5.0 %collective-permute-start = (f32[24,2048]{1,0:T(8,128)}, f32[24,2048]{1,0:T(8,128)S(1)}, u32[]{:S(2)}, u32[]{:S(2)}) collective-permute-start(f32[24,2048]{1,0:T(8,128)} %prepare.1), channel_id=1, source_target_pairs={{0,2},{1,3},{2,4},{3,5},{4,6},{5,7},{8,10},{9,11},{10,12},{11,13},... | collective-permute-start | bytes 589832 | tf_op jit(solution)/shard_map/ppermute | solution.py:426
  17.5 1.3 %collective-permute-start.3 = (f32[24,2048]{1,0:T(8,128)}, f32[24,2048]{1,0:T(8,128)S(1)}, u32[]{:S(2)}, u32[]{:S(2)}) collective-permute-start(f32[24,2048]{1,0:T(8,128)} %prepare.1), channel_id=1, source_target_pairs={{2,0},{3,1},{4,2},{5,3},{6,4},{7,5},{10,8},{11,9},{12,10},{13,11},... | collective-permute-start | bytes 589832 | tf_op jit(solution)/shard_map/ppermute | solution.py:426
  18.8 1.3 %collective-permute-start.2 = (f32[24,2048]{1,0:T(8,128)}, f32[24,2048]{1,0:T(8,128)S(1)}, u32[]{:S(2)}, u32[]{:S(2)}) collective-permute-start(f32[24,2048]{1,0:T(8,128)} %prepare.1), channel_id=1, source_target_pairs={{1,0},{2,1},{3,2},{4,3},{5,4},{6,5},{7,6},{9,8},{10,9},{11,10},{12... | collective-permute-start | bytes 589832 | tf_op jit(solution)/shard_map/ppermute | solution.py:426
  20.1 4.6 %collective-permute-start.1 = (f32[24,2048]{1,0:T(8,128)}, f32[24,2048]{1,0:T(8,128)S(1)}, u32[]{:S(2)}, u32[]{:S(2)}) collective-permute-start(f32[24,2048]{1,0:T(8,128)} %prepare.1), channel_id=1, source_target_pairs={{0,1},{1,2},{2,3},{3,4},{4,5},{5,6},{6,7},{8,9},{9,10},{10,11},{11... | collective-permute-start | bytes 589832 | tf_op jit(solution)/shard_map/ppermute | solution.py:426
  24.6 0.6 pad_add_fusion.place_ref
  25.2 0.0 collective-permute-done
  25.2 0.0 copy-start.2
  25.3 7.1 %collective-permute-done.1 = f32[24,2048]{1,0:T(8,128)S(1)} collective-permute-done((f32[24,2048]{1,0:T(8,128)}, f32[24,2048]{1,0:T(8,128)S(1)}, u32[]{:S(2)}, u32[]{:S(2)}) %collective-permute-start.1) | collective-permute-done | bytes 196640 | tf_op jit(solution)/shard_map/ppermute | solution.py:426
  32.5 0.0 collective-permute-done.3
  32.5 0.7 copy.12
  33.2 0.3 copy-done.3
  33.5 9.7 %iterate.3 = (f32[32,24,128]{2,1,0:T(8,128)}, f32[128,1024]{1,0:T(8,128)}, f32[8,2048]{1,0:T(8,128)}) custom-call(s32[2]{0:T(128)} %pad_add_fusion.place_ref, s32[5,128]{1,0:T(8,128)} %bitcast.17, f32[5,24,2048]{2,1,0:T(8,128)} %copy-done.3, f32[8,2,5,8,128]{4,3,2,1,0:T(8,128)} %constant.16.clone.tab_ref, bf16[2,512,256]{2,1,0:T(8,128)(2,1)} %constant.27.t2_ref), custom_call_target="tpu_custom_call" | custom-call | flops 7000000000 | bytes 3000000 | tf_op jit(solution)/shard_map/iterate/pallas_call | solution.py:445
  43.1 20.7 %all_to_all.15.refs_1_ = f32[32,24,128]{2,1,0:T(8,128)} all-to-all(f32[32,24,128]{2,1,0:T(8,128)} %get-tuple-element.26), channel_id=1, replica_groups=mesh['mem'=4,'lat'=8] {'mem','lat'}, dimensions={0} | all-to-all | bytes 786432 | tf_op jit(solution)/shard_map/all_to_all | solution.py:461
  63.8 10.1 %iterate.4 = (f32[32,16,128]{2,1,0:T(8,128)}, f32[128,1024]{1,0:T(8,128)}, f32[8,2048]{1,0:T(8,128)}, f32[6,8,16,128]{3,2,1,0:T(8,128)}, f32[1,128]{1,0:T(1,128)}) custom-call(s32[2]{0:T(128)} %pad_add_fusion.place_ref, s32[5,128]{1,0:T(8,128)} %bitcast.18, f32[5,24,2048]{2,1,0:T(8,128)} %copy-done.3, f32[8,2,5,8,128]{4,3,2,1,0:T(8,128)} %constant.16.clone.tab_ref, ...), custom_call_target="tpu_custom_call" | custom-call | flops 7000000000 | bytes 3000000 | tf_op jit(solution)/shard_map/iterate/pallas_call | solution.py:445
  73.9 3.5 %all-to-all-start.1 = ((f32[32,16,128]{2,1,0:T(8,128)}), f32[32,16,128]{2,1,0:T(8,128)S(1)}, u32[]{:S(2)}, u32[]{:S(2)}) async-start(f32[32,16,128]{2,1,0:T(8,128)} %get-tuple-element.28), calls=%async_computation.1 | async-start | bytes 524288 | tf_op jit(solution)/shard_map/all_to_all | solution.py:461
  77.4 7.7 %side.3 = (f32[128,1024]{1,0:T(8,128)}, f32[4,16,512]{2,1,0:T(8,128)}) custom-call(s32[2]{0:T(128)} %pad_add_fusion.place_ref, s32[5,128]{1,0:T(8,128)} %bitcast.19, f32[8,2048]{1,0:T(8,128)} %get-tuple-element.33.vrow_ref, f32[5,24,2048]{2,1,0:T(8,128)} %copy-done.3, f32[8,2,5,8,128]{4,3,2,1,0:T(8,128)} %constant.16.clone.tab_ref, ...), custom_call_target="tpu_custom_call" | custom-call | flops 4000000000 | bytes 6000000 | tf_op jit(solution)/shard_map/side/pallas_call | solution.py:471
  85.1 2.6 %all-to-all-done.1.refs_1_ = f32[32,16,128]{2,1,0:T(8,128)S(1)} async-done(((f32[32,16,128]{2,1,0:T(8,128)}), f32[32,16,128]{2,1,0:T(8,128)S(1)}, u32[]{:S(2)}, u32[]{:S(2)}) %all-to-all-start.1) | async-done | bytes 262176 | tf_op jit(solution)/shard_map/all_to_all | solution.py:461
  87.7 0.7 copy-done.1
  88.4 10.1 %iterate.5 = (f32[32,16,128]{2,1,0:T(8,128)}, f32[128,1024]{1,0:T(8,128)}, f32[8,2048]{1,0:T(8,128)}, f32[6,8,16,128]{3,2,1,0:T(8,128)}, f32[1,128]{1,0:T(1,128)}) custom-call(s32[2]{0:T(128)} %pad_add_fusion.place_ref, s32[5,128]{1,0:T(8,128)} %bitcast.20, f32[5,24,2048]{2,1,0:T(8,128)} %copy-done.3, f32[8,2,5,8,128]{4,3,2,1,0:T(8,128)} %constant.16.clone.tab_ref, ...), custom_call_target="tpu_custom_call" | custom-call | flops 7000000000 | bytes 3000000 | tf_op jit(solution)/shard_map/iterate/pallas_call | solution.py:445
  98.5 4.0 %all-to-all-start.2 = ((f32[32,16,128]{2,1,0:T(8,128)}), f32[32,16,128]{2,1,0:T(8,128)S(1)}, u32[]{:S(2)}, u32[]{:S(2)}) async-start(f32[32,16,128]{2,1,0:T(8,128)} %get-tuple-element.30), calls=%async_computation.2 | async-start | bytes 524288 | tf_op jit(solution)/shard_map/all_to_all | solution.py:461
  102.5 7.7 %side.4 = (f32[128,1024]{1,0:T(8,128)}, f32[4,16,512]{2,1,0:T(8,128)}) custom-call(s32[2]{0:T(128)} %pad_add_fusion.place_ref, s32[5,128]{1,0:T(8,128)} %bitcast.21, f32[8,2048]{1,0:T(8,128)} %get-tuple-element.36.vrow_ref, f32[5,24,2048]{2,1,0:T(8,128)} %copy-done.3, f32[8,2,5,8,128]{4,3,2,1,0:T(8,128)} %constant.16.clone.tab_ref, ...), custom_call_target="tpu_custom_call" | custom-call | flops 4000000000 | bytes 6000000 | tf_op jit(solution)/shard_map/side/pallas_call | solution.py:471
  110.2 7.7 %side.5 = (f32[128,1024]{1,0:T(8,128)}, f32[4,16,512]{2,1,0:T(8,128)}) custom-call(s32[2]{0:T(128)} %pad_add_fusion.place_ref, s32[5,128]{1,0:T(8,128)} %bitcast.22, f32[8,2048]{1,0:T(8,128)} %get-tuple-element.39.vrow_ref, f32[5,24,2048]{2,1,0:T(8,128)} %copy-done.3, f32[8,2,5,8,128]{4,3,2,1,0:T(8,128)} %constant.16.clone.tab_ref, ...), custom_call_target="tpu_custom_call" | custom-call | flops 4000000000 | bytes 6000000 | tf_op jit(solution)/shard_map/side/pallas_call | solution.py:471
  117.9 0.7 copy-done
  118.6 2.7 %combine.1 = (f32[128,1024]{1,0:T(8,128)}, f32[16,512]{1,0:T(8,128)}, f32[16,512]{1,0:T(8,128)}, f32[16,512]{1,0:T(8,128)}, f32[16,512]{1,0:T(8,128)}) custom-call(s32[2]{0:T(128)} %pad_add_fusion.place_ref, f32[6,8,16,128]{3,2,1,0:T(8,128)} %get-tuple-element.29.state_ref, f32[32,16,128]{2,1,0:T(8,128)} %copy-done, f32[1,128]{1,0:T(1,128)} %get-tuple-element.31.refs_0_, ...), custom_call_target="tpu_custom_call" | custom-call | flops 10000000 | bytes 4000000 | tf_op jit(solution)/shard_map/combine/pallas_call | solution.py:474
  121.3 0.2 collective-permute-start.4
  121.6 1.6 %collective-permute-start.5 = (f32[16,512]{1,0:T(8,128)}, f32[16,512]{1,0:T(8,128)S(1)}, u32[]{:S(2)}, u32[]{:S(2)}) collective-permute-start(f32[16,512]{1,0:T(8,128)} %get-tuple-element.48), channel_id=1, source_target_pairs={{0,16},{8,24},{16,0},{24,8},{1,17},{9,25},{17,1},{25,9},{2,18},{10... | collective-permute-start | bytes 98312 | tf_op jit(solution)/shard_map/ppermute | solution.py:483
  123.2 0.0 collective-permute-start.6
  123.2 0.0 collective-permute-done.4
  123.2 2.5 %collective-permute-done.5 = f32[16,512]{1,0:T(8,128)S(1)} collective-permute-done((f32[16,512]{1,0:T(8,128)}, f32[16,512]{1,0:T(8,128)S(1)}, u32[]{:S(2)}, u32[]{:S(2)}) %collective-permute-start.5) | collective-permute-done | bytes 32800 | tf_op jit(solution)/shard_map/ppermute | solution.py:483
  125.7 1.1 collective-permute-done.6
  126.8 1.4 %add_add_fusion = f32[16,512]{1,0:T(8,128)} fusion(f32[16,512]{1,0:T(8,128)S(1)} %collective-permute-done.6, f32[16,512]{1,0:T(8,128)S(1)} %collective-permute-done.5, f32[16,512]{1,0:T(8,128)} %get-tuple-element.46, f32[16,512]{1,0:T(8,128)S(1)} %collective-permute-done.4), kind=kLoop, calls=%fused_computation.5 | loop fusion | flops 24576 | bytes 163840 | tf_op jit(solution)/shard_map/add | solution.py:483
  (12 shorter events, 0.1 us)
Async XLA Ops:
  12.5 12.7 %collective-permute-start = (f32[24,2048]{1,0:T(8,128)}, f32[24,2048]{1,0:T(8,128)S(1)}, u32[]{:S(2)}, u32[]{:S(2)}) collective-permute-start(f32[24,2048]{1,0:T(8,128)} %prepare.1), channel_id=1, source_target_pairs={{0,2},{1,3},{2,4},{3,5},{4,6},{5,7},{8,10},{9,11},{10,12},{11,13},... | collective-permute-start | bytes 589832 | tf_op jit(solution)/shard_map/ppermute | solution.py:426
  17.5 15.0 %collective-permute-start.3 = (f32[24,2048]{1,0:T(8,128)}, f32[24,2048]{1,0:T(8,128)S(1)}, u32[]{:S(2)}, u32[]{:S(2)}) collective-permute-start(f32[24,2048]{1,0:T(8,128)} %prepare.1), channel_id=1, source_target_pairs={{2,0},{3,1},{4,2},{5,3},{6,4},{7,5},{10,8},{11,9},{12,10},{13,11},... | collective-permute-start | bytes 589832 | tf_op jit(solution)/shard_map/ppermute | solution.py:426
  18.8 13.7 %collective-permute-start.2 = (f32[24,2048]{1,0:T(8,128)}, f32[24,2048]{1,0:T(8,128)S(1)}, u32[]{:S(2)}, u32[]{:S(2)}) collective-permute-start(f32[24,2048]{1,0:T(8,128)} %prepare.1), channel_id=1, source_target_pairs={{1,0},{2,1},{3,2},{4,3},{5,4},{6,5},{7,6},{9,8},{10,9},{11,10},{12... | collective-permute-start | bytes 589832 | tf_op jit(solution)/shard_map/ppermute | solution.py:426
  20.1 12.3 %collective-permute-start.1 = (f32[24,2048]{1,0:T(8,128)}, f32[24,2048]{1,0:T(8,128)S(1)}, u32[]{:S(2)}, u32[]{:S(2)}) collective-permute-start(f32[24,2048]{1,0:T(8,128)} %prepare.1), channel_id=1, source_target_pairs={{0,1},{1,2},{2,3},{3,4},{4,5},{5,6},{6,7},{8,9},{9,10},{10,11},{11... | collective-permute-start | bytes 589832 | tf_op jit(solution)/shard_map/ppermute | solution.py:426
  25.2 7.1 %copy-start.2 = (f32[24,2048]{1,0:T(8,128)S(1)}, f32[24,2048]{1,0:T(8,128)}, u32[]{:S(2)}) copy-start(f32[24,2048]{1,0:T(8,128)} %prepare.1) | copy-start | bytes 589828
  32.5 1.0 copy-start.3
  73.9 13.8 %all-to-all-start.1 = ((f32[32,16,128]{2,1,0:T(8,128)}), f32[32,16,128]{2,1,0:T(8,128)S(1)}, u32[]{:S(2)}, u32[]{:S(2)}) async-start(f32[32,16,128]{2,1,0:T(8,128)} %get-tuple-element.28), calls=%async_computation.1 | async-start | bytes 524288 | tf_op jit(solution)/shard_map/all_to_all | solution.py:461
  87.7 0.7 copy-start.1
  98.5 19.4 %all-to-all-start.2 = ((f32[32,16,128]{2,1,0:T(8,128)}), f32[32,16,128]{2,1,0:T(8,128)S(1)}, u32[]{:S(2)}, u32[]{:S(2)}) async-start(f32[32,16,128]{2,1,0:T(8,128)} %get-tuple-element.30), calls=%async_computation.2 | async-start | bytes 524288 | tf_op jit(solution)/shard_map/all_to_all | solution.py:461
  117.9 0.7 copy-start
  121.3 1.9 %collective-permute-start.4 = (f32[16,512]{1,0:T(8,128)}, f32[16,512]{1,0:T(8,128)S(1)}, u32[]{:S(2)}, u32[]{:S(2)}) collective-permute-start(f32[16,512]{1,0:T(8,128)} %get-tuple-element.47), channel_id=1, source_target_pairs={{0,8},{8,0},{16,24},{24,16},{1,9},{9,1},{17,25},{25,17},{2,10},{10... | collective-permute-start | bytes 98312 | tf_op jit(solution)/shard_map/ppermute | solution.py:483
  121.6 4.1 %collective-permute-start.5 = (f32[16,512]{1,0:T(8,128)}, f32[16,512]{1,0:T(8,128)S(1)}, u32[]{:S(2)}, u32[]{:S(2)}) collective-permute-start(f32[16,512]{1,0:T(8,128)} %get-tuple-element.48), channel_id=1, source_target_pairs={{0,16},{8,24},{16,0},{24,8},{1,17},{9,25},{17,1},{25,9},{2,18},{10... | collective-permute-start | bytes 98312 | tf_op jit(solution)/shard_map/ppermute | solution.py:483
  123.2 3.6 %collective-permute-start.6 = (f32[16,512]{1,0:T(8,128)}, f32[16,512]{1,0:T(8,128)S(1)}, u32[]{:S(2)}, u32[]{:S(2)}) collective-permute-start(f32[16,512]{1,0:T(8,128)} %get-tuple-element.49), channel_id=1, source_target_pairs={{0,24},{8,16},{16,8},{24,0},{1,25},{9,17},{17,9},{25,1},{2,26},{10... | collective-permute-start | bytes 98312 | tf_op jit(solution)/shard_map/ppermute | solution.py:483

commit v7 on v6

--- a/solution.py
+++ b/solution.py
@@ -17,6 +17,9 @@
 EDGE = 128
 META = 8
 WINDOW = 768
+SMALL = 512
+VMEM_LIMIT = 24 * 2**20
+REST = 256
 
 
 def lat_tables(bands, coarse_rows):
@@ -168,10 +171,23 @@
     out_ref[...] = srt_ref[:, :slots]
 
 
-def windows(bound_ref, d, c):
-    s, e = bound_ref[d, c], bound_ref[d, 64 + c]
-    start = s // 128 * 128
-    return start, jnp.where(e > s, (e - start + WINDOW - 1) // WINDOW, 0)
+def window(bound_ref, d, c):
+    return bound_ref[d, c] // 128 * 128, bound_ref[d, 64 + c]
+
+
+def rest(bound_ref, d, blocks, done, fn):
+    def block(c, _):
+        start, end = window(bound_ref, d, c)
+        start = start + jnp.where(c < blocks, done, 0)
+        trips = jnp.where(end > start, (end - start + REST - 1) // REST, 0)
+
+        def more(i, _):
+            fn(c, start + i * REST, REST)
+            return 0
+
+        return lax.fori_loop(0, trips, more, 0)
+
+    lax.fori_loop(0, blocks + 1, block, 0)
 
 
 def scatter(bound_ref, q_ref, tab, v_of, first, last, lhs_ref, at_ref, x_ref, members, coarse_rows):
@@ -196,27 +212,26 @@
             lhs_ref[k * coarse_rows : (k + 1) * coarse_rows, :slots] = hi
             lhs_ref[half + k * coarse_rows : half + (k + 1) * coarse_rows, :slots] = lo
 
-        def one(c, start):
-            at = pl.ds(pl.multiple_of(start, 128), WINDOW)
-            hat = hat_of(at_ref[0:1, at] - c * float(BLK), BLK)
+        def one(c, start, size):
+            at = pl.ds(pl.multiple_of(start, 128), size)
+            to = pl.ds(pl.multiple_of(c * BLK, BLK), BLK)
+            hat = hat_of(at_ref[0:1, at] - jnp.float32(c) * float(BLK), BLK)
             got = dot(lhs_ref[:, at], hat, ((1,), (1,)))
-            return got[:half] + got[half:]
-
+            x_ref[:, to] = x_ref[:, to] + (got[:half] + got[half:])
+
+        longest = 0
         for c in range(blocks):
-            to = slice(c * BLK, (c + 1) * BLK)
-            x_ref[:, to] = x_ref[:, to] + one(float(c), windows(bound_ref, d, c)[0])
-
-        def rest(c, _):
-            start, trips = windows(bound_ref, d, c)
-            to = pl.ds(pl.multiple_of(c * BLK, BLK), BLK)
-
-            def more(i, _):
-                x_ref[:, to] = x_ref[:, to] + one(c.astype(jnp.float32), start + i * WINDOW)
-                return 0
-
-            return lax.fori_loop(jnp.where(c < blocks, 1, 0), trips, more, 0)
-
-        return lax.fori_loop(0, blocks + 1, rest, 0)
+            start, end = window(bound_ref, d, c)
+            longest = jnp.maximum(longest, end - start)
+
+        def run(size):
+            for c in range(blocks):
+                one(c, window(bound_ref, d, c)[0], size)
+
+        pl.when(longest <= SMALL)(lambda: run(SMALL))
+        pl.when(longest > SMALL)(lambda: run(WINDOW))
+        rest(bound_ref, d, blocks, WINDOW, one)
+        return 0
 
     lax.fori_loop(first, last, band, 0)
     x_ref[:, :EDGE] = x_ref[:, :EDGE] + x_ref[:, blocks * BLK : blocks * BLK + EDGE]
@@ -261,11 +276,12 @@
     share = tiles // groups
     band = place_ref[1]
     if order == 0:
-        part_ref, b_ref, vrow_ref, lhs_ref, at_ref, x_ref, rows_ref, bhl_ref, own_ref = refs
+        out_ref, b_ref, vrow_ref, lhs_ref, at_ref, x_ref, rows_ref, bhl_ref, own_ref, part_ref = refs
         for d in range(NREL):
             vrow_ref[d : d + 1, :] = pull_of(q_ref[d, members + 2 : members + 3, :], q_ref[d, members + 3 : members + 4, :])[0]
     else:
-        old_ref, hits_ref, part_ref, b_ref, vrow_ref, state_ref, step_ref, lhs_ref, at_ref, x_ref, rows_ref, bhl_ref, own_ref = refs
+        old_ref, in_ref, out_ref, b_ref, vrow_ref, state_ref, step_ref, lhs_ref, at_ref, x_ref, rows_ref, bhl_ref, own_ref, part_ref, hits_ref = refs
+        pltpu.sync_copy(in_ref, hits_ref)
         hits = sum_mem(hits_ref[:, :tiles, :], bands)
         if order == 1:
             for g in range(groups):
@@ -307,13 +323,13 @@
     own_ref[:, slots:] = jnp.zeros((members + META, WINDOW), jnp.float32)
     rows_ref[...] = jnp.zeros_like(rows_ref)
 
-    def gather(c, start):
-        at = pl.ds(pl.multiple_of(start, 128), WINDOW)
+    def gather(c, start, size):
+        at = pl.ds(pl.multiple_of(start, 128), size)
         row = jnp.floor(own_ref[members + 1 : members + 2, at] * 0.5)
         hat = hat_of(own_ref[members : members + 1, at] - jnp.float32(c) * float(BLK), BLK)
         got = dot(bhl_ref[:, pl.ds(pl.multiple_of(c * BLK, BLK), BLK)], hat)
-        mask = jnp.where(full((coarse_rows, WINDOW), 0) == row, scale2, 0.0)
-        total = jnp.zeros((coarse_rows, WINDOW), jnp.float32)
+        mask = jnp.where(full((coarse_rows, size), 0) == row, scale2, 0.0)
+        total = jnp.zeros((coarse_rows, size), jnp.float32)
         for k in range(members):
             r = slice(k * coarse_rows, (k + 1) * coarse_rows)
             r2 = slice(half + k * coarse_rows, half + (k + 1) * coarse_rows)
@@ -321,18 +337,8 @@
         rows_ref[0:1, at] = rows_ref[0:1, at] + jnp.sum(total * mask, axis=0, keepdims=True)
 
     for c in range(blocks):
-        gather(c, windows(bound_ref, REACH, c)[0])
-
-    def rest(c, _):
-        start, trips = windows(bound_ref, REACH, c)
-
-        def more(i, _):
-            gather(c, start + i * WINDOW)
-            return 0
-
-        return lax.fori_loop(jnp.where(c < blocks, 1, 0), trips, more, 0)
-
-    lax.fori_loop(0, blocks + 1, rest, 0)
+        gather(c, window(bound_ref, REACH, c)[0], WINDOW)
+    rest(bound_ref, REACH, blocks, WINDOW, gather)
     for i in range(tiles):
         part_ref[0, i : i + 1, :] = rows_ref[0:1, i * 128 : (i + 1) * 128]
     if order == 0:
@@ -343,6 +349,7 @@
                 to = tiles + r * share + i
                 part_ref[0, to : to + 1, :] = row[:, i * 128 : (i + 1) * 128]
     part_ref[1:] = jnp.broadcast_to(part_ref[0][None], (part_ref.shape[0] - 1,) + part_ref.shape[1:])
+    pltpu.sync_copy(part_ref, out_ref)
 
 
 def side_kernel(
@@ -380,9 +387,10 @@
             image_ref[group, :, to : to + stop - start] = part[:, start:stop]
 
 
-def combine_kernel(place_ref, state_ref, hits_ref, *refs):
+def combine_kernel(place_ref, state_ref, in_ref, *refs):
     steps, controls, images = refs[: ITERS - 1], refs[ITERS - 1 : 2 * ITERS - 1], refs[2 * ITERS - 1 : 3 * ITERS - 1]
-    control_ref, block_refs = refs[3 * ITERS - 1], refs[3 * ITERS :]
+    control_ref, block_refs, hits_ref = refs[3 * ITERS - 1], refs[3 * ITERS : -1], refs[-1]
+    pltpu.sync_copy(in_ref, hits_ref)
     last = step_of(sum_mem(hits_ref[...], state_ref.shape[1]), state_ref[2], state_ref[3])[0:1, 0:1]
     steps = [s[0:1, 0:1] for s in steps] + [last]
     for away, block_ref in enumerate(block_refs):
@@ -405,6 +413,8 @@
 
     smem = pl.BlockSpec(memory_space=pltpu.SMEM)
     vmem = pl.BlockSpec(memory_space=pltpu.VMEM)
+    anywhere = pl.BlockSpec(memory_space=pl.ANY)
+    params = pltpu.CompilerParams(vmem_limit_bytes=VMEM_LIMIT)
     f32 = functools.partial(jax.ShapeDtypeStruct, dtype=jnp.float32)
 
     field = perturbation.reshape(members * fine_rows, lon_cells)
@@ -419,6 +429,7 @@
             pltpu.VMEM((members + META, slots + 512), jnp.float32),
         ],
         cost_estimate=pl.CostEstimate(flops=4 * 10**9, bytes_accessed=2 * 10**6, transcendentals=0),
+        compiler_params=params,
         name="prepare",
     )(obs_count, field, obs_cells, innovation, obs_scale)
     near = []
@@ -447,12 +458,15 @@
                 iter_kernel, members=members, coarse_rows=coarse_rows, scale2=scale * scale, order=order, bands=bands, groups=groups
             ),
             out_shape=outs,
-            in_specs=[smem] * 2 + [vmem] * (len(ins) - 2),
-            out_specs=[vmem] * len(outs),
+            in_specs=[smem] * 2 + [vmem] * 3 + ([vmem, anywhere] if iteration else []),
+            out_specs=[anywhere] + [vmem] * (len(outs) - 1),
             scratch_shapes=scratch
             + [pltpu.VMEM((8, padded), jnp.float32)]
-            + [pltpu.VMEM((2 * half, coarse_cols + BLK), jnp.bfloat16), pltpu.VMEM((members + META, padded), jnp.float32)],
+            + [pltpu.VMEM((2 * half, coarse_cols + BLK), jnp.bfloat16), pltpu.VMEM((members + META, padded), jnp.float32)]
+            + [pltpu.VMEM(block, jnp.float32)]
+            + ([pltpu.VMEM(hits.shape, jnp.float32)] if iteration else []),
             cost_estimate=pl.CostEstimate(flops=7 * 10**9, bytes_accessed=3 * 10**6, transcendentals=0),
+            compiler_params=params,
             name="iterate",
         )(*ins)
         if iteration:
@@ -466,6 +480,7 @@
             out_specs=[vmem] * 2,
             scratch_shapes=scratch,
             cost_estimate=pl.CostEstimate(flops=4 * 10**9, bytes_accessed=6 * 10**6, transcendentals=0),
+            compiler_params=params,
             name="side",
         )
         control, image = side(place, bound, got[2], near, tables, t1, got[1], field)
@@ -474,9 +489,11 @@
     control, image, *away = pl.pallas_call(
         combine_kernel,
         out_shape=[f32((half, coarse_cols))] + [f32((fine_rows, width))] * groups,
-        in_specs=[smem] + [vmem] * (3 * ITERS + 1),
+        in_specs=[smem, vmem, anywhere] + [vmem] * (3 * ITERS - 1),
         out_specs=[vmem] * (1 + groups),
+        scratch_shapes=[pltpu.VMEM(hits.shape, jnp.float32)],
         cost_estimate=pl.CostEstimate(flops=10**7, bytes_accessed=4 * 10**6, transcendentals=0),
+        compiler_params=params,
         name="combine",
     )(place, state, hits, *steps, *controls, *images)
     for n, block in enumerate(away):

time: 129 us -> 129 us (level)
  local copies, waits for them, and re-layouts: 2.42 us -> 18 us
  Pallas kernels: 66.8 us -> 54.7 us
  starting transfers between devices: 21.5 us -> 19.9 us
    unnamed x13 -> x61, local copies, waits for them, and re-layouts: 2.41 us -> 18 us
    pallas_call x3, Pallas kernels: 23.1 us -> 17.2 us  [on_device(): control, image = side(place, bound, got[2], near, tables, t1, got[1], field)]
    pallas_call x3, Pallas kernels: 29.8 us -> 26.5 us  [on_device(): pl.pallas_call(functools.partial(iter_kernel, members=members, coarse_row...]
    pallas_call x1, Pallas kernels: 11.2 us -> 9.29 us  [on_device(): pl.pallas_call(functools.partial(prepare_kernel, members=members, fine_ro...]
    all_to_all x2, starting transfers between devices: 7.52 us -> 5.94 us  [on_device(): hits = lax.all_to_all(got[0], ('mem', 'lat'), 0, 0, tiled=True)]
  transfers between devices with their start and end apart: 9 -> 9, of which waited for: 4 -> 4; matrix products, arithmetic and copies ran while one was open for 1% -> 0% of each run, Pallas kernels for 18% -> 13%
where the time goes in v7:
time: 129 us; the launch traced here: 128 us
  Pallas kernels  54.7 us (42%)
  blocking collectives  20 us (16%)
  starting transfers between devices  19.9 us (15%)
  local copies, waits for them, and re-layouts  18 us (14%)
  waiting for transfers between devices  13.1 us (10%)
  between operations  1.59 us (1%)
    pallas_call x3, Pallas kernels, on_device(): pl.pallas_call(functools.partial(iter_kernel, members=members, coarse_row...  26.5 us
    all_to_all x1, blocking collectives, on_device(): hits = lax.all_to_all(got[0], ('mem', 'lat'), 0, 0, tiled=True)  20 us
    unnamed x61, local copies, waits for them, and re-layouts  18 us
    pallas_call x3, Pallas kernels, on_device(): control, image = side(place, bound, got[2], near, tables, t1, got[1], field)  17.2 us
    ppermute x4, starting transfers between devices, on_device(): lax.ppermute(own, 'lat', [(s, s - d) for s in range(bands) if 0 <= s - d...  12.1 us
    pallas_call x1, Pallas kernels, on_device(): pl.pallas_call(functools.partial(prepare_kernel, members=members, fine_ro...  9.29 us
    ppermute x4, waiting for transfers between devices, on_device(): lax.ppermute(own, 'lat', [(s, s - d) for s in range(bands) if 0 <= s - d...  7.32 us
    all_to_all x2, starting transfers between devices, on_device(): hits = lax.all_to_all(got[0], ('mem', 'lat'), 0, 0, tiled=True)  5.94 us
  transfers between devices with their start and end apart: 9, of which 4 were waited for; matrix products, arithmetic and copies ran while one was open for 0% of the time, Pallas kernels for 13%

profile of v7, /device:TPU:0, one launch (start us, length us, event | category | flops | bytes accessed | tf_op | source)
XLA Modules:
  0.0 128.1 jit_solution(15874055811860981709)
XLA Ops:
  1.3 1.2 copy-done.2
  4.6 9.3 %prepare.1 = f32[24,2048]{1,0:T(8,128)S(1)} custom-call(s32[1]{0:T(128)S(6)} %copy.17.count_ref, bf16[256,2048]{1,0:T(8,128)(2,1)S(1)} %bitcast.23, s32[1,2048]{1,0:T(1,128)S(1)} %copy-done.7, f32[1,2048]{1,0:T(1,128)S(1)} %copy-done.5, f32[1,2048]{1,0:T(1,128)S(1)} %copy-done.6), custom_call_target="tpu_custom_call" | custom-call | flops 4000000000 | bytes 2000000 | tf_op jit(solution)/shard_map/prepare/pallas_call | solution.py:421
  13.9 5.0 %collective-permute-start = (f32[24,2048]{1,0:T(8,128)S(1)}, f32[24,2048]{1,0:T(8,128)S(1)}, u32[]{:S(2)}, u32[]{:S(2)}) collective-permute-start(f32[24,2048]{1,0:T(8,128)S(1)} %prepare.1), channel_id=1, source_target_pairs={{0,2},{1,3},{2,4},{3,5},{4,6},{5,7},{8,10},{9,11},{10,12},{11,13},... | collective-permute-start | bytes 589832 | tf_op jit(solution)/shard_map/ppermute | solution.py:437
  18.9 1.3 %collective-permute-start.3 = (f32[24,2048]{1,0:T(8,128)S(1)}, f32[24,2048]{1,0:T(8,128)S(1)}, u32[]{:S(2)}, u32[]{:S(2)}) collective-permute-start(f32[24,2048]{1,0:T(8,128)S(1)} %prepare.1), channel_id=1, source_target_pairs={{2,0},{3,1},{4,2},{5,3},{6,4},{7,5},{10,8},{11,9},{12,10},{13,11},... | collective-permute-start | bytes 589832 | tf_op jit(solution)/shard_map/ppermute | solution.py:437
  20.2 1.3 %collective-permute-start.2 = (f32[24,2048]{1,0:T(8,128)S(1)}, f32[24,2048]{1,0:T(8,128)S(1)}, u32[]{:S(2)}, u32[]{:S(2)}) collective-permute-start(f32[24,2048]{1,0:T(8,128)S(1)} %prepare.1), channel_id=1, source_target_pairs={{1,0},{2,1},{3,2},{4,3},{5,4},{6,5},{7,6},{9,8},{10,9},{11,10},{12... | collective-permute-start | bytes 589832 | tf_op jit(solution)/shard_map/ppermute | solution.py:437
  21.5 4.6 %collective-permute-start.1 = (f32[24,2048]{1,0:T(8,128)S(1)}, f32[24,2048]{1,0:T(8,128)S(1)}, u32[]{:S(2)}, u32[]{:S(2)}) collective-permute-start(f32[24,2048]{1,0:T(8,128)S(1)} %prepare.1), channel_id=1, source_target_pairs={{0,1},{1,2},{2,3},{3,4},{4,5},{5,6},{6,7},{8,9},{9,10},{10,11},{11... | collective-permute-start | bytes 589832 | tf_op jit(solution)/shard_map/ppermute | solution.py:437
  26.1 7.3 %collective-permute-done.1 = f32[24,2048]{1,0:T(8,128)S(1)} collective-permute-done((f32[24,2048]{1,0:T(8,128)S(1)}, f32[24,2048]{1,0:T(8,128)S(1)}, u32[]{:S(2)}, u32[]{:S(2)}) %collective-permute-start.1) | collective-permute-done | bytes 196640 | tf_op jit(solution)/shard_map/ppermute | solution.py:437
  33.6 1.0 copy-done.12
  34.9 8.3 %iterate.3 = (f32[32,24,128]{2,1,0:T(8,128)S(1)}, f32[128,1024]{1,0:T(8,128)S(1)}, f32[8,2048]{1,0:T(8,128)S(1)}) custom-call(s32[2]{0:T(128)S(1)} %pad_add_fusion.place_ref, s32[5,128]{1,0:T(8,128)S(1)} %bitcast.17, f32[5,24,2048]{2,1,0:T(8,128)S(1)} %bitcast_dynamic-update-slice_fusion.q_ref, f32[8,2,5,8,128]{4,3,2,1,0:T(8,128)S(1)} %copy-done.14, ...), custom_call_target="tpu_custom_call" | custom-call | flops 7000000000 | bytes 3000000 | tf_op jit(solution)/shard_map/iterate/pallas_call | solution.py:456
  44.1 20.0 %all_to_all.15.refs_1_ = f32[32,24,128]{2,1,0:T(8,128)S(1)} all-to-all(f32[32,24,128]{2,1,0:T(8,128)S(1)} %get-tuple-element.26), channel_id=1, replica_groups=mesh['mem'=4,'lat'=8] {'mem','lat'}, dimensions={0} | all-to-all | bytes 786432 | tf_op jit(solution)/shard_map/all_to_all | solution.py:475
  64.1 9.2 %iterate.4 = (f32[32,16,128]{2,1,0:T(8,128)}, f32[128,1024]{1,0:T(8,128)S(1)}, f32[8,2048]{1,0:T(8,128)S(1)}, f32[6,8,16,128]{3,2,1,0:T(8,128)S(1)}, f32[1,128]{1,0:T(1,128)S(1)}) custom-call(s32[2]{0:T(128)S(1)} %pad_add_fusion.place_ref, s32[5,128]{1,0:T(8,128)S(1)} %bitcast.18, f32[5,24,2048]{2,1,0:T(8,128)S(1)} %bitcast_dynamic-update-slice_fusion.q_ref, ...), custom_call_target="tpu_custom_call" | custom-call | flops 7000000000 | bytes 3000000 | tf_op jit(solution)/shard_map/iterate/pallas_call | solution.py:456
  74.8 2.8 %all-to-all-start.1 = ((f32[32,16,128]{2,1,0:T(8,128)}), f32[32,16,128]{2,1,0:T(8,128)S(1)}, u32[]{:S(2)}, u32[]{:S(2)}) async-start(f32[32,16,128]{2,1,0:T(8,128)} %get-tuple-element.28), calls=%async_computation.1 | async-start | bytes 524288 | tf_op jit(solution)/shard_map/all_to_all | solution.py:475
  77.6 1.0 copy-done.9
  78.7 1.0 copy-done.23
  79.7 5.7 %side.3 = (f32[128,1024]{1,0:T(8,128)S(1)}, f32[4,16,512]{2,1,0:T(8,128)S(1)}) custom-call(s32[2]{0:T(128)S(1)} %pad_add_fusion.place_ref, s32[5,128]{1,0:T(8,128)S(1)} %bitcast.19, f32[8,2048]{1,0:T(8,128)S(1)} %get-tuple-element.33.vrow_ref, f32[5,24,2048]{2,1,0:T(8,128)S(1)} %bitcast_dynamic-update-slice_fusion.q_ref, ...), custom_call_target="tpu_custom_call" | custom-call | flops 4000000000 | bytes 6000000 | tf_op jit(solution)/shard_map/side/pallas_call | solution.py:486
  85.5 2.4 %all-to-all-done.1.refs_1_ = f32[32,16,128]{2,1,0:T(8,128)S(1)} async-done(((f32[32,16,128]{2,1,0:T(8,128)}), f32[32,16,128]{2,1,0:T(8,128)S(1)}, u32[]{:S(2)}, u32[]{:S(2)}) %all-to-all-start.1) | async-done | bytes 262176 | tf_op jit(solution)/shard_map/all_to_all | solution.py:475
  87.9 1.0 copy-done.13
  88.9 1.0 copy-done.15
  89.9 1.0 copy-done.25
  90.9 9.0 %iterate.5 = (f32[32,16,128]{2,1,0:T(8,128)}, f32[128,1024]{1,0:T(8,128)S(1)}, f32[8,2048]{1,0:T(8,128)S(1)}, f32[6,8,16,128]{3,2,1,0:T(8,128)S(1)}, f32[1,128]{1,0:T(1,128)S(1)}) custom-call(s32[2]{0:T(128)S(1)} %pad_add_fusion.place_ref, s32[5,128]{1,0:T(8,128)S(1)} %bitcast.20, f32[5,24,2048]{2,1,0:T(8,128)S(1)} %bitcast_dynamic-update-slice_fusion.q_ref, ...), custom_call_target="tpu_custom_call" | custom-call | flops 7000000000 | bytes 3000000 | tf_op jit(solution)/shard_map/iterate/pallas_call | solution.py:456
  99.9 0.8 copy-done.20
  101.3 3.2 %all-to-all-start.2 = ((f32[32,16,128]{2,1,0:T(8,128)}), f32[32,16,128]{2,1,0:T(8,128)S(1)}, u32[]{:S(2)}, u32[]{:S(2)}) async-start(f32[32,16,128]{2,1,0:T(8,128)} %get-tuple-element.30), calls=%async_computation.2 | async-start | bytes 524288 | tf_op jit(solution)/shard_map/all_to_all | solution.py:475
  104.5 1.2 copy-done.4
  105.7 1.0 copy-done.16
  106.7 1.0 copy-done.19
  107.7 5.7 %side.4 = (f32[128,1024]{1,0:T(8,128)S(1)}, f32[4,16,512]{2,1,0:T(8,128)S(1)}) custom-call(s32[2]{0:T(128)S(1)} %pad_add_fusion.place_ref, s32[5,128]{1,0:T(8,128)S(1)} %bitcast.21, f32[8,2048]{1,0:T(8,128)S(1)} %get-tuple-element.36.vrow_ref, f32[5,24,2048]{2,1,0:T(8,128)S(1)} %bitcast_dynamic-update-slice_fusion.q_ref, ...), custom_call_target="tpu_custom_call" | custom-call | flops 4000000000 | bytes 6000000 | tf_op jit(solution)/shard_map/side/pallas_call | solution.py:486
  113.6 1.2 copy-done.1
  114.7 5.8 %side.5 = (f32[128,1024]{1,0:T(8,128)S(1)}, f32[4,16,512]{2,1,0:T(8,128)S(1)}) custom-call(s32[2]{0:T(128)S(1)} %pad_add_fusion.place_ref, s32[5,128]{1,0:T(8,128)S(1)} %bitcast.22, f32[8,2048]{1,0:T(8,128)S(1)} %copy-done.27, f32[5,24,2048]{2,1,0:T(8,128)S(1)} %copy-done.1, f32[8,2,5,8,128]{4,3,2,1,0:T(8,128)S(1)} %copy-done.17, ...), custom_call_target="tpu_custom_call" | custom-call | flops 4000000000 | bytes 6000000 | tf_op jit(solution)/shard_map/side/pallas_call | solution.py:486
  120.5 1.6 %combine.1 = (f32[128,1024]{1,0:T(8,128)}, f32[16,512]{1,0:T(8,128)S(1)}, f32[16,512]{1,0:T(8,128)S(1)}, f32[16,512]{1,0:T(8,128)S(1)}, f32[16,512]{1,0:T(8,128)S(1)}) custom-call(s32[2]{0:T(128)S(1)} %pad_add_fusion.place_ref, f32[6,8,16,128]{3,2,1,0:T(8,128)S(1)} %get-tuple-element.29.state_ref, f32[32,16,128]{2,1,0:T(8,128)S(1)} %all-to-all-done.2.in_ref, ...), custom_call_target="tpu_custom_call" | custom-call | flops 10000000 | bytes 4000000 | tf_op jit(solution)/shard_map/combine/pallas_call | solution.py:489
  122.4 1.6 %collective-permute-start.5 = (f32[16,512]{1,0:T(8,128)S(1)}, f32[16,512]{1,0:T(8,128)S(1)}, u32[]{:S(2)}, u32[]{:S(2)}) collective-permute-start(f32[16,512]{1,0:T(8,128)S(1)} %get-tuple-element.48), channel_id=1, source_target_pairs={{0,16},{8,24},{16,0},{24,8},{1,17},{9,25},{17,1},{25,9},{2,18},{10... | collective-permute-start | bytes 98312 | tf_op jit(solution)/shard_map/ppermute | solution.py:500
  124.0 2.3 %collective-permute-done.5 = f32[16,512]{1,0:T(8,128)S(1)} collective-permute-done((f32[16,512]{1,0:T(8,128)S(1)}, f32[16,512]{1,0:T(8,128)S(1)}, u32[]{:S(2)}, u32[]{:S(2)}) %collective-permute-start.5) | collective-permute-done | bytes 32800 | tf_op jit(solution)/shard_map/ppermute | solution.py:500
  126.3 1.1 collective-permute-done.6
  (60 shorter events, 6.5 us)
Async XLA Ops:
  1.3 1.2 copy-start.2
  13.9 12.2 %collective-permute-start = (f32[24,2048]{1,0:T(8,128)S(1)}, f32[24,2048]{1,0:T(8,128)S(1)}, u32[]{:S(2)}, u32[]{:S(2)}) collective-permute-start(f32[24,2048]{1,0:T(8,128)S(1)} %prepare.1), channel_id=1, source_target_pairs={{0,2},{1,3},{2,4},{3,5},{4,6},{5,7},{8,10},{9,11},{10,12},{11,13},... | collective-permute-start | bytes 589832 | tf_op jit(solution)/shard_map/ppermute | solution.py:437
  18.9 14.7 %collective-permute-start.3 = (f32[24,2048]{1,0:T(8,128)S(1)}, f32[24,2048]{1,0:T(8,128)S(1)}, u32[]{:S(2)}, u32[]{:S(2)}) collective-permute-start(f32[24,2048]{1,0:T(8,128)S(1)} %prepare.1), channel_id=1, source_target_pairs={{2,0},{3,1},{4,2},{5,3},{6,4},{7,5},{10,8},{11,9},{12,10},{13,11},... | collective-permute-start | bytes 589832 | tf_op jit(solution)/shard_map/ppermute | solution.py:437
  20.2 13.4 %collective-permute-start.2 = (f32[24,2048]{1,0:T(8,128)S(1)}, f32[24,2048]{1,0:T(8,128)S(1)}, u32[]{:S(2)}, u32[]{:S(2)}) collective-permute-start(f32[24,2048]{1,0:T(8,128)S(1)} %prepare.1), channel_id=1, source_target_pairs={{1,0},{2,1},{3,2},{4,3},{5,4},{6,5},{7,6},{9,8},{10,9},{11,10},{12... | collective-permute-start | bytes 589832 | tf_op jit(solution)/shard_map/ppermute | solution.py:437
  21.5 12.0 %collective-permute-start.1 = (f32[24,2048]{1,0:T(8,128)S(1)}, f32[24,2048]{1,0:T(8,128)S(1)}, u32[]{:S(2)}, u32[]{:S(2)}) collective-permute-start(f32[24,2048]{1,0:T(8,128)S(1)} %prepare.1), channel_id=1, source_target_pairs={{0,1},{1,2},{2,3},{3,4},{4,5},{5,6},{6,7},{8,9},{9,10},{10,11},{11... | collective-permute-start | bytes 589832 | tf_op jit(solution)/shard_map/ppermute | solution.py:437
  33.5 1.1 copy-start.12
  33.5 1.4 %copy-start.14 = (f32[8,2,5,8,128]{4,3,2,1,0:T(8,128)S(1)}, f32[8,2,5,8,128]{4,3,2,1,0:T(8,128)}, u32[]{:S(2)}) copy-start(f32[8,2,5,8,128]{4,3,2,1,0:T(8,128)} %constant.16.clone.tab_ref) | copy-start | bytes 983044
  33.6 70.9 %copy-start = (f32[5,24,2048]{2,1,0:T(8,128)}, f32[5,24,2048]{2,1,0:T(8,128)S(1)}, u32[]{:S(2)}) copy-start(f32[5,24,2048]{2,1,0:T(8,128)S(1)} %bitcast_dynamic-update-slice_fusion.q_ref) | copy-start | bytes 2949124
  43.3 0.8 copy-start.22
  44.1 20.0 %copy-start.8 = (s32[1,2048]{1,0:T(1,128)S(1)}, s32[1,2048]{1,0:T(1,128)}, u32[]{:S(2)}) copy-start(s32[1,2048]{1,0:T(1,128)} %refs_0_.1) | copy-start | bytes 24580
  64.1 13.5 %copy-start.3 = (bf16[16,16,2048]{2,1,0:T(8,128)(2,1)S(1)}, bf16[16,16,2048]{2,1,0:T(8,128)(2,1)}, u32[]{:S(2)}) copy-start(bf16[16,16,2048]{2,1,0:T(8,128)(2,1)} %param.8) | copy-start | bytes 3145732
  73.3 0.8 copy-start.18
  74.8 13.1 %all-to-all-start.1 = ((f32[32,16,128]{2,1,0:T(8,128)}), f32[32,16,128]{2,1,0:T(8,128)S(1)}, u32[]{:S(2)}, u32[]{:S(2)}) async-start(f32[32,16,128]{2,1,0:T(8,128)} %get-tuple-element.28), calls=%async_computation.1 | async-start | bytes 524288 | tf_op jit(solution)/shard_map/all_to_all | solution.py:475
  77.6 1.0 copy-start.9
  78.7 1.0 copy-start.23
  87.9 1.0 copy-start.13
  88.9 1.0 copy-start.15
  89.9 1.0 copy-start.25
  99.9 0.8 copy-start.20
  100.7 3.8 %copy-start.10 = (bf16[2,512,256]{2,1,0:T(8,128)(2,1)S(1)}, bf16[2,512,256]{2,1,0:T(8,128)(2,1)}, u32[]{:S(2)}) copy-start(bf16[2,512,256]{2,1,0:T(8,128)(2,1)} %constant.34.t1_ref) | copy-start | bytes 1572868
  101.3 19.2 %all-to-all-start.2 = ((f32[32,16,128]{2,1,0:T(8,128)}), f32[32,16,128]{2,1,0:T(8,128)S(1)}, u32[]{:S(2)}, u32[]{:S(2)}) async-start(f32[32,16,128]{2,1,0:T(8,128)} %get-tuple-element.30), calls=%async_computation.2 | async-start | bytes 524288 | tf_op jit(solution)/shard_map/all_to_all | solution.py:475
  104.5 1.2 copy-start.4
  105.7 1.0 copy-start.16
  106.7 1.0 copy-start.19
  107.7 5.8 %copy-start.11 = (bf16[2,512,256]{2,1,0:T(8,128)(2,1)S(1)}, bf16[2,512,256]{2,1,0:T(8,128)(2,1)}, u32[]{:S(2)}) copy-start(bf16[2,512,256]{2,1,0:T(8,128)(2,1)} %constant.34.t1_ref) | copy-start | bytes 1572868
  107.7 5.8 %copy-start.17 = (f32[8,2,5,8,128]{4,3,2,1,0:T(8,128)S(1)}, f32[8,2,5,8,128]{4,3,2,1,0:T(8,128)}, u32[]{:S(2)}) copy-start(f32[8,2,5,8,128]{4,3,2,1,0:T(8,128)} %constant.16.clone.tab_ref) | copy-start | bytes 983044
  107.7 5.8 %copy-start.21 = (f32[128,1024]{1,0:T(8,128)S(1)}, f32[128,1024]{1,0:T(8,128)}, u32[]{:S(2)}) copy-start(f32[128,1024]{1,0:T(8,128)} %copy-done.20) | copy-start | bytes 1572868
  107.7 5.8 %copy-start.27 = (f32[8,2048]{1,0:T(8,128)S(1)}, f32[8,2048]{1,0:T(8,128)}, u32[]{:S(2)}) copy-start(f32[8,2048]{1,0:T(8,128)} %copy-done.26) | copy-start | bytes 196612
  113.5 1.2 copy-start.1
  122.2 1.9 %collective-permute-start.4 = (f32[16,512]{1,0:T(8,128)S(1)}, f32[16,512]{1,0:T(8,128)S(1)}, u32[]{:S(2)}, u32[]{:S(2)}) collective-permute-start(f32[16,512]{1,0:T(8,128)S(1)} %get-tuple-element.47), channel_id=1, source_target_pairs={{0,8},{8,0},{16,24},{24,16},{1,9},{9,1},{17,25},{25,17},{2,10},{10... | collective-permute-start | bytes 98312 | tf_op jit(solution)/shard_map/ppermute | solution.py:500
  122.4 3.9 %collective-permute-start.5 = (f32[16,512]{1,0:T(8,128)S(1)}, f32[16,512]{1,0:T(8,128)S(1)}, u32[]{:S(2)}, u32[]{:S(2)}) collective-permute-start(f32[16,512]{1,0:T(8,128)S(1)} %get-tuple-element.48), channel_id=1, source_target_pairs={{0,16},{8,24},{16,0},{24,8},{1,17},{9,25},{17,1},{25,9},{2,18},{10... | collective-permute-start | bytes 98312 | tf_op jit(solution)/shard_map/ppermute | solution.py:500
  124.0 3.4 %collective-permute-start.6 = (f32[16,512]{1,0:T(8,128)S(1)}, f32[16,512]{1,0:T(8,128)S(1)}, u32[]{:S(2)}, u32[]{:S(2)}) collective-permute-start(f32[16,512]{1,0:T(8,128)S(1)} %get-tuple-element.49), channel_id=1, source_target_pairs={{0,24},{8,16},{16,8},{24,0},{1,25},{9,17},{17,9},{25,1},{2,26},{10... | collective-permute-start | bytes 98312 | tf_op jit(solution)/shard_map/ppermute | solution.py:500
  (5 other events, 3.5 us)

commit v8 on v7

--- a/solution.py
+++ b/solution.py
@@ -90,7 +90,15 @@
     return jnp.sum(jnp.where(mask, 1.0, 0.0)).astype(jnp.int32)
 
 
-def prepare_kernel(count_ref, p_ref, cell_ref, innovation_ref, scale_ref, out_ref, key_ref, kcol_ref, srt_ref, *, members, fine_rows):
+def fetch(*copies):
+    started = [pltpu.make_async_copy(*copy) for copy in copies]
+    for copy in started:
+        copy.start()
+    return started
+
+
+def prepare_kernel(count_ref, far_ref, cell_ref, innovation_ref, scale_ref, out_ref, key_ref, kcol_ref, srt_ref, p_ref, sem, *, members, fine_rows):
+    ready = fetch((far_ref, p_ref, sem.at[0]))
     lon = p_ref.shape[1]
     slots = cell_ref.shape[1]
     cell = cell_ref[...].astype(jnp.float32)
@@ -159,6 +167,7 @@
         srt_ref[0:members, at] = srt_ref[0:members, at] + jnp.sum(got * mask[None], axis=1)
 
     starts = [s // 128 * 128 for s in edges[:-1]]
+    ready[0].wait()
     for c, start in enumerate(starts):
         window(c, start)
     for c, start in enumerate(starts):
@@ -190,7 +199,7 @@
     lax.fori_loop(0, blocks + 1, block, 0)
 
 
-def scatter(bound_ref, q_ref, tab, v_of, first, last, lhs_ref, at_ref, x_ref, members, coarse_rows):
+def scatter(bound_ref, q_ref, tab, v_of, first, last, lhs_ref, at_ref, x_ref, members, coarse_rows, short=False):
     slots = q_ref.shape[2]
     half = members * coarse_rows
     blocks = x_ref.shape[1] // BLK - 1
@@ -228,8 +237,11 @@
             for c in range(blocks):
                 one(c, window(bound_ref, d, c)[0], size)
 
-        pl.when(longest <= SMALL)(lambda: run(SMALL))
-        pl.when(longest > SMALL)(lambda: run(WINDOW))
+        if short:
+            pl.when(longest <= SMALL)(lambda: run(SMALL))
+            pl.when(longest > SMALL)(lambda: run(WINDOW))
+        else:
+            run(WINDOW)
         rest(bound_ref, d, blocks, WINDOW, one)
         return 0
 
@@ -270,17 +282,24 @@
             rows_ref[d : d + 1, i * 128 : (i + 1) * 128] = tile[i : i + 1, :]
 
 
-def iter_kernel(place_ref, bound_ref, q_ref, tab_ref, t2_ref, *refs, members, coarse_rows, scale2, order, bands, groups):
+def iter_kernel(place_ref, bound_ref, q_far, tab_far, t2_far, *refs, members, coarse_rows, scale2, order, bands, groups):
+    q_ref, tab_ref, t2_ref, b_ref, sem = refs[-5:]
+    refs = refs[:-5]
     slots = q_ref.shape[2]
+    ready = fetch((q_far, q_ref, sem.at[0]), (tab_far.at[place_ref[1], 0], tab_ref, sem.at[1]), (t2_far, t2_ref, sem.at[2]))
     tiles = slots // 128
     share = tiles // groups
     band = place_ref[1]
     if order == 0:
-        out_ref, b_ref, vrow_ref, lhs_ref, at_ref, x_ref, rows_ref, bhl_ref, own_ref, part_ref = refs
+        out_ref, b_far, vrow_ref, lhs_ref, at_ref, x_ref, rows_ref, bhl_ref, own_ref, part_ref = refs
+        ready[0].wait()
         for d in range(NREL):
             vrow_ref[d : d + 1, :] = pull_of(q_ref[d, members + 2 : members + 3, :], q_ref[d, members + 3 : members + 4, :])[0]
     else:
-        old_ref, in_ref, out_ref, b_ref, vrow_ref, state_ref, step_ref, lhs_ref, at_ref, x_ref, rows_ref, bhl_ref, own_ref, part_ref, hits_ref = refs
+        old_far, in_ref, out_ref, b_far, vrow_ref, state_far, step_ref = refs[:7]
+        lhs_ref, at_ref, x_ref, rows_ref, bhl_ref, own_ref, part_ref, hits_ref, old_ref, state_ref = refs[7:]
+        if order == 2:
+            ready += fetch((old_far, old_ref, sem.at[3]))
         pltpu.sync_copy(in_ref, hits_ref)
         hits = sum_mem(hits_ref[:, :tiles, :], bands)
         if order == 1:
@@ -292,6 +311,7 @@
             v, w = pull_of(state_ref[0], state_ref[1])
             observed, lam = 0.0, 0.0
         else:
+            ready[3].wait()
             state_ref[0:2] = old_ref[0:2]
             v, w, observed, lam = old_ref[2], old_ref[3], old_ref[4], old_ref[5]
         step = step_of(hits, v, w)
@@ -304,7 +324,9 @@
         state_ref[3] = weight
         state_ref[4] = observed
         state_ref[5] = lam
+        saved = fetch((state_ref, state_far, sem.at[4]))
         lay_rows(vrow_ref, lambda b: state_ref[2, b], (band, bands))
+        ready[0].wait()
 
     def v_of(d):
         return vrow_ref[pl.ds(d, 1), :]
@@ -312,9 +334,12 @@
     half = members * coarse_rows
     blocks = x_ref.shape[1] // BLK - 1
     cols = blocks * BLK
-    scatter(bound_ref, q_ref, lambda d: tab_ref[band, 0, d], v_of, 0, NREL, lhs_ref, at_ref, x_ref, members, coarse_rows)
+    ready[1].wait()
+    scatter(bound_ref, q_ref, lambda d: tab_ref[d], v_of, 0, NREL, lhs_ref, at_ref, x_ref, members, coarse_rows, True)
+    ready[2].wait()
     b = lon_filter(x_ref[:, :cols], t2_ref)
     b_ref[...] = b
+    b_saved = fetch((b_ref, b_far, sem.at[5]))
     hi, lo = split(b)
     bhl_ref[:half, :cols] = hi
     bhl_ref[half:, :cols] = lo
@@ -350,17 +375,29 @@
                 part_ref[0, to : to + 1, :] = row[:, i * 128 : (i + 1) * 128]
     part_ref[1:] = jnp.broadcast_to(part_ref[0][None], (part_ref.shape[0] - 1,) + part_ref.shape[1:])
     pltpu.sync_copy(part_ref, out_ref)
+    b_saved[0].wait()
+    if order:
+        saved[0].wait()
 
 
 def side_kernel(
-    place_ref, bound_ref, vrow_ref, q_ref, tab_ref, t1_ref, b_ref, p_ref, control_ref, image_ref, lhs_ref, at_ref, x_ref,
-    *, members, fine_rows, coarse_rows, scale,
+    place_ref, bound_ref, vrow_ref, q_far, tab_far, t1_far, b_far, p_far, control_ref, image_ref, lhs_ref, at_ref, x_ref,
+    q_ref, tab_ref, t1_ref, b_ref, p_ref, sem, *, members, fine_rows, coarse_rows, scale,
 ):
     def v_of(d):
         return vrow_ref[pl.ds(d, 1), :]
 
-    tab = lambda d: tab_ref[place_ref[1], 1, d]
+    near = pl.ds(REACH - 1, 3)
+    ready = fetch(
+        (q_far.at[near], q_ref.at[near], sem.at[0]), (tab_far.at[place_ref[1], 1], tab_ref, sem.at[1]), (t1_far, t1_ref, sem.at[2]),
+        (b_far, b_ref, sem.at[3]), (p_far, p_ref, sem.at[4]),
+    )
+    ready[0].wait()
+    ready[1].wait()
+    tab = lambda d: tab_ref[d]
     scatter(bound_ref, q_ref, tab, v_of, REACH - 1, REACH + 2, lhs_ref, at_ref, x_ref, members, coarse_rows)
+    for copy in ready[2:]:
+        copy.wait()
     control_ref[...] = scale * lon_filter(x_ref[:, : b_ref.shape[1]], t1_ref)
 
     b = b_ref[...]
@@ -414,6 +451,7 @@
     smem = pl.BlockSpec(memory_space=pltpu.SMEM)
     vmem = pl.BlockSpec(memory_space=pltpu.VMEM)
     anywhere = pl.BlockSpec(memory_space=pl.ANY)
+    far = pl.BlockSpec(memory_space=pltpu.HBM)
     params = pltpu.CompilerParams(vmem_limit_bytes=VMEM_LIMIT)
     f32 = functools.partial(jax.ShapeDtypeStruct, dtype=jnp.float32)
 
@@ -421,15 +459,16 @@
     own = pl.pallas_call(
         functools.partial(prepare_kernel, members=members, fine_rows=fine_rows),
         out_shape=f32((members + META, slots)),
-        in_specs=[smem] + [vmem] * 4,
+        in_specs=[smem, far] + [vmem] * 3,
         out_specs=vmem,
         scratch_shapes=[
             pltpu.VMEM((8, slots), jnp.float32),
             pltpu.VMEM((slots, 128), jnp.float32),
             pltpu.VMEM((members + META, slots + 512), jnp.float32),
+            pltpu.VMEM(field.shape, field.dtype),
+            pltpu.SemaphoreType.DMA((1,)),
         ],
         cost_estimate=pl.CostEstimate(flops=4 * 10**9, bytes_accessed=2 * 10**6, transcendentals=0),
-        compiler_params=params,
         name="prepare",
     )(obs_count, field, obs_cells, innovation, obs_scale)
     near = []
@@ -458,15 +497,16 @@
                 iter_kernel, members=members, coarse_rows=coarse_rows, scale2=scale * scale, order=order, bands=bands, groups=groups
             ),
             out_shape=outs,
-            in_specs=[smem] * 2 + [vmem] * 3 + ([vmem, anywhere] if iteration else []),
-            out_specs=[anywhere] + [vmem] * (len(outs) - 1),
+            in_specs=[smem] * 2 + [far] * 3 + ([far, anywhere] if iteration else []),
+            out_specs=[anywhere, far, vmem] + ([far, vmem] if iteration else []),
             scratch_shapes=scratch
             + [pltpu.VMEM((8, padded), jnp.float32)]
             + [pltpu.VMEM((2 * half, coarse_cols + BLK), jnp.bfloat16), pltpu.VMEM((members + META, padded), jnp.float32)]
             + [pltpu.VMEM(block, jnp.float32)]
-            + ([pltpu.VMEM(hits.shape, jnp.float32)] if iteration else []),
+            + ([pltpu.VMEM(hits.shape, jnp.float32)] + [pltpu.VMEM((6, bands, tiles, 128), jnp.float32)] * 2 if iteration else [])
+            + [pltpu.VMEM(near.shape, jnp.float32), pltpu.VMEM(tables.shape[2:], jnp.float32), pltpu.VMEM(t2.shape, t2.dtype)]
+            + [pltpu.VMEM((half, coarse_cols), jnp.float32), pltpu.SemaphoreType.DMA((6,))],
             cost_estimate=pl.CostEstimate(flops=7 * 10**9, bytes_accessed=3 * 10**6, transcendentals=0),
-            compiler_params=params,
             name="iterate",
         )(*ins)
         if iteration:
@@ -476,11 +516,12 @@
         side = pl.pallas_call(
             functools.partial(side_kernel, members=members, fine_rows=fine_rows, coarse_rows=coarse_rows, scale=scale),
             out_shape=[f32((half, coarse_cols)), f32((groups, fine_rows, width))],
-            in_specs=[smem] * 2 + [vmem] * 6,
+            in_specs=[smem] * 2 + [vmem] + [far] * 5,
             out_specs=[vmem] * 2,
-            scratch_shapes=scratch,
+            scratch_shapes=scratch
+            + [pltpu.VMEM(near.shape, jnp.float32), pltpu.VMEM(tables.shape[2:], jnp.float32), pltpu.VMEM(t1.shape, t1.dtype)]
+            + [pltpu.VMEM((half, coarse_cols), jnp.float32), pltpu.VMEM(field.shape, field.dtype), pltpu.SemaphoreType.DMA((5,))],
             cost_estimate=pl.CostEstimate(flops=4 * 10**9, bytes_accessed=6 * 10**6, transcendentals=0),
-            compiler_params=params,
             name="side",
         )
         control, image = side(place, bound, got[2], near, tables, t1, got[1], field)

time: 129 us -> 131 us (1.016)
  Pallas kernels: 54.7 us -> 69.7 us
  local copies, waits for them, and re-layouts: 18 us -> 4.32 us
    unnamed x61 -> x31, local copies, waits for them, and re-layouts: 18 us -> 4.3 us
    pallas_call x3, Pallas kernels: 26.5 us -> 33.8 us  [on_device(): pl.pallas_call(functools.partial(iter_kernel, members=members, coarse_row...]
    pallas_call x3, Pallas kernels: 17.2 us -> 23.5 us  [on_device(): control, image = side(place, bound, got[2], near, tables, t1, got[1], field)]
    pallas_call x1, Pallas kernels: 9.29 us -> 10.8 us  [on_device(): pl.pallas_call(functools.partial(prepare_kernel, members=members, fine_ro...]
  transfers between devices with their start and end apart: 9 -> 9, of which waited for: 4 -> 4; matrix products, arithmetic and copies ran while one was open for 0% -> 0% of each run, Pallas kernels for 13% -> 18%
where the time goes in v8:
time: 131 us; the launch traced here: 130 us
  Pallas kernels  69.7 us (53%)
  blocking collectives  20.2 us (15%)
  starting transfers between devices  19.9 us (15%)
  waiting for transfers between devices  13 us (10%)
  local copies, waits for them, and re-layouts  4.32 us (3%)
  between operations  1.58 us (1%)
    pallas_call x3, Pallas kernels, on_device(): pl.pallas_call(functools.partial(iter_kernel, members=members, coarse_row...  33.8 us
    pallas_call x3, Pallas kernels, on_device(): control, image = side(place, bound, got[2], near, tables, t1, got[1], field)  23.5 us
    all_to_all x1, blocking collectives, on_device(): hits = lax.all_to_all(got[0], ('mem', 'lat'), 0, 0, tiled=True)  20.2 us
    ppermute x4, starting transfers between devices, on_device(): lax.ppermute(own, 'lat', [(s, s - d) for s in range(bands) if 0 <= s - d...  12.1 us
    pallas_call x1, Pallas kernels, on_device(): pl.pallas_call(functools.partial(prepare_kernel, members=members, fine_ro...  10.8 us
    ppermute x4, waiting for transfers between devices, on_device(): lax.ppermute(own, 'lat', [(s, s - d) for s in range(bands) if 0 <= s - d...  7.13 us
    all_to_all x2, starting transfers between devices, on_device(): hits = lax.all_to_all(got[0], ('mem', 'lat'), 0, 0, tiled=True)  5.87 us
    unnamed x31, local copies, waits for them, and re-layouts  4.3 us
  transfers between devices with their start and end apart: 9, of which 4 were waited for; matrix products, arithmetic and copies ran while one was open for 0% of the time, Pallas kernels for 18%

profile of v8, /device:TPU:0, one launch (start us, length us, event | category | flops | bytes accessed | tf_op | source)
XLA Modules:
  0.0 129.9 jit_solution(4934253957516955866)
XLA Ops:
  1.3 10.8 %prepare.1 = f32[24,2048]{1,0:T(8,128)} custom-call(s32[1]{0:T(128)S(6)} %copy.17.count_ref, bf16[256,2048]{1,0:T(8,128)(2,1)} %bitcast.23, s32[1,2048]{1,0:T(1,128)} %refs_0_.1, f32[1,2048]{1,0:T(1,128)} %innovation_ref.1, f32[1,2048]{1,0:T(1,128)} %scale_ref.1), custom_call_target="tpu_custom_call" | custom-call | flops 4000000000 | bytes 2000000 | tf_op jit(solution)/shard_map/prepare/pallas_call | solution.py:459
  12.0 5.0 %collective-permute-start = (f32[24,2048]{1,0:T(8,128)}, f32[24,2048]{1,0:T(8,128)S(1)}, u32[]{:S(2)}, u32[]{:S(2)}) collective-permute-start(f32[24,2048]{1,0:T(8,128)} %prepare.1), channel_id=1, source_target_pairs={{0,2},{1,3},{2,4},{3,5},{4,6},{5,7},{8,10},{9,11},{10,12},{11,13},... | collective-permute-start | bytes 589832 | tf_op jit(solution)/shard_map/ppermute | solution.py:476
  17.0 1.3 collective-permute-start.3
  18.3 1.3 collective-permute-start.2
  19.6 4.6 %collective-permute-start.1 = (f32[24,2048]{1,0:T(8,128)}, f32[24,2048]{1,0:T(8,128)S(1)}, u32[]{:S(2)}, u32[]{:S(2)}) collective-permute-start(f32[24,2048]{1,0:T(8,128)} %prepare.1), channel_id=1, source_target_pairs={{0,1},{1,2},{2,3},{3,4},{4,5},{5,6},{6,7},{8,9},{9,10},{10,11},{11... | collective-permute-start | bytes 589832 | tf_op jit(solution)/shard_map/ppermute | solution.py:476
  24.2 0.6 pad_add_fusion.place_ref
  24.8 0.0 copy-start.11
  24.8 7.1 %collective-permute-done.1 = f32[24,2048]{1,0:T(8,128)S(1)} collective-permute-done((f32[24,2048]{1,0:T(8,128)}, f32[24,2048]{1,0:T(8,128)S(1)}, u32[]{:S(2)}, u32[]{:S(2)}) %collective-permute-start.1) | collective-permute-done | bytes 196640 | tf_op jit(solution)/shard_map/ppermute | solution.py:476
  32.1 0.7 copy.12
  32.7 0.3 copy-done.12
  33.0 10.9 %iterate.3 = (f32[32,24,128]{2,1,0:T(8,128)}, f32[128,1024]{1,0:T(8,128)}, f32[8,2048]{1,0:T(8,128)}) custom-call(s32[2]{0:T(128)} %pad_add_fusion.place_ref, s32[5,128]{1,0:T(8,128)} %bitcast.17, f32[5,24,2048]{2,1,0:T(8,128)} %copy-done.12, f32[8,2,5,8,128]{4,3,2,1,0:T(8,128)} %constant.16.clone.tab_far, bf16[2,512,256]{2,1,0:T(8,128)(2,1)} %constant.27.t2_far), custom_call_target="tpu_custom_call" | custom-call | flops 7000000000 | bytes 3000000 | tf_op jit(solution)/shard_map/iterate/pallas_call | solution.py:495
  44.0 20.2 %all_to_all.15.refs_1_ = f32[32,24,128]{2,1,0:T(8,128)} all-to-all(f32[32,24,128]{2,1,0:T(8,128)} %get-tuple-element.26), channel_id=1, replica_groups=mesh['mem'=4,'lat'=8] {'mem','lat'}, dimensions={0} | all-to-all | bytes 786432 | tf_op jit(solution)/shard_map/all_to_all | solution.py:515
  64.2 11.4 %iterate.4 = (f32[32,16,128]{2,1,0:T(8,128)}, f32[128,1024]{1,0:T(8,128)}, f32[8,2048]{1,0:T(8,128)}, f32[6,8,16,128]{3,2,1,0:T(8,128)}, f32[1,128]{1,0:T(1,128)}) custom-call(s32[2]{0:T(128)} %pad_add_fusion.place_ref, s32[5,128]{1,0:T(8,128)} %bitcast.18, f32[5,24,2048]{2,1,0:T(8,128)} %copy-done.12, f32[8,2,5,8,128]{4,3,2,1,0:T(8,128)} %constant.16.clone.tab_far, ...), custom_call_target="tpu_custom_call" | custom-call | flops 7000000000 | bytes 3000000 | tf_op jit(solution)/shard_map/iterate/pallas_call | solution.py:495
  75.6 2.8 %all-to-all-start.1 = ((f32[32,16,128]{2,1,0:T(8,128)}), f32[32,16,128]{2,1,0:T(8,128)S(1)}, u32[]{:S(2)}, u32[]{:S(2)}) async-start(f32[32,16,128]{2,1,0:T(8,128)} %get-tuple-element.28), calls=%async_computation.1 | async-start | bytes 524288 | tf_op jit(solution)/shard_map/all_to_all | solution.py:515
  78.4 7.8 %side.3 = (f32[128,1024]{1,0:T(8,128)}, f32[4,16,512]{2,1,0:T(8,128)}) custom-call(s32[2]{0:T(128)} %pad_add_fusion.place_ref, s32[5,128]{1,0:T(8,128)} %bitcast.19, f32[8,2048]{1,0:T(8,128)} %get-tuple-element.33.vrow_ref, f32[5,24,2048]{2,1,0:T(8,128)} %copy-done.12, f32[8,2,5,8,128]{4,3,2,1,0:T(8,128)} %constant.16.clone.tab_far, ...), custom_call_target="tpu_custom_call" | custom-call | flops 4000000000 | bytes 6000000 | tf_op jit(solution)/shard_map/side/pallas_call | solution.py:527
  86.2 2.5 %all-to-all-done.1.refs_1_ = f32[32,16,128]{2,1,0:T(8,128)S(1)} async-done(((f32[32,16,128]{2,1,0:T(8,128)}), f32[32,16,128]{2,1,0:T(8,128)S(1)}, u32[]{:S(2)}, u32[]{:S(2)}) %all-to-all-start.1) | async-done | bytes 262176 | tf_op jit(solution)/shard_map/all_to_all | solution.py:515
  88.7 0.7 copy-done.10
  89.4 11.4 %iterate.5 = (f32[32,16,128]{2,1,0:T(8,128)}, f32[128,1024]{1,0:T(8,128)}, f32[8,2048]{1,0:T(8,128)}, f32[6,8,16,128]{3,2,1,0:T(8,128)}, f32[1,128]{1,0:T(1,128)}) custom-call(s32[2]{0:T(128)} %pad_add_fusion.place_ref, s32[5,128]{1,0:T(8,128)} %bitcast.20, f32[5,24,2048]{2,1,0:T(8,128)} %copy-done.12, f32[8,2,5,8,128]{4,3,2,1,0:T(8,128)} %constant.16.clone.tab_far, ...), custom_call_target="tpu_custom_call" | custom-call | flops 7000000000 | bytes 3000000 | tf_op jit(solution)/shard_map/iterate/pallas_call | solution.py:495
  100.8 3.1 %all-to-all-start.2 = ((f32[32,16,128]{2,1,0:T(8,128)}), f32[32,16,128]{2,1,0:T(8,128)S(1)}, u32[]{:S(2)}, u32[]{:S(2)}) async-start(f32[32,16,128]{2,1,0:T(8,128)} %get-tuple-element.30), calls=%async_computation.2 | async-start | bytes 524288 | tf_op jit(solution)/shard_map/all_to_all | solution.py:515
  103.9 7.8 %side.4 = (f32[128,1024]{1,0:T(8,128)}, f32[4,16,512]{2,1,0:T(8,128)}) custom-call(s32[2]{0:T(128)} %pad_add_fusion.place_ref, s32[5,128]{1,0:T(8,128)} %bitcast.21, f32[8,2048]{1,0:T(8,128)} %get-tuple-element.36.vrow_ref, f32[5,24,2048]{2,1,0:T(8,128)} %copy-done.12, f32[8,2,5,8,128]{4,3,2,1,0:T(8,128)} %constant.16.clone.tab_far, ...), custom_call_target="tpu_custom_call" | custom-call | flops 4000000000 | bytes 6000000 | tf_op jit(solution)/shard_map/side/pallas_call | solution.py:527
  111.8 7.9 %side.5 = (f32[128,1024]{1,0:T(8,128)}, f32[4,16,512]{2,1,0:T(8,128)}) custom-call(s32[2]{0:T(128)} %pad_add_fusion.place_ref, s32[5,128]{1,0:T(8,128)} %bitcast.22, f32[8,2048]{1,0:T(8,128)} %get-tuple-element.39.vrow_ref, f32[5,24,2048]{2,1,0:T(8,128)} %copy-done.12, f32[8,2,5,8,128]{4,3,2,1,0:T(8,128)} %constant.16.clone.tab_far, ...), custom_call_target="tpu_custom_call" | custom-call | flops 4000000000 | bytes 6000000 | tf_op jit(solution)/shard_map/side/pallas_call | solution.py:527
  119.8 0.5 copy-done.7
  120.3 0.0 copy-done.8
  120.3 0.1 copy-done.9
  120.4 1.0 copy-done.2
  121.4 0.9 copy-done.6
  122.3 1.6 %combine.1 = (f32[128,1024]{1,0:T(8,128)}, f32[16,512]{1,0:T(8,128)S(1)}, f32[16,512]{1,0:T(8,128)S(1)}, f32[16,512]{1,0:T(8,128)S(1)}, f32[16,512]{1,0:T(8,128)S(1)}) custom-call(s32[2]{0:T(128)S(1)} %copy-done.7, f32[6,8,16,128]{3,2,1,0:T(8,128)S(1)} %copy-done.3, f32[32,16,128]{2,1,0:T(8,128)S(1)} %all-to-all-done.2.in_ref, f32[1,128]{1,0:T(1,128)S(1)} %copy-done.8, ...), custom_call_target="tpu_custom_call" | custom-call | flops 10000000 | bytes 4000000 | tf_op jit(solution)/shard_map/combine/pallas_call | solution.py:530
  124.0 0.2 collective-permute-start.4
  124.2 1.6 %collective-permute-start.5 = (f32[16,512]{1,0:T(8,128)S(1)}, f32[16,512]{1,0:T(8,128)S(1)}, u32[]{:S(2)}, u32[]{:S(2)}) collective-permute-start(f32[16,512]{1,0:T(8,128)S(1)} %get-tuple-element.48), channel_id=1, source_target_pairs={{0,16},{8,24},{16,0},{24,8},{1,17},{9,25},{17,1},{25,9},{2,18},{10... | collective-permute-start | bytes 98312 | tf_op jit(solution)/shard_map/ppermute | solution.py:541
  125.8 2.3 %collective-permute-done.5 = f32[16,512]{1,0:T(8,128)S(1)} collective-permute-done((f32[16,512]{1,0:T(8,128)S(1)}, f32[16,512]{1,0:T(8,128)S(1)}, u32[]{:S(2)}, u32[]{:S(2)}) %collective-permute-start.5) | collective-permute-done | bytes 32800 | tf_op jit(solution)/shard_map/ppermute | solution.py:541
  128.1 1.1 collective-permute-done.6
  129.2 0.6 add_add_fusion
  (30 shorter events, 0.1 us)
Async XLA Ops:
  12.0 12.7 %collective-permute-start = (f32[24,2048]{1,0:T(8,128)}, f32[24,2048]{1,0:T(8,128)S(1)}, u32[]{:S(2)}, u32[]{:S(2)}) collective-permute-start(f32[24,2048]{1,0:T(8,128)} %prepare.1), channel_id=1, source_target_pairs={{0,2},{1,3},{2,4},{3,5},{4,6},{5,7},{8,10},{9,11},{10,12},{11,13},... | collective-permute-start | bytes 589832 | tf_op jit(solution)/shard_map/ppermute | solution.py:476
  17.0 15.0 %collective-permute-start.3 = (f32[24,2048]{1,0:T(8,128)}, f32[24,2048]{1,0:T(8,128)S(1)}, u32[]{:S(2)}, u32[]{:S(2)}) collective-permute-start(f32[24,2048]{1,0:T(8,128)} %prepare.1), channel_id=1, source_target_pairs={{2,0},{3,1},{4,2},{5,3},{6,4},{7,5},{10,8},{11,9},{12,10},{13,11},... | collective-permute-start | bytes 589832 | tf_op jit(solution)/shard_map/ppermute | solution.py:476
  18.3 13.7 %collective-permute-start.2 = (f32[24,2048]{1,0:T(8,128)}, f32[24,2048]{1,0:T(8,128)S(1)}, u32[]{:S(2)}, u32[]{:S(2)}) collective-permute-start(f32[24,2048]{1,0:T(8,128)} %prepare.1), channel_id=1, source_target_pairs={{1,0},{2,1},{3,2},{4,3},{5,4},{6,5},{7,6},{9,8},{10,9},{11,10},{12... | collective-permute-start | bytes 589832 | tf_op jit(solution)/shard_map/ppermute | solution.py:476
  19.6 12.3 %collective-permute-start.1 = (f32[24,2048]{1,0:T(8,128)}, f32[24,2048]{1,0:T(8,128)S(1)}, u32[]{:S(2)}, u32[]{:S(2)}) collective-permute-start(f32[24,2048]{1,0:T(8,128)} %prepare.1), channel_id=1, source_target_pairs={{0,1},{1,2},{2,3},{3,4},{4,5},{5,6},{6,7},{8,9},{9,10},{10,11},{11... | collective-permute-start | bytes 589832 | tf_op jit(solution)/shard_map/ppermute | solution.py:476
  24.8 7.2 %copy-start.11 = (f32[24,2048]{1,0:T(8,128)S(1)}, f32[24,2048]{1,0:T(8,128)}, u32[]{:S(2)}) copy-start(f32[24,2048]{1,0:T(8,128)} %prepare.1) | copy-start | bytes 589828
  32.0 1.0 copy-start.12
  75.6 13.1 %all-to-all-start.1 = ((f32[32,16,128]{2,1,0:T(8,128)}), f32[32,16,128]{2,1,0:T(8,128)S(1)}, u32[]{:S(2)}, u32[]{:S(2)}) async-start(f32[32,16,128]{2,1,0:T(8,128)} %get-tuple-element.28), calls=%async_computation.1 | async-start | bytes 524288 | tf_op jit(solution)/shard_map/all_to_all | solution.py:515
  88.7 0.7 copy-start.10
  100.8 18.8 %all-to-all-start.2 = ((f32[32,16,128]{2,1,0:T(8,128)}), f32[32,16,128]{2,1,0:T(8,128)S(1)}, u32[]{:S(2)}, u32[]{:S(2)}) async-start(f32[32,16,128]{2,1,0:T(8,128)} %get-tuple-element.30), calls=%async_computation.2 | async-start | bytes 524288 | tf_op jit(solution)/shard_map/all_to_all | solution.py:515
  111.7 8.0 %copy-start = (f32[128,1024]{1,0:T(8,128)S(1)}, f32[128,1024]{1,0:T(8,128)}, u32[]{:S(2)}) copy-start(f32[128,1024]{1,0:T(8,128)} %get-tuple-element.35.refs_2_) | copy-start | bytes 1572868
  111.7 8.0 %copy-start.1 = (f32[128,1024]{1,0:T(8,128)S(1)}, f32[128,1024]{1,0:T(8,128)}, u32[]{:S(2)}) copy-start(f32[128,1024]{1,0:T(8,128)} %get-tuple-element.38.refs_3_) | copy-start | bytes 1572868
  111.7 8.0 %copy-start.3 = (f32[6,8,16,128]{3,2,1,0:T(8,128)S(1)}, f32[6,8,16,128]{3,2,1,0:T(8,128)}, u32[]{:S(2)}) copy-start(f32[6,8,16,128]{3,2,1,0:T(8,128)} %get-tuple-element.29.state_ref) | copy-start | bytes 1179652
  111.8 8.0 %copy-start.4 = (f32[4,16,512]{2,1,0:T(8,128)S(1)}, f32[4,16,512]{2,1,0:T(8,128)}, u32[]{:S(2)}) copy-start(f32[4,16,512]{2,1,0:T(8,128)} %get-tuple-element.42.refs_5_) | copy-start | bytes 393220
  111.8 8.0 %copy-start.5 = (f32[4,16,512]{2,1,0:T(8,128)S(1)}, f32[4,16,512]{2,1,0:T(8,128)}, u32[]{:S(2)}) copy-start(f32[4,16,512]{2,1,0:T(8,128)} %get-tuple-element.43.refs_6_) | copy-start | bytes 393220
  119.7 0.6 copy-start.7
  119.7 0.6 copy-start.8
  119.7 0.7 copy-start.9
  120.4 1.0 copy-start.2
  121.4 0.9 copy-start.6
  124.0 1.9 %collective-permute-start.4 = (f32[16,512]{1,0:T(8,128)S(1)}, f32[16,512]{1,0:T(8,128)S(1)}, u32[]{:S(2)}, u32[]{:S(2)}) collective-permute-start(f32[16,512]{1,0:T(8,128)S(1)} %get-tuple-element.47), channel_id=1, source_target_pairs={{0,8},{8,0},{16,24},{24,16},{1,9},{9,1},{17,25},{25,17},{2,10},{10... | collective-permute-start | bytes 98312 | tf_op jit(solution)/shard_map/ppermute | solution.py:541
  124.2 3.9 %collective-permute-start.5 = (f32[16,512]{1,0:T(8,128)S(1)}, f32[16,512]{1,0:T(8,128)S(1)}, u32[]{:S(2)}, u32[]{:S(2)}) collective-permute-start(f32[16,512]{1,0:T(8,128)S(1)} %get-tuple-element.48), channel_id=1, source_target_pairs={{0,16},{8,24},{16,0},{24,8},{1,17},{9,25},{17,1},{25,9},{2,18},{10... | collective-permute-start | bytes 98312 | tf_op jit(solution)/shard_map/ppermute | solution.py:541
  125.8 3.4 %collective-permute-start.6 = (f32[16,512]{1,0:T(8,128)S(1)}, f32[16,512]{1,0:T(8,128)S(1)}, u32[]{:S(2)}, u32[]{:S(2)}) collective-permute-start(f32[16,512]{1,0:T(8,128)S(1)} %get-tuple-element.49), channel_id=1, source_target_pairs={{0,24},{8,16},{16,8},{24,0},{1,25},{9,17},{17,9},{25,1},{2,26},{10... | collective-permute-start | bytes 98312 | tf_op jit(solution)/shard_map/ppermute | solution.py:541
